TPU v7x, 128 devices: a whole 4x4x4 slice. The times are simulated.
128 devices in a mesh: row: 8 (over x, core), col: 16 (over z, y).
Axes of the slice: x: 4, y: 4, z: 4, core: 2. Of those that a mesh axis runs over, the one named last changes fastest.
Arguments:
- concentration: float32 [256, 256, 256], P('row', 'col'), may hold values from 0 to 1
Outputs:
- concentration_next: float32 [256, 256, 256], P('row', 'col')
- strain: float32 [6, 256, 256, 256], P(None, 'row', 'col')
- residual_norms: float32 [2], replicated
All inputs are finite; a program needn't handle non-finite values.
Results may differ from a plain program's by a relative error of at most 0.0003.
Values sent between devices are 32-bit elements; how exact they have to be, the bound alone decides.
No kernel may reach another device: no remote copies, remote signals or barrier semaphores. Data moves between devices by JAX's collectives and lax.ppermute only.
A program may use at most 192 MiB of HBM per device.

v0:
```python
import math

import jax
import jax.numpy as jnp
from jax import lax
from jax.sharding import Mesh
from jax.sharding import PartitionSpec as P

ITERS = 2
COL = ("col_0", "col_1")
ROW = ("row_0", "row_1")
ROW_COL = ("row_0", "row_1", "col_0", "col_1")


FIRST_LOW = 1.0
FIRST_RISE = 0.6
SHEAR_LOW = 0.7
SHEAR_RISE = 0.8
FIRST_REF = 1.3
SHEAR_REF = 1.1
BETA_REF = 2.4 / 3.5
EIGEN_STRAIN = 0.5
WELL_HEIGHT = 1.0
TIME_STEP = 0.5
GRADIENT_ENERGY = 0.5


def one_axis_at_a_time(shard, axes):
    for axis in axes:
        shard = lax.psum(shard, axis)
    return shard


def moduli(conc):
    return (FIRST_LOW + FIRST_RISE * conc, SHEAR_LOW + SHEAR_RISE * conc)


def polarization(strain, conc):
    first, shear = moduli(conc)
    trace = strain[0] + strain[1] + strain[2]
    normal = (first - FIRST_REF) * trace - (3.0 * first + 2.0 * shear) * EIGEN_STRAIN * conc
    excess = 2.0 * (shear - SHEAR_REF)
    return jnp.stack(
        [
            normal + excess * strain[0],
            normal + excess * strain[1],
            normal + excess * strain[2],
            excess * strain[3],
            excess * strain[4],
            excess * strain[5],
        ]
    )


def green_operator(tau, wave_x, wave_y, wave_z):
    square = wave_x * wave_x + wave_y * wave_y + wave_z * wave_z
    nonzero = square > 0.0
    safe = jnp.where(nonzero, square, 1.0)
    scale = jnp.where(nonzero, 1.0 / (SHEAR_REF * safe), 0.0)
    force_x = tau[0] * wave_x + tau[5] * wave_y + tau[4] * wave_z
    force_y = tau[5] * wave_x + tau[1] * wave_y + tau[3] * wave_z
    force_z = tau[4] * wave_x + tau[3] * wave_y + tau[2] * wave_z
    along = (wave_x * force_x + wave_y * force_y + wave_z * force_z) * (BETA_REF / safe)
    moved_x = scale * (force_x - along * wave_x)
    moved_y = scale * (force_y - along * wave_y)
    moved_z = scale * (force_z - along * wave_z)
    return jnp.stack(
        [
            -wave_x * moved_x,
            -wave_y * moved_y,
            -wave_z * moved_z,
            -0.5 * (wave_y * moved_z + wave_z * moved_y),
            -0.5 * (wave_x * moved_z + wave_z * moved_x),
            -0.5 * (wave_x * moved_y + wave_y * moved_x),
        ]
    )


def potential(strain, conc):
    first, shear = moduli(conc)
    dilation = EIGEN_STRAIN * conc
    part_x = strain[0] - dilation
    part_y = strain[1] - dilation
    part_z = strain[2] - dilation
    trace = part_x + part_y + part_z
    energy = (
        part_x * part_x
        + part_y * part_y
        + part_z * part_z
        + 2.0 * (strain[3] * strain[3] + strain[4] * strain[4] + strain[5] * strain[5])
    )
    chemical = 2.0 * WELL_HEIGHT * conc * (1.0 - conc) * (1.0 - 2.0 * conc)
    return (
        chemical
        + 0.5 * FIRST_RISE * trace * trace
        + SHEAR_RISE * energy
        - EIGEN_STRAIN * (3.0 * first + 2.0 * shear) * trace
    )


def build_tables(length):
    index = jnp.arange(length, dtype=jnp.int32)
    product = index[:, None] * index[None, :] % length
    angle = product.astype(jnp.float32) * (2.0 * math.pi / length)
    cosine = jnp.cos(angle)
    sine = jnp.sin(angle)
    half_length = length // 2
    ahead = jnp.stack(
        [jnp.stack([cosine, -sine], axis=1), jnp.stack([sine, cosine], axis=1)], axis=0
    )
    back = (
        jnp.stack([jnp.stack([cosine, sine], axis=1), jnp.stack([-sine, cosine], axis=1)], axis=0)
        / length
    )
    back = back.transpose(0, 1, 3, 2)
    z_ahead = jnp.stack([cosine[:, :half_length], -sine[:, :half_length]], axis=1)
    weight = (jnp.where(jnp.arange(half_length, dtype=jnp.int32) == 0, 1.0, 2.0) / length)[:, None]
    z_back = jnp.stack([cosine[:half_length, :] * weight, -sine[:half_length, :] * weight], axis=0)
    return (ahead, back, z_ahead, z_back)


def signed_waves(index, length):
    shifted = jnp.where(index < length // 2, index, index - length)
    return shifted.astype(jnp.float32) * (2.0 * math.pi / length)


def plain_waves(index, length):
    return index.astype(jnp.float32) * (2.0 * math.pi / length)


def contract(form, data, table):
    return jnp.einsum(
        form, data, table, precision=lax.Precision.HIGHEST, preferred_element_type=jnp.float32
    )


def z_forward(fields, tables):
    members, local_x, local_y, length = fields.shape
    half_length = length // 2
    spectrum = contract("fxyz,zbk->fbkxy", fields, tables[2])
    return spectrum.reshape(members, 2, 1, half_length, local_x * local_y)


def z_inverse(spectrum, tables, local_x, local_y):
    members = spectrum.shape[0]
    half_length = tables[3].shape[1]
    spectrum = spectrum.reshape(members, 2, half_length, local_x, local_y)
    return contract("fakxy,akz->fxyz", spectrum, tables[3])


def forward_col(fields, tables):
    members, local_x, local_y, length = fields.shape
    half_length = length // 2
    spectrum = z_forward(fields, tables)
    spectrum = lax.all_to_all(spectrum, COL, split_axis=3, concat_axis=2, tiled=True)
    ncols = lax.axis_size(COL)
    kz_local = half_length // ncols
    spectrum = spectrum.reshape(members, 2, ncols, kz_local, local_x, local_y)
    spectrum = contract(
        "fackxl,aclbm->fbmkx", spectrum, tables[0].reshape(2, ncols, local_y, 2, length)
    )
    spectrum = spectrum.reshape(members, 2, 1, length, kz_local * local_x)
    spectrum = lax.all_to_all(spectrum, ROW, split_axis=3, concat_axis=2, tiled=True)
    nrows = lax.axis_size(ROW)
    ky_local = length // nrows
    spectrum = spectrum.reshape(members, 2, nrows, ky_local, kz_local, local_x)
    spectrum = contract(
        "farjkx,arxbm->fbjkm", spectrum, tables[0].reshape(2, nrows, local_x, 2, length)
    )
    wave_y = signed_waves(
        lax.axis_index(ROW) * ky_local + jnp.arange(ky_local, dtype=jnp.int32), length
    )[:, None, None]
    wave_z = plain_waves(
        lax.axis_index(COL) * kz_local + jnp.arange(kz_local, dtype=jnp.int32), length
    )[None, :, None]
    wave_x = signed_waves(jnp.arange(length, dtype=jnp.int32), length)[None, None, :]
    return (spectrum, (wave_x, wave_y, wave_z))


def inverse_col(spectrum, tables, local_x, local_y):
    members, parts, ky_local, kz_local, length = spectrum.shape
    nrows = lax.axis_size(ROW)
    ncols = lax.axis_size(COL)
    spectrum = contract(
        "fajkm,amrxb->fbrjkx", spectrum, tables[1].reshape(2, length, nrows, local_x, 2)
    )
    spectrum = spectrum.reshape(members, 2, nrows, ky_local, kz_local * local_x)
    spectrum = lax.all_to_all(spectrum, ROW, split_axis=2, concat_axis=3, tiled=True)
    spectrum = spectrum.reshape(members, 2, length, kz_local, local_x)
    spectrum = contract(
        "fajkx,ajclb->fbckxl", spectrum, tables[1].reshape(2, length, ncols, local_y, 2)
    )
    spectrum = spectrum.reshape(members, 2, ncols, kz_local, local_x * local_y)
    spectrum = lax.all_to_all(spectrum, COL, split_axis=2, concat_axis=3, tiled=True)
    return z_inverse(spectrum, tables, local_x, local_y)


def forward_group(fields, tables):
    return forward_col(fields, tables)


def inverse_group(spectrum, tables, local_x, local_y):
    return inverse_col(spectrum, tables, local_x, local_y)


def forward(fields, tables):
    return forward_group(fields, tables)


def inverse(spectrum, tables, local_x, local_y):
    return inverse_group(spectrum, tables, local_x, local_y)


def shards(concentration):
    local_x, local_y, length = concentration.shape
    tables = build_tables(length)
    strain = jnp.zeros((6, local_x, local_y, length), jnp.float32)
    sums = []
    for sweep in range(ITERS):
        tau = polarization(strain, concentration)
        spectrum, waves = forward(tau, tables)
        spectrum = green_operator(spectrum, waves[0], waves[1], waves[2])
        updated = inverse(spectrum, tables, local_x, local_y)
        change = updated - strain
        partial_sum = jnp.sum(change * change)
        sums.append(one_axis_at_a_time(partial_sum, ROW_COL))
        strain = updated
    totals = jnp.stack(sums)
    residual_norms = jnp.sqrt(totals / length**3)
    drive = potential(strain, concentration)
    spectrum, waves = forward(jnp.stack([concentration, drive]), tables)
    square = waves[0] * waves[0] + waves[1] * waves[1] + waves[2] * waves[2]
    denominator = 1.0 + TIME_STEP * GRADIENT_ENERGY * square * square
    updated_spectrum = (spectrum[0] - TIME_STEP * square * spectrum[1]) / denominator
    concentration_next = inverse(updated_spectrum[None], tables, local_x, local_y)[0]
    return (concentration_next, strain, residual_norms)


def solution(mesh):
    split = Mesh(mesh.devices.reshape(4, 2, 4, 4), ("row_0", "row_1", "col_0", "col_1"))
    in_specs = (P(ROW, COL, None),)
    out_specs = (P(ROW, COL, None), P(None, ROW, COL, None), P())
    return jax.shard_map(
        shards, mesh=split, in_specs=in_specs, out_specs=out_specs, check_vma=False
    )
```

profile of v0, /device:TPU:1, one launch (start us, length us, event | category | flops | bytes accessed | tf_op | source)
XLA Modules:
  0.0 1128.2 jit_solution(896907391976863344)
XLA Ops:
  31.7 45.8 %all-to-all-done = f32[6,2,1,128,512]{4,1,0,2,3:T(2,128)} async-done(((f32[6,2,1,128,512]{4,1,0,2,3:T(2,128)}), f32[6,2,1,128,512]{4,1,0,2,3:T(2,128)}, u32[]{:S(2)}, u32[]{:S(2)}) %all-to-all-start) | async-done | bytes 3145760 | tf_op jit(solution)/shard_map/all_to_all | solution.py:155
  93.4 38.7 %fusion.2 = f32[2,256,6,8,32,1,1]{1,4,6,5,3,2,0:T(8,128)} fusion(f32[1,16,16,1,256]{4,2,1,0,3:T(8,128)S(1)} %get-tuple-element.51, f32[1,16,16,1,256]{4,2,1,0,3:T(8,128)S(1)} %get-tuple-element.50, f32[1,16,16,1,256]{4,2,1,0,3:T(8,128)S(1)} %get-tuple-element.49, f32[6,2,16,8,32,16]{5,4,1,0,3,2:T(8,128)} %reshape.525), kind=kOutput, calls=%fused_computation.2 | convolution fusion | flops 4832624640 | bytes 7077888 | tf_op jit(solution)/shard_map/fackxl,aclbm->fbmkx/dot_general | solution.py:132
  150.1 32.0 %all-to-all-done.1 = f32[6,2,1,256,256]{4,1,0,2,3:T(2,128)} async-done(((f32[6,2,1,256,256]{4,1,0,2,3:T(2,128)}), f32[6,2,1,256,256]{4,1,0,2,3:T(2,128)}, u32[]{:S(2)}, u32[]{:S(2)}) %all-to-all-start.1) | async-done | bytes 3145760 | tf_op jit(solution)/shard_map/all_to_all | solution.py:163
  191.4 26.6 %fusion.41 = f32[6,2,32,8,256]{4,2,3,0,1:T(8,128)S(1)} fusion(f32[6,2,8,32,8,32]{5,4,1,0,3,2:T(8,128)} %reshape.526, f32[1,8,32,1,256]{4,2,1,0,3:T(8,128)S(1)} %get-tuple-element.54, f32[1,8,32,1,256]{4,2,1,0,3:T(8,128)S(1)} %get-tuple-element.53, f32[1,8,32,1,256]{4,2,1,0,3:T(8,128)S(1)} %get-tuple-element.52), kind=kOutput, calls=%fused_computation.39 | convolution fusion | flops 4832624640 | bytes 7077888 | tf_op jit(solution)/shard_map/farjkx,arxbm->fbjkm/dot_general | solution.py:132
  219.8 22.4 %fusion.35 = f32[8,32,2,6,32,8,1]{4,1,6,5,3,2,0:T(8,128)} fusion(f32[2,256,8,32,2,1,1]{1,3,2,4,0,6,5:T(8,128)S(1)} %bitcast.362, f32[6,2,32,8,256]{4,2,3,0,1:T(8,128)S(1)} %multiply_dynamic-update-slice_fusion.6), kind=kOutput, calls=%fused_computation.31 | convolution fusion | flops 4831838208 | bytes 7340032 | tf_op jit(solution)/shard_map/fajkm,amrxb->fbrjkx/dot_general | solution.py:132
  251.0 42.1 %all_to_all.48 = f32[6,2,8,32,256]{4,3,1,0,2:T(8,128)S(1)} all-to-all(f32[6,2,8,32,256]{4,3,1,0,2:T(8,128)} %copy.96), channel_id=1, replica_groups=mesh['row_0'=4,'row_1'=2,'col_0'=4,'col_1'=4] {'row_0','row_1'}, dimensions={2} | all-to-all | bytes 6291456 | tf_op jit(solution)/shard_map/all_to_all | solution.py:188
  303.5 27.1 %fusion.20 = f32[6,2,16,8,32,16]{4,5,3,0,1,2:T(8,128)} fusion(f32[6,2,256,8,32,1,1]{4,3,2,1,0,6,5:T(8,128)} %bitcast.357, f32[2,256,16,16,2,1,1]{1,3,2,4,0,6,5:T(8,128)S(1)} %bitcast.363), kind=kOutput, calls=%fused_computation.20 | convolution fusion | flops 4831838208 | bytes 7340032 | tf_op jit(solution)/shard_map/fajkx,ajclb->fbckxl/dot_general | solution.py:132
  330.6 17.8 %copy.207 = f32[6,2,16,8,32,16]{5,4,3,1,0,2:T(8,128)} copy(f32[6,2,16,8,32,16]{4,5,3,0,1,2:T(8,128)} %fusion.20) | data formatting | bytes 6291456 | tf_op jit(solution)/shard_map/reshape | solution.py:193
  348.4 21.5 %reshape.527 = f32[6,2,16,8,512]{4,3,1,0,2:T(8,128)} reshape(f32[6,2,16,8,32,16]{5,4,3,1,0,2:T(8,128)} %copy.207) | data formatting | bytes 6291456 | tf_op jit(solution)/shard_map/reshape | solution.py:193
  375.1 46.6 %all-to-all-done.3 = f32[6,2,16,8,512]{4,3,1,0,2:T(8,128)} async-done(((f32[6,2,16,8,512]{4,3,1,0,2:T(8,128)}), f32[6,2,16,8,512]{4,3,1,0,2:T(8,128)}, u32[]{:S(2)}, u32[]{:S(2)}) %all-to-all-start.3) | async-done | bytes 3145760 | tf_op jit(solution)/shard_map/all_to_all | solution.py:194
  440.9 50.0 %fusion.47 = f32[6,32,16,256]{3,2,1,0:T(8,128)S(1)} fusion(f32[6,2,128,32,16]{4,3,2,1,0:T(8,128)} %reshape.466, f32[1,128,256]{2,1,0:T(8,128)S(1)} %get-tuple-element.56, f32[1,128,256]{2,1,0:T(8,128)S(1)} %get-tuple-element.55), kind=kOutput, calls=%fused_computation.41 | convolution fusion | flops 2415984640 | bytes 6553600 | tf_op jit(solution)/shard_map/fakxy,akz->fxyz/dot_general | solution.py:132
  509.9 42.9 %all_to_all.49 = f32[6,2,1,128,512]{4,1,0,2,3:T(2,128)} all-to-all(f32[6,2,1,128,512]{4,1,0,2,3:T(2,128)} %copy.111), channel_id=1, replica_groups=mesh['row_0'=4,'row_1'=2,'col_0'=4,'col_1'=4] {'col_0','col_1'}, dimensions={3} | all-to-all | bytes 6291456 | tf_op jit(solution)/shard_map/all_to_all | solution.py:155
  568.8 38.7 %fusion = f32[2,256,6,8,32,1,1]{1,4,6,5,3,2,0:T(8,128)} fusion(f32[1,16,16,1,256]{4,2,1,0,3:T(8,128)S(1)} %copy-done.19, f32[1,16,16,1,256]{4,2,1,0,3:T(8,128)S(1)} %copy-done.16, f32[1,16,16,1,256]{4,2,1,0,3:T(8,128)S(1)} %copy-done.13, f32[6,2,16,8,32,16]{5,4,1,0,3,2:T(8,128)} %reshape.528), kind=kOutput, calls=%fused_computation | convolution fusion | flops 4832624640 | bytes 7077888 | tf_op jit(solution)/shard_map/fackxl,aclbm->fbmkx/dot_general | solution.py:132
  613.3 44.9 %all_to_all.50 = f32[6,2,1,256,256]{4,1,0,2,3:T(2,128)} all-to-all(f32[6,2,1,256,256]{4,1,0,2,3:T(2,128)} %copy.114), channel_id=1, replica_groups=mesh['row_0'=4,'row_1'=2,'col_0'=4,'col_1'=4] {'row_0','row_1'}, dimensions={3} | all-to-all | bytes 6291456 | tf_op jit(solution)/shard_map/all_to_all | solution.py:163
  667.7 26.6 %fusion.44 = f32[6,2,32,8,256]{4,2,3,0,1:T(8,128)S(1)} fusion(f32[6,2,8,32,8,32]{5,4,1,0,3,2:T(8,128)} %reshape.529, f32[1,8,32,1,256]{4,2,1,0,3:T(8,128)S(1)} %copy-done.28, f32[1,8,32,1,256]{4,2,1,0,3:T(8,128)S(1)} %copy-done.25, f32[1,8,32,1,256]{4,2,1,0,3:T(8,128)S(1)} %copy-done.22), kind=kOutput, calls=%fused_computation.40 | convolution fusion | flops 4832624640 | bytes 7077888 | tf_op jit(solution)/shard_map/farjkx,arxbm->fbjkm/dot_general | solution.py:132
  696.0 22.4 %fusion.31 = f32[8,32,2,6,32,8,1]{4,1,6,5,3,2,0:T(8,128)} fusion(f32[2,256,8,32,2,1,1]{1,3,2,4,0,6,5:T(8,128)S(1)} %bitcast.364, f32[6,2,32,8,256]{4,2,3,0,1:T(8,128)S(1)} %multiply_dynamic-update-slice_fusion), kind=kOutput, calls=%fused_computation.27 | convolution fusion | flops 4831838208 | bytes 7340032 | tf_op jit(solution)/shard_map/fajkm,amrxb->fbrjkx/dot_general | solution.py:132
  727.2 42.4 %all_to_all.51 = f32[6,2,8,32,256]{4,3,1,0,2:T(8,128)S(1)} all-to-all(f32[6,2,8,32,256]{4,3,1,0,2:T(8,128)} %copy.119), channel_id=1, replica_groups=mesh['row_0'=4,'row_1'=2,'col_0'=4,'col_1'=4] {'row_0','row_1'}, dimensions={2} | all-to-all | bytes 6291456 | tf_op jit(solution)/shard_map/all_to_all | solution.py:188
  780.1 27.1 %fusion.23 = f32[6,2,16,8,32,16]{4,5,3,0,1,2:T(8,128)} fusion(f32[6,2,256,8,32,1,1]{4,3,2,1,0,6,5:T(8,128)} %bitcast.359, f32[2,256,16,16,2,1,1]{1,3,2,4,0,6,5:T(8,128)S(1)} %bitcast.365), kind=kOutput, calls=%fused_computation.21 | convolution fusion | flops 4831838208 | bytes 7340032 | tf_op jit(solution)/shard_map/fajkx,ajclb->fbckxl/dot_general | solution.py:132
  807.2 17.8 %copy.218 = f32[6,2,16,8,32,16]{5,4,3,1,0,2:T(8,128)} copy(f32[6,2,16,8,32,16]{4,5,3,0,1,2:T(8,128)} %fusion.23) | data formatting | bytes 6291456 | tf_op jit(solution)/shard_map/reshape | solution.py:193
  825.0 21.5 %reshape.530 = f32[6,2,16,8,512]{4,3,1,0,2:T(8,128)} reshape(f32[6,2,16,8,32,16]{5,4,3,1,0,2:T(8,128)} %copy.218) | data formatting | bytes 6291456 | tf_op jit(solution)/shard_map/reshape | solution.py:193
  846.5 42.3 %all_to_all.52 = f32[6,2,16,8,512]{4,3,1,0,2:T(8,128)S(1)} all-to-all(f32[6,2,16,8,512]{4,3,1,0,2:T(8,128)} %reshape.530), channel_id=1, replica_groups=mesh['row_0'=4,'row_1'=2,'col_0'=4,'col_1'=4] {'col_0','col_1'}, dimensions={2} | all-to-all | bytes 6291456 | tf_op jit(solution)/shard_map/all_to_all | solution.py:194
  906.0 58.5 %multiply_reduce_fusion.1 = (f32[]{:T(128)}, f32[]{:T(128)}, f32[6,32,16,256]{3,2,1,0:T(8,128)S(1)}) fusion(f32[6,32,16,256]{3,2,1,0:T(8,128)} %copy-done.1, f32[1,128,256]{2,1,0:T(8,128)S(1)} %get-tuple-element.56, f32[1,128,256]{2,1,0:T(8,128)S(1)} %get-tuple-element.55, f32[6,2,128,32,16]{4,3,2,1,0:T(8,128)} %reshape.474), kind=kOutput, calls=%fused_computation.36 | convolution fusion | flops 2419916800 | bytes 9699336 | tf_op jit(solution)/shard_map/fakxy,akz->fxyz/dot_general | solution.py:132
  971.0 18.7 %all_to_all.53 = f32[2,2,1,128,512]{4,1,0,2,3:T(2,128)S(1)} all-to-all(f32[2,2,1,128,512]{4,1,0,2,3:T(2,128)S(1)} %copy.135), channel_id=1, replica_groups=mesh['row_0'=4,'row_1'=2,'col_0'=4,'col_1'=4] {'col_0','col_1'}, dimensions={3} | all-to-all | bytes 2097152 | tf_op jit(solution)/shard_map/all_to_all | solution.py:155
  1009.4 20.3 %all_to_all.54 = f32[2,2,1,256,256]{4,1,0,2,3:T(2,128)S(1)} all-to-all(f32[2,2,1,256,256]{4,1,0,2,3:T(2,128)S(1)} %copy.138), channel_id=1, replica_groups=mesh['row_0'=4,'row_1'=2,'col_0'=4,'col_1'=4] {'row_0','row_1'}, dimensions={3} | all-to-all | bytes 2097152 | tf_op jit(solution)/shard_map/all_to_all | solution.py:163
  (167 shorter events, 331.9 us)
Async XLA Ops:
  0.6 6.8 copy-start
  1.6 7.0 copy-start.8
  2.6 6.0 copy-start.10
  21.7 55.9 %all-to-all-start = ((f32[6,2,1,128,512]{4,1,0,2,3:T(2,128)}), f32[6,2,1,128,512]{4,1,0,2,3:T(2,128)}, u32[]{:S(2)}, u32[]{:S(2)}) async-start(f32[6,2,1,128,512]{4,1,0,2,3:T(2,128)} %copy.88), calls=%async_computation | async-start | bytes 6291456 | tf_op jit(solution)/shard_map/all_to_all | solution.py:155
  31.7 61.7 %copy-start.12 = (f32[1,16,16,1,256]{4,2,1,0,3:T(8,128)}, f32[1,16,16,1,256]{4,2,1,0,3:T(8,128)S(1)}, u32[]{:S(2)}) copy-start(f32[1,16,16,1,256]{4,2,1,0,3:T(8,128)S(1)} %get-tuple-element.49) | copy-start | bytes 786436
  31.7 61.7 %copy-start.15 = (f32[1,16,16,1,256]{4,2,1,0,3:T(8,128)}, f32[1,16,16,1,256]{4,2,1,0,3:T(8,128)S(1)}, u32[]{:S(2)}) copy-start(f32[1,16,16,1,256]{4,2,1,0,3:T(8,128)S(1)} %get-tuple-element.50) | copy-start | bytes 786436
  31.7 61.7 %copy-start.18 = (f32[1,16,16,1,256]{4,2,1,0,3:T(8,128)}, f32[1,16,16,1,256]{4,2,1,0,3:T(8,128)S(1)}, u32[]{:S(2)}) copy-start(f32[1,16,16,1,256]{4,2,1,0,3:T(8,128)S(1)} %get-tuple-element.51) | copy-start | bytes 786436
  138.0 44.1 %all-to-all-start.1 = ((f32[6,2,1,256,256]{4,1,0,2,3:T(2,128)}), f32[6,2,1,256,256]{4,1,0,2,3:T(2,128)}, u32[]{:S(2)}, u32[]{:S(2)}) async-start(f32[6,2,1,256,256]{4,1,0,2,3:T(2,128)} %copy.91), calls=%async_computation.1 | async-start | bytes 6291456 | tf_op jit(solution)/shard_map/all_to_all | solution.py:163
  149.0 42.4 %copy-start.21 = (f32[1,8,32,1,256]{4,2,1,0,3:T(8,128)}, f32[1,8,32,1,256]{4,2,1,0,3:T(8,128)S(1)}, u32[]{:S(2)}) copy-start(f32[1,8,32,1,256]{4,2,1,0,3:T(8,128)S(1)} %get-tuple-element.52) | copy-start | bytes 786436
  149.0 42.4 %copy-start.24 = (f32[1,8,32,1,256]{4,2,1,0,3:T(8,128)}, f32[1,8,32,1,256]{4,2,1,0,3:T(8,128)S(1)}, u32[]{:S(2)}) copy-start(f32[1,8,32,1,256]{4,2,1,0,3:T(8,128)S(1)} %get-tuple-element.53) | copy-start | bytes 786436
  149.0 42.4 %copy-start.27 = (f32[1,8,32,1,256]{4,2,1,0,3:T(8,128)}, f32[1,8,32,1,256]{4,2,1,0,3:T(8,128)S(1)}, u32[]{:S(2)}) copy-start(f32[1,8,32,1,256]{4,2,1,0,3:T(8,128)S(1)} %get-tuple-element.54) | copy-start | bytes 786436
  369.9 5.1 copy-start.9
  369.9 5.1 copy-start.11
  369.9 51.7 %all-to-all-start.3 = ((f32[6,2,16,8,512]{4,3,1,0,2:T(8,128)}), f32[6,2,16,8,512]{4,3,1,0,2:T(8,128)}, u32[]{:S(2)}, u32[]{:S(2)}) async-start(f32[6,2,16,8,512]{4,3,1,0,2:T(8,128)} %reshape.527), calls=%async_computation.3 | async-start | bytes 6291456 | tf_op jit(solution)/shard_map/all_to_all | solution.py:194
  552.8 16.0 %copy-start.13 = (f32[1,16,16,1,256]{4,2,1,0,3:T(8,128)S(1)}, f32[1,16,16,1,256]{4,2,1,0,3:T(8,128)}, u32[]{:S(2)}) copy-start(f32[1,16,16,1,256]{4,2,1,0,3:T(8,128)} %copy-done.12) | copy-start | bytes 786436
  552.8 16.0 %copy-start.16 = (f32[1,16,16,1,256]{4,2,1,0,3:T(8,128)S(1)}, f32[1,16,16,1,256]{4,2,1,0,3:T(8,128)}, u32[]{:S(2)}) copy-start(f32[1,16,16,1,256]{4,2,1,0,3:T(8,128)} %copy-done.15) | copy-start | bytes 786436
  552.8 16.0 %copy-start.19 = (f32[1,16,16,1,256]{4,2,1,0,3:T(8,128)S(1)}, f32[1,16,16,1,256]{4,2,1,0,3:T(8,128)}, u32[]{:S(2)}) copy-start(f32[1,16,16,1,256]{4,2,1,0,3:T(8,128)} %copy-done.18) | copy-start | bytes 786436
  658.2 9.5 copy-start.22
  658.2 9.5 copy-start.25
  658.2 9.5 copy-start.28
  989.7 4.9 copy-start.20
  1032.7 10.0 copy-start.6
  1032.7 10.0 copy-start.7
  1076.5 37.6 %all-to-all-start.11 = ((f32[1,2,16,8,512]{4,3,1,0,2:T(8,128)}), f32[1,2,16,8,512]{4,3,1,0,2:T(8,128)S(1)}, u32[]{:S(2)}, u32[]{:S(2)}) async-start(f32[1,2,16,8,512]{4,3,1,0,2:T(8,128)} %reshape.533), calls=%async_computation.11 | async-start | bytes 1048576 | tf_op jit(solution)/shard_map/all_to_all | solution.py:194
  (14 other events, 31.3 us)
where the time goes:
time: 1140 us; the launch traced here: 1130 us
  matrix products  389 us (34%)
  blocking collectives  300 us (26%)
  local copies, waits for them, and re-layouts  263 us (23%)
  waiting for transfers between devices  124 us (11%)
  other arithmetic  26.5 us (2%)
  starting transfers between devices  24 us (2%)
    dot_general x18, matrix products, contract(): jnp.einsum(form, data, table, precision=lax.Precision.HIGHEST, preferred_...  389 us
    all_to_all x3, blocking collectives, inverse_col(): lax.all_to_all(spectrum, ROW, split_axis=2, concat_axis=3, tiled=True)  98.5 us
    reshape x6, local copies, waits for them, and re-layouts, inverse_col(): spectrum = spectrum.reshape(members, 2, ncols, kz_local, local_x * local_y)  86.4 us
    all_to_all x2, blocking collectives, forward_col(): lax.all_to_all(spectrum, ROW, split_axis=3, concat_axis=2, tiled=True)  65.2 us
    all_to_all x2, blocking collectives, forward_col(): lax.all_to_all(spectrum, COL, split_axis=3, concat_axis=2, tiled=True)  61.6 us
    all_to_all x2, waiting for transfers between devices, inverse_col(): lax.all_to_all(spectrum, COL, split_axis=2, concat_axis=3, tiled=True)  46.6 us
    all_to_all x1, waiting for transfers between devices, forward_col(): lax.all_to_all(spectrum, COL, split_axis=3, concat_axis=2, tiled=True)  45.8 us
    all_to_all x1, blocking collectives, inverse_col(): lax.all_to_all(spectrum, COL, split_axis=2, concat_axis=3, tiled=True)  42.3 us
  transfers between devices with their start and end apart: 4, of which 3 were waited for; matrix products, arithmetic and copies ran while one was open for 1% of the time, Pallas kernels for 0%

commit v1 on v0

v1 whole, which is shorter than its diff:
```python
import math
from functools import partial

import jax
import jax.numpy as jnp
import numpy as np
from jax import lax
from jax.experimental import pallas as pl
from jax.experimental.pallas import tpu as pltpu
from jax.sharding import Mesh
from jax.sharding import PartitionSpec as P

AXES = ("row_0", "row_1", "col_0", "col_1")

FIRST_LOW = 1.0
FIRST_RISE = 0.6
SHEAR_LOW = 0.7
SHEAR_RISE = 0.8
FIRST_REF = 1.3
SHEAR_REF = 1.1
BETA_REF = 2.4 / 3.5
EIGEN_STRAIN = 0.5
WELL_HEIGHT = 1.0
TIME_STEP = 0.5
GRADIENT_ENERGY = 0.5

N = 256
HALF = N // 2
ROWS = 8
COLS = 16
DEVICES = ROWS * COLS
LX = N // ROWS
LY = N // COLS
LOW = 8
HIGH = LX // LOW
CELLS = LX * LY
LANES = 128
UNIT = 2.0 * math.pi / N
F32 = jnp.float32
BF16 = jnp.bfloat16
INTERPRET = False


def pieces_of(table, count):
    rest = table.astype(np.float32)
    pieces = []
    for _ in range(count):
        piece = rest.astype(jnp.bfloat16)
        rest = rest - piece.astype(np.float32)
        pieces.append(piece)
    return np.stack(pieces)


def build_tables():
    index = np.arange(N)
    angle = 2.0 * np.pi / N * (index[:, None] * index[None, :] % N)
    cosine = np.cos(angle)
    sine = np.sin(angle)
    ahead = np.concatenate([cosine[:HALF], -sine[:HALF]], axis=0)
    weight = np.where(np.arange(HALF) == 0, 1.0, 2.0) / float(N) ** 3
    back = np.concatenate([cosine[:, :HALF] * weight, -sine[:, :HALF] * weight], axis=1)
    return pieces_of(cosine, 2), pieces_of(sine, 2), pieces_of(ahead, 3), pieces_of(back, 2)


def split(value, count):
    pieces = []
    for i in range(count):
        piece = value.astype(BF16)
        pieces.append(piece)
        if i + 1 < count:
            value = value - piece.astype(F32)
    return pieces


def product(left, right):
    count = len(right)
    total = None
    for order in reversed(range(count)):
        for i in range(order + 1):
            term = jnp.dot(left[i], right[order - i], preferred_element_type=F32)
            total = term if total is None else total + term
    return total


def table(ref):
    return [ref[i] for i in range(ref.shape[0])]


def swap_lanes(parts, granule):
    parts = list(parts)
    axis = parts[0].ndim - 1
    lane = lax.broadcasted_iota(jnp.int32, parts[0].shape, axis)
    step = 1
    while step < len(parts):
        width = granule * step
        low = (lane & width) == 0
        for i in range(len(parts)):
            if i & step == 0:
                a, b = parts[i], parts[i + step]
                parts[i] = jnp.where(low, a, pltpu.roll(b, width, axis))
                parts[i + step] = jnp.where(low, pltpu.roll(a, LANES - width, axis), b)
        step *= 2
    return parts


def z_ahead(value, f, fields, ahead_ref, out_ref):
    spectrum = product(table(ahead_ref), split(value, 3))
    for t in range(LOW // 2):
        lanes = slice(t * LANES, (t + 1) * LANES)
        parts = swap_lanes([spectrum[:HALF, lanes], spectrum[HALF:, lanes]], LANES // 2)
        for i in range(2):
            out_ref[pl.ds(f * LOW + 2 * t + i, HALF, stride=fields * LOW), :] = parts[i]


def z_back(in_ref, f, fields, back_ref, spec_ref):
    for t in range(LOW // 2):
        lanes = slice(t * LANES, (t + 1) * LANES)
        parts = [
            in_ref[pl.ds(f * LOW + 2 * t + i, HALF, stride=fields * LOW), :] for i in range(2)
        ]
        real, imag = swap_lanes(parts, LANES // 2)
        spec_ref[:HALF, lanes] = real
        spec_ref[HALF:, lanes] = imag
    return product(table(back_ref), split(spec_ref[...], 2))


def x_lines(real, imag, sign, cos_ref, sin_ref):
    data = split(jnp.concatenate([real, imag], axis=1), 2)
    even = product(table(cos_ref), data)
    odd = product(table(sin_ref), data)
    if sign < 0:
        return even[:, :N] + odd[:, N:], even[:, N:] - odd[:, :N]
    return even[:, :N] - odd[:, N:], even[:, N:] + odd[:, :N]


def y_lines(real, imag, sign, cos_ref, sin_ref):
    data = split(jnp.concatenate([real, imag], axis=0), 2)
    even = product(data, table(cos_ref))
    odd = product(data, table(sin_ref))
    if sign < 0:
        return even[:N] + odd[N:], even[N:] - odd[:N]
    return even[:N] - odd[N:], even[N:] + odd[:N]


def rows_of(block, fields, f):
    start = block * fields * LOW + f * LOW
    return pl.ds(start if isinstance(start, int) else pl.multiple_of(start, LOW), LOW)


def plane_gather(in_ref, f, fields, plane_ref):
    for i in range(ROWS):
        for h in range(2):
            parts = [in_ref[rows_of(i * COLS + h * 8 + j, fields, f), :] for j in range(8)]
            parts = swap_lanes(parts, LY)
            for g in range(8):
                x = i * LX + g % HIGH * LOW
                plane_ref[g // HIGH, x : x + LOW, h * LANES : (h + 1) * LANES] = parts[g]


def plane_scatter(plane_ref, f, fields, out_ref):
    for i in range(ROWS):
        for h in range(2):
            parts = []
            for g in range(8):
                x = i * LX + g % HIGH * LOW
                parts.append(plane_ref[g // HIGH, x : x + LOW, h * LANES : (h + 1) * LANES])
            parts = swap_lanes(parts, LY)
            for j in range(8):
                out_ref[rows_of(i * COLS + h * 8 + j, fields, f), :] = parts[j]


def plane_ahead(in_ref, f, fields, cos_ref, sin_ref, plane_ref):
    plane_gather(in_ref, f, fields, plane_ref)
    real, imag = x_lines(plane_ref[0], plane_ref[1], -1, cos_ref, sin_ref)
    return y_lines(real, imag, -1, cos_ref, sin_ref)


def plane_back(real, imag, f, fields, cos_ref, sin_ref, plane_ref, out_ref):
    real, imag = y_lines(real, imag, 1, cos_ref, sin_ref)
    real, imag = x_lines(real, imag, 1, cos_ref, sin_ref)
    plane_ref[0] = real
    plane_ref[1] = imag
    plane_scatter(plane_ref, f, fields, out_ref)


def signed(index):
    return jnp.where(index < HALF, index, index - N).astype(F32) * UNIT


def waves(place_ref, start, count):
    shape = (count, N)
    wave_x = signed(lax.broadcasted_iota(jnp.int32, shape, 0) + start)
    wave_y = signed(lax.broadcasted_iota(jnp.int32, shape, 1))
    wave_z = jnp.full(shape, place_ref[0], jnp.int32).astype(F32) * UNIT
    return wave_x, wave_y, wave_z


def fold(total):
    total = sum(total[:, t * LANES : (t + 1) * LANES] for t in range(CELLS // LANES))
    return total + pltpu.roll(total, 4, 0)


def source_kernel(conc_ref, ahead_ref, cells_ref, out_ref, lines_ref):
    for low in range(LOW):
        for high in range(HIGH):
            start = (low * HIGH + high) * LY
            lines_ref[start : start + LY, :] = conc_ref[high * LOW + low]
    conc = lines_ref[...].T
    cells_ref[...] = conc
    first = FIRST_LOW + FIRST_RISE * conc
    shear = SHEAR_LOW + SHEAR_RISE * conc
    z_ahead(-(3.0 * first + 2.0 * shear) * EIGEN_STRAIN * conc, 0, 2, ahead_ref, out_ref)
    z_ahead(conc, 1, 2, ahead_ref, out_ref)


def plane_first_kernel(
    place_ref, in_ref, cos_ref, sin_ref, out_ref, conc_ref, plane_ref, spec_ref, line_ref
):
    real, imag = plane_ahead(in_ref, 1, 2, cos_ref, sin_ref, plane_ref)
    conc_ref[0] = real
    conc_ref[1] = imag
    real, imag = plane_ahead(in_ref, 0, 2, cos_ref, sin_ref, plane_ref)
    spec_ref[0] = real
    spec_ref[1] = imag
    wave_x, wave_y, wave_z = waves(place_ref, 0, N)
    square = wave_x * wave_x + wave_y * wave_y + wave_z * wave_z
    nonzero = square > 0.0
    safe = jnp.where(nonzero, square, 1.0)
    scale = jnp.where(nonzero, -(1.0 - BETA_REF) / (SHEAR_REF * safe), 0.0)
    real = spec_ref[0] * scale
    imag = spec_ref[1] * scale
    for power in range(3):
        if power:
            real = real * wave_y
            imag = imag * wave_y
        line_ref[power, 0], line_ref[power, 1] = y_lines(real, imag, 1, cos_ref, sin_ref)
    plan = ((2, 0, 0), (0, 2, 0), (0, 0, 2), (0, 1, 1), (1, 0, 1), (1, 1, 0))
    for f, (power_x, power_y, power_z) in enumerate(plan):
        real = line_ref[power_y, 0]
        imag = line_ref[power_y, 1]
        factor = None
        for wave in [wave_x] * power_x + [wave_z] * power_z:
            factor = wave if factor is None else factor * wave
        if factor is not None:
            real = real * factor
            imag = imag * factor
        real, imag = x_lines(real, imag, 1, cos_ref, sin_ref)
        plane_ref[0] = real
        plane_ref[1] = imag
        plane_scatter(plane_ref, f, 6, out_ref)


def plane_green_kernel(place_ref, in_ref, cos_ref, sin_ref, out_ref, plane_ref, spec_ref):
    def ahead(f, carry):
        real, imag = plane_ahead(in_ref, f, 6, cos_ref, sin_ref, plane_ref)
        spec_ref[f, 0] = real
        spec_ref[f, 1] = imag
        return carry

    lax.fori_loop(0, 6, ahead, 0)

    def block(b, carry):
        start = pl.multiple_of(b * 8, 8)
        wave_x, wave_y, wave_z = waves(place_ref, start, 8)
        square = wave_x * wave_x + wave_y * wave_y + wave_z * wave_z
        nonzero = square > 0.0
        safe = jnp.where(nonzero, square, 1.0)
        inverse = 1.0 / safe
        scale = jnp.where(nonzero, inverse * (1.0 / SHEAR_REF), 0.0)
        inverse = inverse * BETA_REF
        rows = pl.ds(start, 8)
        for part in range(2):
            tau = [spec_ref[f, part, rows, :] for f in range(6)]
            force_x = tau[0] * wave_x + tau[5] * wave_y + tau[4] * wave_z
            force_y = tau[5] * wave_x + tau[1] * wave_y + tau[3] * wave_z
            force_z = tau[4] * wave_x + tau[3] * wave_y + tau[2] * wave_z
            along = (wave_x * force_x + wave_y * force_y + wave_z * force_z) * inverse
            moved_x = scale * (along * wave_x - force_x)
            moved_y = scale * (along * wave_y - force_y)
            moved_z = scale * (along * wave_z - force_z)
            spec_ref[0, part, rows, :] = wave_x * moved_x
            spec_ref[1, part, rows, :] = wave_y * moved_y
            spec_ref[2, part, rows, :] = wave_z * moved_z
            spec_ref[3, part, rows, :] = 0.5 * (wave_y * moved_z + wave_z * moved_y)
            spec_ref[4, part, rows, :] = 0.5 * (wave_x * moved_z + wave_z * moved_x)
            spec_ref[5, part, rows, :] = 0.5 * (wave_x * moved_y + wave_y * moved_x)
        return carry

    lax.fori_loop(0, N // 8, block, 0)

    def back(f, carry):
        plane_back(
            spec_ref[f, 0], spec_ref[f, 1], f, 6, cos_ref, sin_ref, plane_ref, out_ref
        )
        return carry

    lax.fori_loop(0, 6, back, 0)


def plane_update_kernel(
    place_ref, in_ref, conc_ref, cos_ref, sin_ref, out_ref, norm_ref, plane_ref
):
    real, imag = plane_ahead(in_ref, 0, 2, cos_ref, sin_ref, plane_ref)
    wave_x, wave_y, wave_z = waves(place_ref, 0, N)
    square = wave_x * wave_x + wave_y * wave_y + wave_z * wave_z
    inverse = 1.0 / (1.0 + TIME_STEP * GRADIENT_ENERGY * square * square)
    real = (conc_ref[0] - TIME_STEP * square * real) * inverse
    imag = (conc_ref[1] - TIME_STEP * square * imag) * inverse
    plane_back(real, imag, 0, 1, cos_ref, sin_ref, plane_ref, out_ref)

    total = in_ref[rows_of(0, 2, 1), :]
    for device in range(1, DEVICES):
        total = total + in_ref[rows_of(device, 2, 1), :]
    total = jnp.broadcast_to(jnp.sum(total, axis=1, keepdims=True), (8, LANES))
    total = total + pltpu.roll(total, 7, 0)
    total = total + pltpu.roll(total, 6, 0)
    norm_ref[...] = jnp.sqrt(total * (1.0 / float(N) ** 3))


def z_sweep_kernel(
    in_ref, conc_ref, back_ref, ahead_ref, strain_ref, out_ref, sum_ref, spec_ref, tau_ref
):
    def inverse(f, carry):
        strain_ref[f] = z_back(in_ref, f, 6, back_ref, spec_ref)
        return carry

    lax.fori_loop(0, 6, inverse, 0)

    def block(b, total):
        rows = pl.ds(pl.multiple_of(b * 8, 8), 8)
        conc = conc_ref[rows, :]
        strain = [strain_ref[f, rows, :] for f in range(6)]
        first = FIRST_LOW + FIRST_RISE * conc
        shear = SHEAR_LOW + SHEAR_RISE * conc
        trace = strain[0] + strain[1] + strain[2]
        normal = (first - FIRST_REF) * trace - (3.0 * first + 2.0 * shear) * EIGEN_STRAIN * conc
        excess = 2.0 * (shear - SHEAR_REF)
        for f in range(6):
            tau = excess * strain[f]
            tau_ref[f, rows, :] = tau + normal if f < 3 else tau
            total = total + strain[f] * strain[f]
        return total

    sum_ref[...] = lax.fori_loop(0, N // 8, block, jnp.zeros((8, CELLS), F32))

    def ahead(f, carry):
        z_ahead(tau_ref[f], f, 6, ahead_ref, out_ref)
        return carry

    lax.fori_loop(0, 6, ahead, 0)


def z_drive_kernel(
    in_ref,
    conc_ref,
    past_ref,
    sum_ref,
    back_ref,
    ahead_ref,
    strain_ref,
    out_ref,
    cells_ref,
    spec_ref,
    drive_ref,
):
    def inverse(f, carry):
        strain = z_back(in_ref, f, 6, back_ref, spec_ref)
        cells_ref[f] = strain
        lines = strain.T
        for low in range(LOW):
            for high in range(HIGH):
                start = (low * HIGH + high) * LY
                strain_ref[f, high * LOW + low] = lines[start : start + LY, :]
        return carry

    lax.fori_loop(0, 6, inverse, 0)

    def block(b, total):
        rows = pl.ds(pl.multiple_of(b * 8, 8), 8)
        conc = conc_ref[rows, :]
        strain = [cells_ref[f, rows, :] for f in range(6)]
        first = FIRST_LOW + FIRST_RISE * conc
        shear = SHEAR_LOW + SHEAR_RISE * conc
        dilation = EIGEN_STRAIN * conc
        part = [strain[f] - dilation for f in range(3)]
        trace = part[0] + part[1] + part[2]
        energy = (
            part[0] * part[0]
            + part[1] * part[1]
            + part[2] * part[2]
            + 2.0 * (strain[3] * strain[3] + strain[4] * strain[4] + strain[5] * strain[5])
        )
        chemical = 2.0 * WELL_HEIGHT * conc * (1.0 - conc) * (1.0 - 2.0 * conc)
        drive_ref[rows, :] = (
            chemical
            + 0.5 * FIRST_RISE * trace * trace
            + SHEAR_RISE * energy
            - EIGEN_STRAIN * (3.0 * first + 2.0 * shear) * trace
        )
        for f in range(6):
            change = strain[f] - past_ref[f, rows, :]
            total = total + change * change
        return total

    total = lax.fori_loop(0, N // 8, block, jnp.zeros((8, CELLS), F32))
    row = lax.broadcasted_iota(jnp.int32, (8, LANES), 0)
    sums = jnp.where(row < 4, fold(sum_ref[...]), fold(total))
    for device in range(DEVICES):
        out_ref[rows_of(device, 2, 1), :] = sums
    z_ahead(drive_ref[...], 0, 2, ahead_ref, out_ref)


def z_last_kernel(in_ref, back_ref, out_ref, spec_ref):
    lines = z_back(in_ref, 0, 1, back_ref, spec_ref).T
    for low in range(LOW):
        for high in range(HIGH):
            start = (low * HIGH + high) * LY
            out_ref[high * LOW + low] = lines[start : start + LY, :]


def call(kernel, name, args, outs, scratch=(), places=0):
    memory = [pltpu.SMEM] * places + [pltpu.VMEM] * (len(args) - places)
    return pl.pallas_call(
        kernel,
        out_shape=[jax.ShapeDtypeStruct(shape, F32) for shape in outs],
        in_specs=[pl.BlockSpec(memory_space=m) for m in memory],
        out_specs=[pl.BlockSpec(memory_space=pltpu.VMEM) for _ in outs],
        scratch_shapes=[pltpu.VMEM(shape, F32) for shape in scratch],
        name=name,
        interpret=INTERPRET,
        compiler_params=pltpu.CompilerParams(vmem_limit_bytes=48 * 1024 * 1024),
    )(*args)


def exchange(array):
    return lax.all_to_all(array, AXES, split_axis=0, concat_axis=0, tiled=True)


def wire(fields):
    return (DEVICES * fields * LOW, LANES)


BLOCK = (LX, LY, N)
CELL = (N, CELLS)
PLANE = (2, N, N)


def shards(concentration):
    cosine, sine, ahead, back = [jnp.asarray(table) for table in build_tables()]
    place = lax.axis_index(AXES).astype(jnp.int32)[None]

    conc, data = call(
        source_kernel, "source", (concentration, ahead), [CELL, wire(2)], [(CELLS, N)]
    )
    data = exchange(data)
    data, conc_spec = call(
        plane_first_kernel,
        "plane_first",
        (place, data, cosine, sine),
        [wire(6), PLANE],
        [PLANE, PLANE, (3, *PLANE)],
        places=1,
    )
    data = exchange(data)
    past, data, sums = call(
        z_sweep_kernel,
        "z_sweep",
        (data, conc, back, ahead),
        [(6, *CELL), wire(6), (8, CELLS)],
        [CELL, (6, *CELL)],
    )
    data = exchange(data)
    (data,) = call(
        plane_green_kernel,
        "plane_green",
        (place, data, cosine, sine),
        [wire(6)],
        [PLANE, (6, *PLANE)],
        places=1,
    )
    data = exchange(data)
    strain, data = call(
        z_drive_kernel,
        "z_drive",
        (data, conc, past, sums, back, ahead),
        [(6, *BLOCK), wire(2)],
        [(6, *CELL), CELL, CELL],
    )
    data = exchange(data)
    data, norms = call(
        plane_update_kernel,
        "plane_update",
        (place, data, conc_spec, cosine, sine),
        [wire(1), (8, LANES)],
        [PLANE],
        places=1,
    )
    data = exchange(data)
    (conc_next,) = call(z_last_kernel, "z_last", (data, back), [BLOCK], [CELL])
    return conc_next, strain, norms[::4, 0]


def solution(mesh):
    whole = Mesh(mesh.devices.reshape(4, 2, 4, 4), AXES)
    row, col = AXES[:2], AXES[2:]
    return jax.shard_map(
        shards,
        mesh=whole,
        in_specs=(P(row, col, None),),
        out_specs=(P(row, col, None), P(None, row, col, None), P()),
        check_vma=False,
    )
```

time: 1140 us -> 279 us (0.24); the launches traced: 1130 us -> 279 us
  matrix products: 389 us -> 0 us
  local copies, waits for them, and re-layouts: 263 us -> 2.08 us
  blocking collectives: 300 us -> 161 us
  waiting for transfers between devices: 124 us -> 32.4 us
  Pallas kernels: 0 us -> 66.2 us
  other arithmetic: 26.5 us -> 0.63 us
    dot_general x18 -> x0, matrix products: 389 us -> none  [contract(): jnp.einsum(form, data, table, precision=lax.Precision.HIGHEST, preferred_...]
    reshape x25 -> x0, local copies, waits for them, and re-layouts: 236 us -> none  [the longest x6 86.4 us: inverse_col(): spectrum = spectrum.reshape(members, 2, ncols, kz_local, local_x * local_y)]
    all_to_all x8 -> x4, blocking collectives: 268 us -> 161 us  [exchange(): return lax.all_to_all(array, AXES, split_axis=0, concat_axis=0, tiled=True)]
    all_to_all x4 -> x2, waiting for transfers between devices: 124 us -> 32.4 us  [exchange(): return lax.all_to_all(array, AXES, split_axis=0, concat_axis=0, tiled=True)]
    pallas_call x0 -> x7, Pallas kernels: none -> 66.2 us  [call(): pl.pallas_call(kernel, out_shape=[jax.ShapeDtypeStruct(shape, F32) for sh...]
    psum x4 -> x0, blocking collectives: 32.1 us -> none  [one_axis_at_a_time(): shard = lax.psum(shard, axis)]
    unnamed x20 -> x0, other arithmetic: 12.3 us -> none
    all_to_all x4 -> x2, starting transfers between devices: 24 us -> 16.1 us  [exchange(): return lax.all_to_all(array, AXES, split_axis=0, concat_axis=0, tiled=True)]
  transfers between devices with their start and end apart: 4 -> 2, of which waited for: 3 -> 2; matrix products, arithmetic and copies ran while one was open for 1% -> 0% of each run, Pallas kernels for 0% -> 0%
where the time goes in v1:
time: 279 us
  blocking collectives  161 us (58%)
  Pallas kernels  66.2 us (24%)
  waiting for transfers between devices  32.4 us (12%)
  starting transfers between devices  16.1 us (6%)
    all_to_all x4, blocking collectives, exchange(): return lax.all_to_all(array, AXES, split_axis=0, concat_axis=0, tiled=True)  161 us
    pallas_call x7, Pallas kernels, call(): pl.pallas_call(kernel, out_shape=[jax.ShapeDtypeStruct(shape, F32) for sh...  66.2 us
    all_to_all x2, waiting for transfers between devices, exchange(): return lax.all_to_all(array, AXES, split_axis=0, concat_axis=0, tiled=True)  32.4 us
    all_to_all x2, starting transfers between devices, exchange(): return lax.all_to_all(array, AXES, split_axis=0, concat_axis=0, tiled=True)  16.1 us
  transfers between devices with their start and end apart: 2, of which 2 were waited for; matrix products, arithmetic and copies ran while one was open for 0% of the time, Pallas kernels for 0%

profile of v1, /device:TPU:1, one launch (start us, length us, event | category | flops | bytes accessed | tf_op | source)
XLA Modules:
  0.0 278.7 jit_solution(14522532397801867123)
XLA Ops:
  0.6 0.0 copy-start
  0.6 1.0 copy-done
  1.6 1.0 copy-done.6
  2.7 2.4 source.1
  5.1 11.5 %all-to-all-start = ((f32[128,16,128]{2,1,0:T(8,128)}), f32[128,16,128]{2,1,0:T(8,128)S(1)}, u32[]{:S(2)}, u32[]{:S(2)}) async-start(f32[128,16,128]{2,1,0:T(8,128)} %bitcast.1), calls=%async_computation | async-start | bytes 2097152 | tf_op jit(solution)/shard_map/all_to_all | solution.py:436
  16.6 18.9 %all-to-all-done = f32[128,16,128]{2,1,0:T(8,128)S(1)} async-done(((f32[128,16,128]{2,1,0:T(8,128)}), f32[128,16,128]{2,1,0:T(8,128)S(1)}, u32[]{:S(2)}, u32[]{:S(2)}) %all-to-all-start) | async-done | bytes 1048608 | tf_op jit(solution)/shard_map/all_to_all | solution.py:436
  35.5 0.0 copy-done.4
  35.5 0.0 copy-done.5
  35.5 7.9 %plane_first.1 = (f32[6144,128]{1,0:T(8,128)S(1)}, f32[2,256,256]{2,1,0:T(8,128)S(1)}) custom-call(s32[1]{0:T(128)} %bitcast.place_ref, f32[2048,128]{1,0:T(8,128)S(1)} %bitcast.16, bf16[2,256,256]{2,1,0:T(8,128)(2,1)S(1)} %copy-done.5, bf16[2,256,256]{2,1,0:T(8,128)(2,1)S(1)} %copy-done.4), custom_call_target="tpu_custom_call" | custom-call | tf_op jit(solution)/shard_map/plane_first/pallas_call | solution.py:423
  43.4 0.0 copy-start.1
  43.4 0.0 copy-start.3
  43.4 45.1 %all_to_all.66 = f32[128,48,128]{2,1,0:T(8,128)} all-to-all(f32[128,48,128]{2,1,0:T(8,128)S(1)} %bitcast.17), channel_id=1, replica_groups=mesh['row_0'=4,'row_1'=2,'col_0'=4,'col_1'=4] {'row_0','row_1','col_0','..., dimensions={0} | all-to-all | bytes 6291456 | tf_op jit(solution)/shard_map/all_to_all | solution.py:436
  88.6 12.4 %z_sweep.1 = (f32[6,256,512]{2,1,0:T(8,128)S(1)}, f32[6144,128]{1,0:T(8,128)}, f32[8,512]{1,0:T(8,128)S(1)}) custom-call(f32[6144,128]{1,0:T(8,128)} %bitcast.20, f32[256,512]{1,0:T(8,128)S(1)} %get-tuple-element.16.conc_ref, bf16[2,256,256]{2,1,0:T(8,128)(2,1)S(1)} %copy-done.3, bf16[3,256,256]{2,1,0:T(8,128)(2,1)S(1)} %copy-done.1), custom_call_target="tpu_custom_call" | custom-call | tf_op jit(solution)/shard_map/z_sweep/pallas_call | solution.py:423
  100.9 46.0 %all_to_all.67 = f32[128,48,128]{2,1,0:T(8,128)} all-to-all(f32[128,48,128]{2,1,0:T(8,128)} %bitcast.22), channel_id=1, replica_groups=mesh['row_0'=4,'row_1'=2,'col_0'=4,'col_1'=4] {'row_0','row_1','col_0','..., dimensions={0} | all-to-all | bytes 6291456 | tf_op jit(solution)/shard_map/all_to_all | solution.py:436
  147.0 0.0 copy-done.2
  147.0 28.4 %plane_green.1 = f32[6144,128]{1,0:T(8,128)S(1)} custom-call(s32[1]{0:T(128)} %bitcast.place_ref, f32[6144,128]{1,0:T(8,128)} %bitcast.21, bf16[2,256,256]{2,1,0:T(8,128)(2,1)S(1)} %copy-done.5, bf16[2,256,256]{2,1,0:T(8,128)(2,1)S(1)} %copy-done.4), custom_call_target="tpu_custom_call" | custom-call | tf_op jit(solution)/shard_map/plane_green/pallas_call | solution.py:423
  175.4 45.4 %all_to_all.68 = f32[128,48,128]{2,1,0:T(8,128)S(1)} all-to-all(f32[128,48,128]{2,1,0:T(8,128)S(1)} %bitcast.14), channel_id=1, replica_groups=mesh['row_0'=4,'row_1'=2,'col_0'=4,'col_1'=4] {'row_0','row_1','col_0','..., dimensions={0} | all-to-all | bytes 6291456 | tf_op jit(solution)/shard_map/all_to_all | solution.py:436
  220.8 8.9 %z_drive.1 = (f32[6,32,16,256]{3,2,1,0:T(8,128)}, f32[2048,128]{1,0:T(8,128)S(1)}) custom-call(f32[6144,128]{1,0:T(8,128)S(1)} %bitcast.13, f32[256,512]{1,0:T(8,128)S(1)} %get-tuple-element.16.conc_ref, f32[6,256,512]{2,1,0:T(8,128)} %copy-done.2, f32[8,512]{1,0:T(8,128)S(1)} %get-tuple-element.19.sum_ref, bf16[2,256,256]{2,1,0:T(8,128)(2,1)S(1)} %copy-done.3, ...), custom_call_target="tpu_custom_call" | custom-call | tf_op jit(solution)/shard_map/z_drive/pallas_call | solution.py:423
  229.7 24.0 %all_to_all.69 = f32[128,16,128]{2,1,0:T(8,128)S(1)} all-to-all(f32[128,16,128]{2,1,0:T(8,128)S(1)} %bitcast.19), channel_id=1, replica_groups=mesh['row_0'=4,'row_1'=2,'col_0'=4,'col_1'=4] {'row_0','row_1','col_0','..., dimensions={0} | all-to-all | bytes 2097152 | tf_op jit(solution)/shard_map/all_to_all | solution.py:436
  253.7 4.7 %plane_update.1 = (f32[1024,128]{1,0:T(8,128)}, f32[8,128]{1,0:T(8,128)S(1)}) custom-call(s32[1]{0:T(128)} %bitcast.place_ref, f32[2048,128]{1,0:T(8,128)S(1)} %bitcast.15, f32[2,256,256]{2,1,0:T(8,128)S(1)} %get-tuple-element.21.conc_ref, bf16[2,256,256]{2,1,0:T(8,128)(2,1)S(1)} %copy-done.5, bf16[2,256,256]{2,1,0:T(8,128)(2,1)S(1)} %copy-done.4), custom_call_target="tpu_custom_call" | custom-call | tf_op jit(solution)/shard_map/plane_update/pallas_call | solution.py:423
  258.4 4.6 %all-to-all-start.5 = ((f32[128,8,128]{2,1,0:T(8,128)}), f32[128,8,128]{2,1,0:T(8,128)S(1)}, u32[]{:S(2)}, u32[]{:S(2)}) async-start(f32[128,8,128]{2,1,0:T(8,128)} %bitcast.11), calls=%async_computation.5 | async-start | bytes 1048576 | tf_op jit(solution)/shard_map/all_to_all | solution.py:436
  263.0 0.6 reduce
  263.7 13.5 %all-to-all-done.5 = f32[128,8,128]{2,1,0:T(8,128)S(1)} async-done(((f32[128,8,128]{2,1,0:T(8,128)}), f32[128,8,128]{2,1,0:T(8,128)S(1)}, u32[]{:S(2)}, u32[]{:S(2)}) %all-to-all-start.5) | async-done | bytes 524320 | tf_op jit(solution)/shard_map/all_to_all | solution.py:436
  277.2 1.5 z_last.1
  (7 shorter events, 0.0 us)
Async XLA Ops:
  0.6 1.0 copy-start
  1.6 1.0 copy-start.6
  2.7 32.8 %copy-start.4 = (bf16[2,256,256]{2,1,0:T(8,128)(2,1)S(1)}, bf16[2,256,256]{2,1,0:T(8,128)(2,1)}, u32[]{:S(2)}) copy-start(bf16[2,256,256]{2,1,0:T(8,128)(2,1)} %constant.32.clone.sin_ref) | copy-start | bytes 786436
  2.7 32.8 %copy-start.5 = (bf16[2,256,256]{2,1,0:T(8,128)(2,1)S(1)}, bf16[2,256,256]{2,1,0:T(8,128)(2,1)}, u32[]{:S(2)}) copy-start(bf16[2,256,256]{2,1,0:T(8,128)(2,1)} %constant.31.clone.cos_ref) | copy-start | bytes 786436
  5.1 30.4 %all-to-all-start = ((f32[128,16,128]{2,1,0:T(8,128)}), f32[128,16,128]{2,1,0:T(8,128)S(1)}, u32[]{:S(2)}, u32[]{:S(2)}) async-start(f32[128,16,128]{2,1,0:T(8,128)} %bitcast.1), calls=%async_computation | async-start | bytes 2097152 | tf_op jit(solution)/shard_map/all_to_all | solution.py:436
  43.4 45.2 %copy-start.1 = (bf16[3,256,256]{2,1,0:T(8,128)(2,1)S(1)}, bf16[3,256,256]{2,1,0:T(8,128)(2,1)}, u32[]{:S(2)}) copy-start(bf16[3,256,256]{2,1,0:T(8,128)(2,1)} %constant.33.clone.ahead_ref) | copy-start | bytes 1179652
  43.4 45.2 %copy-start.3 = (bf16[2,256,256]{2,1,0:T(8,128)(2,1)S(1)}, bf16[2,256,256]{2,1,0:T(8,128)(2,1)}, u32[]{:S(2)}) copy-start(bf16[2,256,256]{2,1,0:T(8,128)(2,1)} %constant.34.clone.back_ref) | copy-start | bytes 786436
  100.9 46.1 %copy-start.2 = (f32[6,256,512]{2,1,0:T(8,128)}, f32[6,256,512]{2,1,0:T(8,128)S(1)}, u32[]{:S(2)}) copy-start(f32[6,256,512]{2,1,0:T(8,128)S(1)} %get-tuple-element.18.past_ref) | copy-start | bytes 9437188
  258.4 18.8 %all-to-all-start.5 = ((f32[128,8,128]{2,1,0:T(8,128)}), f32[128,8,128]{2,1,0:T(8,128)S(1)}, u32[]{:S(2)}, u32[]{:S(2)}) async-start(f32[128,8,128]{2,1,0:T(8,128)} %bitcast.11), calls=%async_computation.5 | async-start | bytes 1048576 | tf_op jit(solution)/shard_map/all_to_all | solution.py:436

commit v2 on v1

v2 whole, which is shorter than its diff:
```python
import math
from functools import partial

import jax
import jax.numpy as jnp
import numpy as np
from jax import lax
from jax.experimental import pallas as pl
from jax.experimental.pallas import tpu as pltpu
from jax.sharding import Mesh
from jax.sharding import PartitionSpec as P

AXES = ("row_0", "row_1", "col_0", "col_1")

FIRST_LOW = 1.0
FIRST_RISE = 0.6
SHEAR_LOW = 0.7
SHEAR_RISE = 0.8
FIRST_REF = 1.3
SHEAR_REF = 1.1
BETA_REF = 2.4 / 3.5
EIGEN_STRAIN = 0.5
WELL_HEIGHT = 1.0
TIME_STEP = 0.5
GRADIENT_ENERGY = 0.5

N = 256
HALF = N // 2
ROWS = 8
COLS = 16
DEVICES = ROWS * COLS
LX = N // ROWS
LY = N // COLS
LOW = 8
HIGH = LX // LOW
CELLS = LX * LY
LANES = 128
UNIT = 2.0 * math.pi / N
F32 = jnp.float32
BF16 = jnp.bfloat16
INTERPRET = False
UNROLL = 1
SOURCE_ROWS = 2 * LOW + 1
FIRST_ROWS = 5 * LOW
SWEEP_ROWS = 6 * LOW
DRIVE_ROWS = LOW
LAST_ROWS = LOW + 1
FIRST_FIELDS = (0, 1, 3, 4, 5)
TRACE = -(1.0 - BETA_REF) / SHEAR_REF


def pieces_of(table, count):
    rest = table.astype(np.float32)
    pieces = []
    for _ in range(count):
        piece = rest.astype(jnp.bfloat16)
        rest = rest - piece.astype(np.float32)
        pieces.append(piece)
    return np.stack(pieces)


def build_tables():
    index = np.arange(N)
    half = np.arange(HALF)
    angle = 2.0 * np.pi / N * (index[:, None] * index[None, :] % N)
    cosine = np.cos(angle)
    sine = np.sin(angle)
    lines = []
    for odd in range(2):
        angle = 2.0 * np.pi / N * ((2 * half[:, None] + odd) * half[None, :] % N)
        lines.append(
            np.block([[np.cos(angle), np.sin(angle)], [-np.sin(angle), np.cos(angle)]])
        )
    line_ahead = np.stack([pieces_of(line, 2) for line in lines])
    line_back = np.stack([pieces_of(line.T, 2) for line in lines])
    ahead = np.concatenate([cosine[:HALF], -sine[:HALF]], axis=0)
    weight = np.where(half == 0, 1.0, 2.0) / float(N) ** 3
    back = np.concatenate([cosine[:, :HALF] * weight, -sine[:, :HALF] * weight], axis=1)
    return line_ahead, line_back, pieces_of(ahead, 3), pieces_of(back, 2)


def split(value, count):
    pieces = []
    for i in range(count):
        piece = value.astype(BF16)
        pieces.append(piece)
        if i + 1 < count:
            value = value - piece.astype(F32)
    return pieces


def product(left, right):
    count = len(right)
    total = None
    for order in reversed(range(count)):
        for i in range(order + 1):
            term = jnp.dot(left[i], right[order - i], preferred_element_type=F32)
            total = term if total is None else total + term
    return total


def table(ref):
    return [ref[i] for i in range(ref.shape[0])]


def swap_lanes(parts, granule):
    parts = list(parts)
    axis = parts[0].ndim - 1
    lane = lax.broadcasted_iota(jnp.int32, parts[0].shape, axis)
    step = 1
    while step < len(parts):
        width = granule * step
        low = (lane & width) == 0
        for i in range(len(parts)):
            if i & step == 0:
                a, b = parts[i], parts[i + step]
                parts[i] = jnp.where(low, a, pltpu.roll(b, width, axis))
                parts[i + step] = jnp.where(low, pltpu.roll(a, LANES - width, axis), b)
        step *= 2
    return parts


def peers_of(row, pitch):
    return pl.ds(row, DEVICES, stride=pitch)


def z_ahead(value, f, pitch, ahead_ref, out_ref):
    spectrum = product(table(ahead_ref), split(value, 3))
    for t in range(LOW // 2):
        lanes = slice(t * LANES, (t + 1) * LANES)
        parts = swap_lanes([spectrum[:HALF, lanes], spectrum[HALF:, lanes]], LANES // 2)
        for i in range(2):
            out_ref[peers_of(f * LOW + 2 * t + i, pitch), :] = parts[i]


def z_back(in_ref, f, pitch, back_ref, spec_ref):
    for t in range(LOW // 2):
        lanes = slice(t * LANES, (t + 1) * LANES)
        parts = [in_ref[peers_of(f * LOW + 2 * t + i, pitch), :] for i in range(2)]
        real, imag = swap_lanes(parts, LANES // 2)
        spec_ref[:HALF, lanes] = real
        spec_ref[HALF:, lanes] = imag
    return product(table(back_ref), split(spec_ref[...], 2))


def rows_of(peer, f, pitch):
    start = peer * pitch + f * LOW
    return pl.ds(start if isinstance(start, int) else pl.multiple_of(start, LOW), LOW)


def plane_row(part, i, high):
    return part * HALF + i % 4 * LX + high * LOW


def plane_ahead(in_ref, f, pitch, ahead_ref, plane_ref):
    for i in range(ROWS // 2):
        for h in range(2):
            near, far = [
                swap_lanes(
                    [in_ref[rows_of(k * COLS + h * 8 + j, f, pitch), :] for j in range(8)], LY
                )
                for k in (i, i + ROWS // 2)
            ]
            for g in range(8):
                row = plane_row(g // HIGH, i, g % HIGH)
                lanes = slice(h * LANES, (h + 1) * LANES)
                plane_ref[0, row : row + LOW, lanes] = near[g] + far[g]
                plane_ref[1, row : row + LOW, lanes] = near[g] - far[g]
    near, far = [], []
    for b in range(2):
        lines = product(table(ahead_ref.at[b]), split(plane_ref[b], 2))
        near.append(jnp.concatenate([lines[:HALF, :HALF], lines[HALF:, :HALF]], axis=1))
        far.append(jnp.concatenate([lines[:HALF, HALF:], lines[HALF:, HALF:]], axis=1))
    near = jnp.concatenate(near, axis=0)
    far = jnp.concatenate(far, axis=0)
    return near + far, near - far


def plane_spectrum(in_ref, f, pitch, ahead_ref, back_ref, plane_ref):
    even, odd = plane_ahead(in_ref, f, pitch, ahead_ref, plane_ref)
    return (
        product(split(even, 2), table(back_ref.at[0])),
        product(split(odd, 2), table(back_ref.at[1])),
    )


def y_back(even, odd, ahead_ref):
    even = product(split(even, 2), table(ahead_ref.at[0]))
    odd = product(split(odd, 2), table(ahead_ref.at[1]))
    near = even + odd
    far = even - odd
    return (
        jnp.concatenate([near[:, :HALF], far[:, :HALF]], axis=1),
        jnp.concatenate([near[:, HALF:], far[:, HALF:]], axis=1),
    )


def x_back(real, imag, f, pitch, back_ref, plane_ref, out_ref):
    lines = []
    for b in range(2):
        rows = slice(b * HALF, (b + 1) * HALF)
        data = jnp.concatenate([real[rows], imag[rows]], axis=0)
        lines.append(product(table(back_ref.at[b]), split(data, 2)))
    plane_ref[0] = lines[0] + lines[1]
    plane_ref[1] = lines[0] - lines[1]
    for i in range(ROWS):
        for h in range(2):
            parts = []
            for g in range(8):
                row = plane_row(g // HIGH, i, g % HIGH)
                parts.append(plane_ref[i // 4, row : row + LOW, h * LANES : (h + 1) * LANES])
            parts = swap_lanes(parts, LY)
            for j in range(8):
                out_ref[rows_of(i * COLS + h * 8 + j, f, pitch), :] = parts[j]


def signed(index):
    return jnp.where(index < HALF, index, index - N).astype(F32) * UNIT


def row_waves(start, count, lanes):
    row = lax.broadcasted_iota(jnp.int32, (count, lanes), 0) + start
    return signed(2 * (row % HALF) + row // HALF)


def waves(place_ref, branch, start, count):
    shape = (count, N)
    lane = lax.broadcasted_iota(jnp.int32, shape, 1)
    wave_y = signed(2 * (lane % HALF) + branch)
    wave_z = jnp.full(shape, place_ref[0], jnp.int32).astype(F32) * UNIT
    return row_waves(start, count, N), wave_y, wave_z


def squares(total):
    total = sum(total[:, t * LANES : (t + 1) * LANES] for t in range(CELLS // LANES))
    total = jnp.sum(total, axis=0, keepdims=True)
    return total + pltpu.roll(total, LANES // 2, 1)


def source_of(conc):
    first = FIRST_LOW + FIRST_RISE * conc
    shear = SHEAR_LOW + SHEAR_RISE * conc
    return -(3.0 * first + 2.0 * shear) * EIGEN_STRAIN * conc


def source_kernel(conc_ref, ahead_ref, cells_ref, out_ref, lines_ref):
    for low in range(LOW):
        for high in range(HIGH):
            start = (low * HIGH + high) * LY
            lines_ref[start : start + LY, :] = conc_ref[high * LOW + low]
    conc = lines_ref[...].T
    cells_ref[...] = conc
    source = source_of(conc)
    total = jnp.sum(source.reshape(N // 8, 8, CELLS), axis=0)
    total = sum(total[:, t * LANES : (t + 1) * LANES] for t in range(CELLS // LANES))
    total = jnp.sum(total, axis=0, keepdims=True)
    out_ref[peers_of(2 * LOW, SOURCE_ROWS), :] = jnp.broadcast_to(total, (DEVICES, LANES))
    z_ahead(source, 0, SOURCE_ROWS, ahead_ref, out_ref)
    z_ahead(conc, 1, SOURCE_ROWS, ahead_ref, out_ref)


def plane_first_kernel(place_ref, in_ref, ahead_ref, back_ref, out_ref, plane_ref, line_ref):
    data = list(plane_spectrum(in_ref, 0, SOURCE_ROWS, ahead_ref, back_ref, plane_ref))
    wave_y = []
    for b in range(2):
        wave_x, wave, wave_z = waves(place_ref, b, 0, N)
        wave_y.append(wave)
        square = wave_x * wave_x + wave * wave + wave_z * wave_z
        nonzero = square > 0.0
        safe = jnp.where(nonzero, square, 1.0)
        data[b] = data[b] * jnp.where(nonzero, TRACE / safe, 0.0)
    for power in range(3):
        if power:
            data = [data[b] * wave_y[b] for b in range(2)]
        line_ref[power, 0], line_ref[power, 1] = y_back(data[0], data[1], ahead_ref)
    wave_x = row_waves(0, N, N)
    wave_z = jnp.full((N, N), place_ref[0], jnp.int32).astype(F32) * UNIT
    plan = ((2, 0, 0), (0, 2, 0), (0, 1, 1), (1, 0, 1), (1, 1, 0))
    for f, (power_x, power_y, power_z) in enumerate(plan):
        real = line_ref[power_y, 0]
        imag = line_ref[power_y, 1]
        factor = None
        for wave in [wave_x] * power_x + [wave_z] * power_z:
            factor = wave if factor is None else factor * wave
        if factor is not None:
            real = real * factor
            imag = imag * factor
        x_back(real, imag, f, FIRST_ROWS, back_ref, plane_ref, out_ref)


def aside_first_kernel(in_ref, cells_ref, ahead_ref, back_ref, conc_ref, trace_ref, plane_ref):
    conc_ref[0], conc_ref[1] = plane_spectrum(
        in_ref, 1, SOURCE_ROWS, ahead_ref, back_ref, plane_ref
    )
    mean = jnp.sum(in_ref[peers_of(2 * LOW, SOURCE_ROWS), :]) * (1.0 / float(N) ** 3)
    source = source_of(cells_ref[...])
    row = lax.broadcasted_iota(jnp.int32, (N, CELLS), 0)
    edge = jnp.where(row % 2 == 0, source, -source)
    edge = jnp.sum(edge, axis=0, keepdims=True) * (1.0 / N)
    edge = jnp.where(row % 2 == 0, edge, -edge)
    trace_ref[...] = TRACE * (source - edge - mean)


def z_sweep_kernel(
    in_ref, cells_ref, trace_ref, back_ref, ahead_ref, strain_ref, out_ref, spec_ref, tau_ref
):
    for f, component in enumerate(FIRST_FIELDS):
        strain_ref[component] = z_back(in_ref, f, FIRST_ROWS, back_ref, spec_ref)

    def block(b, carry):
        rows = pl.ds(pl.multiple_of(b * 8, 8), 8)
        conc = cells_ref[rows, :]
        trace = trace_ref[rows, :]
        strain = [strain_ref[f, rows, :] for f in range(6) if f != 2]
        strain.insert(2, trace - strain[0] - strain[1])
        strain_ref[2, rows, :] = strain[2]
        first = FIRST_LOW + FIRST_RISE * conc
        shear = SHEAR_LOW + SHEAR_RISE * conc
        normal = (first - FIRST_REF) * trace + source_of(conc)
        excess = 2.0 * (shear - SHEAR_REF)
        for f in range(6):
            tau = excess * strain[f]
            tau_ref[f, rows, :] = tau + normal if f < 3 else tau
        return carry

    lax.fori_loop(0, N // 8, block, 0)

    def ahead(f, carry):
        z_ahead(tau_ref[f], f, SWEEP_ROWS, ahead_ref, out_ref)
        return carry

    lax.fori_loop(0, 6, ahead, 0, unroll=UNROLL)


def plane_green_kernel(place_ref, in_ref, ahead_ref, back_ref, out_ref, plane_ref, spec_ref):
    def ahead(f, carry):
        spec_ref[f, 0], spec_ref[f, 1] = plane_spectrum(
            in_ref, f, SWEEP_ROWS, ahead_ref, back_ref, plane_ref
        )
        return carry

    lax.fori_loop(0, 6, ahead, 0, unroll=UNROLL)

    def block(b, carry):
        start = pl.multiple_of(b * 8, 8)
        rows = pl.ds(start, 8)
        for branch in range(2):
            wave_x, wave_y, wave_z = waves(place_ref, branch, start, 8)
            square = wave_x * wave_x + wave_y * wave_y + wave_z * wave_z
            nonzero = square > 0.0
            safe = jnp.where(nonzero, square, 1.0)
            inverse = 1.0 / safe
            scale = jnp.where(nonzero, inverse * (1.0 / SHEAR_REF), 0.0)
            inverse = inverse * BETA_REF
            tau = [spec_ref[f, branch, rows, :] for f in range(6)]
            force_x = tau[0] * wave_x + tau[5] * wave_y + tau[4] * wave_z
            force_y = tau[5] * wave_x + tau[1] * wave_y + tau[3] * wave_z
            force_z = tau[4] * wave_x + tau[3] * wave_y + tau[2] * wave_z
            along = (wave_x * force_x + wave_y * force_y + wave_z * force_z) * inverse
            moved_x = scale * (along * wave_x - force_x)
            moved_y = scale * (along * wave_y - force_y)
            moved_z = scale * (along * wave_z - force_z)
            spec_ref[0, branch, rows, :] = wave_x * moved_x
            spec_ref[1, branch, rows, :] = wave_y * moved_y
            spec_ref[2, branch, rows, :] = wave_z * moved_z
            spec_ref[3, branch, rows, :] = 0.5 * (wave_y * moved_z + wave_z * moved_y)
            spec_ref[4, branch, rows, :] = 0.5 * (wave_x * moved_z + wave_z * moved_x)
            spec_ref[5, branch, rows, :] = 0.5 * (wave_x * moved_y + wave_y * moved_x)
        return carry

    lax.fori_loop(0, N // 8, block, 0)

    def back(f, carry):
        real, imag = y_back(spec_ref[f, 0], spec_ref[f, 1], ahead_ref)
        x_back(real, imag, f, SWEEP_ROWS, back_ref, plane_ref, out_ref)
        return carry

    lax.fori_loop(0, 6, back, 0, unroll=UNROLL)


def z_drive_kernel(in_ref, cells_ref, back_ref, ahead_ref, strain_ref, out_ref, spec_ref, drive_ref):
    def inverse(f, carry):
        strain_ref[f] = z_back(in_ref, f, SWEEP_ROWS, back_ref, spec_ref)
        return carry

    lax.fori_loop(0, 6, inverse, 0, unroll=UNROLL)

    def block(b, carry):
        rows = pl.ds(pl.multiple_of(b * 8, 8), 8)
        conc = cells_ref[rows, :]
        strain = [strain_ref[f, rows, :] for f in range(6)]
        first = FIRST_LOW + FIRST_RISE * conc
        shear = SHEAR_LOW + SHEAR_RISE * conc
        dilation = EIGEN_STRAIN * conc
        part = [strain[f] - dilation for f in range(3)]
        trace = part[0] + part[1] + part[2]
        energy = (
            part[0] * part[0]
            + part[1] * part[1]
            + part[2] * part[2]
            + 2.0 * (strain[3] * strain[3] + strain[4] * strain[4] + strain[5] * strain[5])
        )
        chemical = 2.0 * WELL_HEIGHT * conc * (1.0 - conc) * (1.0 - 2.0 * conc)
        drive_ref[rows, :] = (
            chemical
            + 0.5 * FIRST_RISE * trace * trace
            + SHEAR_RISE * energy
            - EIGEN_STRAIN * (3.0 * first + 2.0 * shear) * trace
        )
        return carry

    lax.fori_loop(0, N // 8, block, 0)
    z_ahead(drive_ref[...], 0, DRIVE_ROWS, ahead_ref, out_ref)


def aside_last_kernel(cells_ref, past_ref, strain_ref, sums_ref):
    def one(f, totals):
        def block(b, totals):
            rows = pl.ds(pl.multiple_of(b * 8, 8), 8)
            past = past_ref[f, rows, :]
            change = cells_ref[f, rows, :] - past
            return totals[0] + past * past, totals[1] + change * change

        lines = cells_ref[f].T
        for low in range(LOW):
            for high in range(HIGH):
                start = (low * HIGH + high) * LY
                strain_ref[f, high * LOW + low] = lines[start : start + LY, :]
        return lax.fori_loop(0, N // 8, block, totals)

    zero = jnp.zeros((8, CELLS), F32)
    totals = lax.fori_loop(0, 6, one, (zero, zero))
    lane = lax.broadcasted_iota(jnp.int32, (1, LANES), 1)
    sums = jnp.where(lane < LANES // 2, squares(totals[0]), squares(totals[1]))
    sums_ref[...] = jnp.broadcast_to(sums, (8, LANES))


def plane_update_kernel(
    place_ref, in_ref, conc_ref, sums_ref, ahead_ref, back_ref, out_ref, plane_ref
):
    data = list(plane_spectrum(in_ref, 0, DRIVE_ROWS, ahead_ref, back_ref, plane_ref))
    for b in range(2):
        wave_x, wave_y, wave_z = waves(place_ref, b, 0, N)
        square = wave_x * wave_x + wave_y * wave_y + wave_z * wave_z
        denominator = 1.0 + TIME_STEP * GRADIENT_ENERGY * square * square
        data[b] = (conc_ref[b] - TIME_STEP * square * data[b]) / denominator
    real, imag = y_back(data[0], data[1], ahead_ref)
    x_back(real, imag, 0, LAST_ROWS, back_ref, plane_ref, out_ref)
    out_ref[peers_of(LOW, LAST_ROWS), :] = jnp.broadcast_to(sums_ref[:1, :], (DEVICES, LANES))


def z_last_kernel(in_ref, back_ref, out_ref, norm_ref, spec_ref):
    sums = in_ref[peers_of(LOW, LAST_ROWS), :]
    lane = lax.broadcasted_iota(jnp.int32, sums.shape, 1)
    row = lax.broadcasted_iota(jnp.int32, (8, LANES), 0)
    first = jnp.sum(jnp.where(lane < LANES // 2, sums, 0.0))
    second = jnp.sum(jnp.where(lane < LANES // 2, 0.0, sums))
    norm_ref[...] = jnp.sqrt(jnp.where(row == 0, first, second) * (1.0 / float(N) ** 3))
    lines = z_back(in_ref, 0, LAST_ROWS, back_ref, spec_ref).T
    for low in range(LOW):
        for high in range(HIGH):
            start = (low * HIGH + high) * LY
            out_ref[high * LOW + low] = lines[start : start + LY, :]


def call(kernel, name, args, outs, scratch=(), places=0, mib=24):
    memory = [pltpu.SMEM] * places + [pltpu.VMEM] * (len(args) - places)
    return pl.pallas_call(
        kernel,
        out_shape=[jax.ShapeDtypeStruct(shape, F32) for shape in outs],
        in_specs=[pl.BlockSpec(memory_space=m) for m in memory],
        out_specs=[pl.BlockSpec(memory_space=pltpu.VMEM) for _ in outs],
        scratch_shapes=[pltpu.VMEM(shape, F32) for shape in scratch],
        name=name,
        interpret=INTERPRET,
        compiler_params=pltpu.CompilerParams(vmem_limit_bytes=mib * 1024 * 1024),
    )(*args)


def exchange(array):
    rows = array.reshape(DEVICES, array.shape[0] // DEVICES * LANES)
    rows = lax.all_to_all(rows, AXES, split_axis=0, concat_axis=0, tiled=True)
    return rows.reshape(array.shape)


def wire(pitch):
    return (DEVICES * pitch, LANES)


BLOCK = (LX, LY, N)
CELL = (N, CELLS)
PLANE = (2, N, N)


def shards(concentration):
    line_ahead, line_back, ahead, back = [jnp.asarray(table) for table in build_tables()]
    place = lax.axis_index(AXES).astype(jnp.int32)[None]

    cells, data = call(
        source_kernel, "source", (concentration, ahead), [CELL, wire(SOURCE_ROWS)], [(CELLS, N)]
    )
    source = exchange(data)
    (data,) = call(
        plane_first_kernel,
        "plane_first",
        (place, source, line_ahead, line_back),
        [wire(FIRST_ROWS)],
        [PLANE, (3, *PLANE)],
        places=1,
    )
    data = exchange(data)
    conc_spec, trace = call(
        aside_first_kernel,
        "aside_first",
        (source, cells, line_ahead, line_back),
        [PLANE, CELL],
        [PLANE],
    )
    past, data = call(
        z_sweep_kernel,
        "z_sweep",
        (data, cells, trace, back, ahead),
        [(6, *CELL), wire(SWEEP_ROWS)],
        [CELL, (6, *CELL)],
    )
    data = exchange(data)
    (data,) = call(
        plane_green_kernel,
        "plane_green",
        (place, data, line_ahead, line_back),
        [wire(SWEEP_ROWS)],
        [PLANE, (6, *PLANE)],
        places=1,
    )
    data = exchange(data)
    strain, data = call(
        z_drive_kernel,
        "z_drive",
        (data, cells, back, ahead),
        [(6, *CELL), wire(DRIVE_ROWS)],
        [CELL, CELL],
    )
    data = exchange(data)
    strain, sums = call(aside_last_kernel, "aside_last", (strain, past), [(6, *BLOCK), (8, LANES)])
    (data,) = call(
        plane_update_kernel,
        "plane_update",
        (place, data, conc_spec, sums, line_ahead, line_back),
        [wire(LAST_ROWS)],
        [PLANE],
        places=1,
    )
    data = exchange(data)
    conc_next, norms = call(
        z_last_kernel, "z_last", (data, back), [BLOCK, (8, LANES)], [CELL]
    )
    return conc_next, strain, norms[:2, 0]


def solution(mesh):
    whole = Mesh(mesh.devices.reshape(4, 2, 4, 4), AXES)
    row, col = AXES[:2], AXES[2:]
    return jax.shard_map(
        shards,
        mesh=whole,
        in_specs=(P(row, col, None),),
        out_specs=(P(row, col, None), P(None, row, col, None), P()),
        check_vma=False,
    )
```

time: 279 us -> 250 us (0.90)
  blocking collectives: 161 us -> 109 us
  Pallas kernels: 66.2 us -> 43.2 us
  waiting for transfers between devices: 32.4 us -> 53.5 us
  local copies, waits for them, and re-layouts: 2.08 us -> 21 us
  starting transfers between devices: 16.1 us -> 21.7 us
    all_to_all x4 -> x3, blocking collectives: 161 us -> 109 us  [exchange(): rows = lax.all_to_all(rows, AXES, split_axis=0, concat_axis=0, tiled=True)]
    pallas_call x7 -> x9, Pallas kernels: 66.2 us -> 43.2 us  [call(): pl.pallas_call(kernel, out_shape=[jax.ShapeDtypeStruct(shape, F32) for sh...]
    all_to_all x2 -> x3, waiting for transfers between devices: 32.4 us -> 53.5 us  [exchange(): rows = lax.all_to_all(rows, AXES, split_axis=0, concat_axis=0, tiled=True)]
    unnamed x14 -> x48, local copies, waits for them, and re-layouts: 2.06 us -> 20.4 us
    all_to_all x2 -> x3, starting transfers between devices: 16.1 us -> 21.7 us  [exchange(): rows = lax.all_to_all(rows, AXES, split_axis=0, concat_axis=0, tiled=True)]
  transfers between devices with their start and end apart: 2 -> 3, of which waited for: 2 -> 3; matrix products, arithmetic and copies ran while one was open for 0% -> 0% of each run, Pallas kernels for 0% -> 2%
where the time goes in v2:
time: 250 us
  blocking collectives  109 us (44%)
  waiting for transfers between devices  53.5 us (21%)
  Pallas kernels  43.2 us (17%)
  starting transfers between devices  21.7 us (9%)
  local copies, waits for them, and re-layouts  21 us (8%)
    all_to_all x3, blocking collectives, exchange(): rows = lax.all_to_all(rows, AXES, split_axis=0, concat_axis=0, tiled=True)  109 us
    all_to_all x3, waiting for transfers between devices, exchange(): rows = lax.all_to_all(rows, AXES, split_axis=0, concat_axis=0, tiled=True)  53.5 us
    pallas_call x9, Pallas kernels, call(): pl.pallas_call(kernel, out_shape=[jax.ShapeDtypeStruct(shape, F32) for sh...  43.2 us
    all_to_all x3, starting transfers between devices, exchange(): rows = lax.all_to_all(rows, AXES, split_axis=0, concat_axis=0, tiled=True)  21.7 us
    unnamed x48, local copies, waits for them, and re-layouts  20.4 us
  transfers between devices with their start and end apart: 3, of which 3 were waited for; matrix products, arithmetic and copies ran while one was open for 0% of the time, Pallas kernels for 2%

profile of v2, /device:TPU:1, one launch (start us, length us, event | category | flops | bytes accessed | tf_op | source)
XLA Modules:
  0.0 249.5 jit_solution(14739668157801284845)
XLA Ops:
  2.8 1.4 source.1
  6.0 11.5 %all-to-all-start = ((f32[128,1,2176]{2,1,0:T(1,128)}), f32[128,1,2176]{2,1,0:T(1,128)S(1)}, u32[]{:S(2)}, u32[]{:S(2)}) async-start(f32[128,1,2176]{2,1,0:T(1,128)} %bitcast.24), calls=%async_computation | async-start | bytes 2228224 | tf_op jit(solution)/shard_map/all_to_all | solution.py:482
  17.5 19.5 %all-to-all-done = f32[128,1,2176]{2,1,0:T(1,128)S(1)} async-done(((f32[128,1,2176]{2,1,0:T(1,128)}), f32[128,1,2176]{2,1,0:T(1,128)S(1)}, u32[]{:S(2)}, u32[]{:S(2)}) %all-to-all-start) | async-done | bytes 1114144 | tf_op jit(solution)/shard_map/all_to_all | solution.py:482
  37.0 4.4 %plane_first.1 = f32[5120,128]{1,0:T(8,128)S(1)} custom-call(s32[1]{0:T(128)} %bitcast.place_ref, f32[2176,128]{1,0:T(8,128)S(1)} %bitcast.18, bf16[2,2,256,256]{3,2,1,0:T(8,128)(2,1)S(1)} %copy-done.4, bf16[2,2,256,256]{3,2,1,0:T(8,128)(2,1)S(1)} %copy-done.3), custom_call_target="tpu_custom_call" | custom-call | tf_op jit(solution)/shard_map/plane_first/pallas_call | solution.py:468
  41.4 1.5 copy-done
  42.9 4.9 %all-to-all-start.1 = ((f32[128,1,5120]{2,1,0:T(1,128)}), f32[128,1,5120]{2,1,0:T(1,128)S(1)}, u32[]{:S(2)}, u32[]{:S(2)}) async-start(f32[128,1,5120]{2,1,0:T(1,128)} %bitcast.17), calls=%async_computation.1 | async-start | bytes 5242880 | tf_op jit(solution)/shard_map/all_to_all | solution.py:482
  47.7 1.2 copy-done.2
  51.1 1.6 aside_first.1
  54.2 28.3 %all-to-all-done.1 = f32[128,1,5120]{2,1,0:T(1,128)S(1)} async-done(((f32[128,1,5120]{2,1,0:T(1,128)}), f32[128,1,5120]{2,1,0:T(1,128)S(1)}, u32[]{:S(2)}, u32[]{:S(2)}) %all-to-all-start.1) | async-done | bytes 2621472 | tf_op jit(solution)/shard_map/all_to_all | solution.py:482
  85.5 6.7 %z_sweep.1 = (f32[6,256,512]{2,1,0:T(8,128)S(1)}, f32[6144,128]{1,0:T(8,128)S(1)}) custom-call(f32[5120,128]{1,0:T(8,128)S(1)} %bitcast.16, f32[256,512]{1,0:T(8,128)S(1)} %copy-done.9, f32[256,512]{1,0:T(8,128)S(1)} %copy-done.20, bf16[2,256,256]{2,1,0:T(8,128)(2,1)S(1)} %copy-done.16, bf16[3,256,256]{2,1,0:T(8,128)(2,1)S(1)} %copy-done.11), custom_call_target="tpu_custom_call" | custom-call | tf_op jit(solution)/shard_map/z_sweep/pallas_call | solution.py:468
  92.3 1.6 copy-done.12
  93.9 45.4 %all_to_all.54 = f32[128,1,6144]{2,1,0:T(1,128)S(1)} all-to-all(f32[128,1,6144]{2,1,0:T(1,128)S(1)} %bitcast.20), channel_id=1, replica_groups=mesh['row_0'=4,'row_1'=2,'col_0'=4,'col_1'=4] {'row_0','row_1','col_0','..., dimensions={0} | all-to-all | bytes 6291456 | tf_op jit(solution)/shard_map/all_to_all | solution.py:482
  139.2 15.0 %plane_green.1 = f32[6144,128]{1,0:T(8,128)S(1)} custom-call(s32[1]{0:T(128)} %bitcast.place_ref, f32[6144,128]{1,0:T(8,128)S(1)} %bitcast.14, bf16[2,2,256,256]{3,2,1,0:T(8,128)(2,1)S(1)} %copy-done.6, bf16[2,2,256,256]{3,2,1,0:T(8,128)(2,1)S(1)} %copy-done.3), custom_call_target="tpu_custom_call" | custom-call | tf_op jit(solution)/shard_map/plane_green/pallas_call | solution.py:468
  154.3 45.4 %all_to_all.55 = f32[128,1,6144]{2,1,0:T(1,128)S(1)} all-to-all(f32[128,1,6144]{2,1,0:T(1,128)S(1)} %bitcast.15), channel_id=1, replica_groups=mesh['row_0'=4,'row_1'=2,'col_0'=4,'col_1'=4] {'row_0','row_1','col_0','..., dimensions={0} | all-to-all | bytes 6291456 | tf_op jit(solution)/shard_map/all_to_all | solution.py:482
  199.6 5.8 %z_drive.1 = (f32[6,256,512]{2,1,0:T(8,128)S(1)}, f32[1024,128]{1,0:T(8,128)}) custom-call(f32[6144,128]{1,0:T(8,128)S(1)} %bitcast.13, f32[256,512]{1,0:T(8,128)S(1)} %copy-done.9, bf16[2,256,256]{2,1,0:T(8,128)(2,1)S(1)} %copy-done.17, bf16[3,256,256]{2,1,0:T(8,128)(2,1)S(1)} %copy-done.11), custom_call_target="tpu_custom_call" | custom-call | tf_op jit(solution)/shard_map/z_drive/pallas_call | solution.py:468
  205.5 1.7 copy-done.14
  207.1 5.3 %all-to-all-start.4 = ((f32[128,1,1024]{2,1,0:T(1,128)}), f32[128,1,1024]{2,1,0:T(1,128)S(1)}, u32[]{:S(2)}, u32[]{:S(2)}) async-start(f32[128,1,1024]{2,1,0:T(1,128)} %bitcast.9), calls=%async_computation.4 | async-start | bytes 1048576 | tf_op jit(solution)/shard_map/all_to_all | solution.py:482
  212.5 1.9 copy-done.13
  214.4 1.9 copy-done.15
  216.3 4.5 %aside_last.1 = (f32[6,32,16,256]{3,2,1,0:T(8,128)}, f32[8,128]{1,0:T(8,128)S(1)}) custom-call(f32[6,256,512]{2,1,0:T(8,128)S(1)} %copy-done.15, f32[6,256,512]{2,1,0:T(8,128)S(1)} %copy-done.13), custom_call_target="tpu_custom_call" | custom-call | tf_op jit(solution)/shard_map/aside_last/pallas_call | solution.py:468
  220.8 5.7 %all-to-all-done.4 = f32[128,1,1024]{2,1,0:T(1,128)S(1)} async-done(((f32[128,1,1024]{2,1,0:T(1,128)}), f32[128,1,1024]{2,1,0:T(1,128)S(1)}, u32[]{:S(2)}, u32[]{:S(2)}) %all-to-all-start.4) | async-done | bytes 524320 | tf_op jit(solution)/shard_map/all_to_all | solution.py:482
  226.5 2.3 plane_update.1
  228.9 18.6 %all_to_all.56 = f32[128,1,1152]{2,1,0:T(1,128)S(1)} all-to-all(f32[128,1,1152]{2,1,0:T(1,128)S(1)} %bitcast.22), channel_id=1, replica_groups=mesh['row_0'=4,'row_1'=2,'col_0'=4,'col_1'=4] {'row_0','row_1','col_0','..., dimensions={0} | all-to-all | bytes 1179648 | tf_op jit(solution)/shard_map/all_to_all | solution.py:482
  247.4 1.5 z_last.1
  (43 shorter events, 11.3 us)
Async XLA Ops:
  0.6 36.4 %copy-start.3 = (bf16[2,2,256,256]{3,2,1,0:T(8,128)(2,1)S(1)}, bf16[2,2,256,256]{3,2,1,0:T(8,128)(2,1)}, u32[]{:S(2)}) copy-start(bf16[2,2,256,256]{3,2,1,0:T(8,128)(2,1)} %constant.32.clone.back_ref) | copy-start | bytes 1572868
  0.6 36.4 %copy-start.4 = (bf16[2,2,256,256]{3,2,1,0:T(8,128)(2,1)S(1)}, bf16[2,2,256,256]{3,2,1,0:T(8,128)(2,1)}, u32[]{:S(2)}) copy-start(bf16[2,2,256,256]{3,2,1,0:T(8,128)(2,1)} %constant.31.clone.ahead_ref) | copy-start | bytes 1572868
  0.7 1.1 copy-start.10
  1.7 1.0 copy-start.21
  5.0 1.0 copy-start.18
  6.0 31.0 %all-to-all-start = ((f32[128,1,2176]{2,1,0:T(1,128)}), f32[128,1,2176]{2,1,0:T(1,128)S(1)}, u32[]{:S(2)}, u32[]{:S(2)}) async-start(f32[128,1,2176]{2,1,0:T(1,128)} %bitcast.24), calls=%async_computation | async-start | bytes 2228224 | tf_op jit(solution)/shard_map/all_to_all | solution.py:482
  37.0 5.9 %copy-start.1 = (f32[128,1,2176]{2,1,0:T(1,128)}, f32[128,1,2176]{2,1,0:T(1,128)S(1)}, u32[]{:S(2)}) copy-start(f32[128,1,2176]{2,1,0:T(1,128)S(1)} %all-to-all-done) | copy-start | bytes 3342340
  41.4 1.5 copy-start
  42.9 39.6 %copy-start.11 = (bf16[3,256,256]{2,1,0:T(8,128)(2,1)S(1)}, bf16[3,256,256]{2,1,0:T(8,128)(2,1)}, u32[]{:S(2)}) copy-start(bf16[3,256,256]{2,1,0:T(8,128)(2,1)} %constant.33.clone.ahead_ref) | copy-start | bytes 1179652
  42.9 39.6 %all-to-all-start.1 = ((f32[128,1,5120]{2,1,0:T(1,128)}), f32[128,1,5120]{2,1,0:T(1,128)S(1)}, u32[]{:S(2)}, u32[]{:S(2)}) async-start(f32[128,1,5120]{2,1,0:T(1,128)} %bitcast.17), calls=%async_computation.1 | async-start | bytes 5242880 | tf_op jit(solution)/shard_map/all_to_all | solution.py:482
  47.7 1.2 copy-start.2
  49.0 1.0 copy-start.5
  50.0 1.0 copy-start.8
  82.5 1.0 copy-start.9
  83.6 0.9 copy-start.16
  84.5 1.0 copy-start.20
  92.2 1.6 copy-start.12
  93.9 45.4 %copy-start.6 = (bf16[2,2,256,256]{3,2,1,0:T(8,128)(2,1)S(1)}, bf16[2,2,256,256]{3,2,1,0:T(8,128)(2,1)}, u32[]{:S(2)}) copy-start(bf16[2,2,256,256]{3,2,1,0:T(8,128)(2,1)} %constant.31.clone.ahead_ref) | copy-start | bytes 1572868
  154.2 45.4 %copy-start.17 = (bf16[2,256,256]{2,1,0:T(8,128)(2,1)S(1)}, bf16[2,256,256]{2,1,0:T(8,128)(2,1)}, u32[]{:S(2)}) copy-start(bf16[2,256,256]{2,1,0:T(8,128)(2,1)} %constant.34.clone.back_ref) | copy-start | bytes 786436
  205.5 1.7 copy-start.14
  207.1 19.4 %all-to-all-start.4 = ((f32[128,1,1024]{2,1,0:T(1,128)}), f32[128,1,1024]{2,1,0:T(1,128)S(1)}, u32[]{:S(2)}, u32[]{:S(2)}) async-start(f32[128,1,1024]{2,1,0:T(1,128)} %bitcast.9), calls=%async_computation.4 | async-start | bytes 1048576 | tf_op jit(solution)/shard_map/all_to_all | solution.py:482
  212.5 1.9 copy-start.13
  214.4 1.9 copy-start.15
  216.3 10.3 %copy-start.23 = (f32[2,256,256]{2,1,0:T(8,128)S(1)}, f32[2,256,256]{2,1,0:T(8,128)}, u32[]{:S(2)}) copy-start(f32[2,256,256]{2,1,0:T(8,128)} %copy-done.22) | copy-start | bytes 1572868
  (3 other events, 2.4 us)

commit v3 on v2

--- a/solution.py
+++ b/solution.py
@@ -243,15 +243,41 @@
     return -(3.0 * first + 2.0 * shear) * EIGEN_STRAIN * conc
 
 
-def source_kernel(conc_ref, ahead_ref, cells_ref, out_ref, lines_ref):
-    for low in range(LOW):
-        for high in range(HIGH):
-            start = (low * HIGH + high) * LY
-            lines_ref[start : start + LY, :] = conc_ref[high * LOW + low]
-    conc = lines_ref[...].T
+def copy_lines(far, lines_ref, sems, inward):
+    copies = []
+    for high in range(HIGH):
+        pair = (far.at[pl.ds(high * LOW, LOW)], lines_ref.at[:, high])
+        source, target = pair if inward else pair[::-1]
+        copies.append(pltpu.make_async_copy(source, target, sems.at[high]))
+    return copies
+
+
+def source_kernel(
+    place_ref,
+    conc_ref,
+    far_ref,
+    cells_ref,
+    out_ref,
+    edge_ref,
+    lines_ref,
+    ahead_ref,
+    sems,
+    far_sem,
+):
+    copies = copy_lines(conc_ref, lines_ref, sems, True)
+    copies.append(pltpu.make_async_copy(far_ref, ahead_ref, far_sem))
+    for copy in copies:
+        copy.start()
+    for copy in copies:
+        copy.wait()
+    conc = lines_ref[...].reshape(CELLS, N).T
     cells_ref[...] = conc
     source = source_of(conc)
     total = jnp.sum(source.reshape(N // 8, 8, CELLS), axis=0)
+    row = lax.broadcasted_iota(jnp.int32, (8, CELLS), 0)
+    edge = jnp.where(row % 2 == 0, total, -total)
+    edge = jnp.sum(edge, axis=0, keepdims=True) * (1.0 / N)
+    edge_ref[...] = jnp.where(row % 2 == 0, edge, -edge)
     total = sum(total[:, t * LANES : (t + 1) * LANES] for t in range(CELLS // LANES))
     total = jnp.sum(total, axis=0, keepdims=True)
     out_ref[peers_of(2 * LOW, SOURCE_ROWS), :] = jnp.broadcast_to(total, (DEVICES, LANES))
@@ -259,7 +285,11 @@
     z_ahead(conc, 1, SOURCE_ROWS, ahead_ref, out_ref)
 
 
-def plane_first_kernel(place_ref, in_ref, ahead_ref, back_ref, out_ref, plane_ref, line_ref):
+def plane_first_kernel(
+    place_ref, in_ref, ahead_ref, back_ref, out_ref, mean_ref, plane_ref, line_ref
+):
+    mean = jnp.sum(in_ref[peers_of(2 * LOW, SOURCE_ROWS), :]) * (1.0 / float(N) ** 3)
+    mean_ref[...] = jnp.full((8, CELLS), mean, F32)
     data = list(plane_spectrum(in_ref, 0, SOURCE_ROWS, ahead_ref, back_ref, plane_ref))
     wave_y = []
     for b in range(2):
@@ -288,21 +318,19 @@
         x_back(real, imag, f, FIRST_ROWS, back_ref, plane_ref, out_ref)
 
 
-def aside_first_kernel(in_ref, cells_ref, ahead_ref, back_ref, conc_ref, trace_ref, plane_ref):
-    conc_ref[0], conc_ref[1] = plane_spectrum(
-        in_ref, 1, SOURCE_ROWS, ahead_ref, back_ref, plane_ref
-    )
-    mean = jnp.sum(in_ref[peers_of(2 * LOW, SOURCE_ROWS), :]) * (1.0 / float(N) ** 3)
-    source = source_of(cells_ref[...])
-    row = lax.broadcasted_iota(jnp.int32, (N, CELLS), 0)
-    edge = jnp.where(row % 2 == 0, source, -source)
-    edge = jnp.sum(edge, axis=0, keepdims=True) * (1.0 / N)
-    edge = jnp.where(row % 2 == 0, edge, -edge)
-    trace_ref[...] = TRACE * (source - edge - mean)
-
-
 def z_sweep_kernel(
-    in_ref, cells_ref, trace_ref, back_ref, ahead_ref, strain_ref, out_ref, spec_ref, tau_ref
+    in_ref,
+    cells_ref,
+    edge_ref,
+    mean_ref,
+    back_ref,
+    ahead_ref,
+    past_ref,
+    out_ref,
+    strain_ref,
+    spec_ref,
+    tau_ref,
+    sem,
 ):
     for f, component in enumerate(FIRST_FIELDS):
         strain_ref[component] = z_back(in_ref, f, FIRST_ROWS, back_ref, spec_ref)
@@ -310,13 +338,14 @@
     def block(b, carry):
         rows = pl.ds(pl.multiple_of(b * 8, 8), 8)
         conc = cells_ref[rows, :]
-        trace = trace_ref[rows, :]
+        source = source_of(conc)
+        trace = TRACE * (source - edge_ref[...] - mean_ref[...])
         strain = [strain_ref[f, rows, :] for f in range(6) if f != 2]
         strain.insert(2, trace - strain[0] - strain[1])
         strain_ref[2, rows, :] = strain[2]
         first = FIRST_LOW + FIRST_RISE * conc
         shear = SHEAR_LOW + SHEAR_RISE * conc
-        normal = (first - FIRST_REF) * trace + source_of(conc)
+        normal = (first - FIRST_REF) * trace + source
         excess = 2.0 * (shear - SHEAR_REF)
         for f in range(6):
             tau = excess * strain[f]
@@ -324,12 +353,15 @@
         return carry
 
     lax.fori_loop(0, N // 8, block, 0)
+    past = pltpu.make_async_copy(strain_ref, past_ref, sem)
+    past.start()
 
     def ahead(f, carry):
         z_ahead(tau_ref[f], f, SWEEP_ROWS, ahead_ref, out_ref)
         return carry
 
     lax.fori_loop(0, 6, ahead, 0, unroll=UNROLL)
+    past.wait()
 
 
 def plane_green_kernel(place_ref, in_ref, ahead_ref, back_ref, out_ref, plane_ref, spec_ref):
@@ -378,9 +410,24 @@
     lax.fori_loop(0, 6, back, 0, unroll=UNROLL)
 
 
-def z_drive_kernel(in_ref, cells_ref, back_ref, ahead_ref, strain_ref, out_ref, spec_ref, drive_ref):
+def z_drive_kernel(
+    in_ref,
+    cells_ref,
+    back_ref,
+    ahead_ref,
+    far_ref,
+    out_ref,
+    strain_ref,
+    spec_ref,
+    drive_ref,
+    sems,
+):
+    def far(f):
+        return pltpu.make_async_copy(strain_ref.at[f], far_ref.at[f], sems.at[f])
+
     def inverse(f, carry):
         strain_ref[f] = z_back(in_ref, f, SWEEP_ROWS, back_ref, spec_ref)
+        far(f).start()
         return carry
 
     lax.fori_loop(0, 6, inverse, 0, unroll=UNROLL)
@@ -411,9 +458,41 @@
 
     lax.fori_loop(0, N // 8, block, 0)
     z_ahead(drive_ref[...], 0, DRIVE_ROWS, ahead_ref, out_ref)
-
-
-def aside_last_kernel(cells_ref, past_ref, strain_ref, sums_ref):
+    for f in range(6):
+        far(f).wait()
+
+
+def aside_kernel(
+    now_ref,
+    then_ref,
+    source_ref,
+    ahead_ref,
+    back_ref,
+    strain_ref,
+    conc_ref,
+    sums_ref,
+    cells_ref,
+    past_ref,
+    data_ref,
+    lines_ref,
+    plane_ref,
+    now_sems,
+    then_sems,
+    source_sem,
+    out_sems,
+):
+    def now(f):
+        return pltpu.make_async_copy(now_ref.at[f], cells_ref.at[f], now_sems.at[f])
+
+    def then(f):
+        return pltpu.make_async_copy(then_ref.at[f], past_ref.at[f], then_sems.at[f])
+
+    for f in range(6):
+        now(f).start()
+        then(f).start()
+    source = pltpu.make_async_copy(source_ref, data_ref, source_sem)
+    source.start()
+
     def one(f, totals):
         def block(b, totals):
             rows = pl.ds(pl.multiple_of(b * 8, 8), 8)
@@ -421,11 +500,11 @@
             change = cells_ref[f, rows, :] - past
             return totals[0] + past * past, totals[1] + change * change
 
-        lines = cells_ref[f].T
-        for low in range(LOW):
-            for high in range(HIGH):
-                start = (low * HIGH + high) * LY
-                strain_ref[f, high * LOW + low] = lines[start : start + LY, :]
+        now(f).wait()
+        lines_ref[f] = cells_ref[f].T.reshape(LOW, HIGH, LY, N)
+        for copy in copy_lines(strain_ref.at[f], lines_ref.at[f], out_sems.at[f], False):
+            copy.start()
+        then(f).wait()
         return lax.fori_loop(0, N // 8, block, totals)
 
     zero = jnp.zeros((8, CELLS), F32)
@@ -433,6 +512,13 @@
     lane = lax.broadcasted_iota(jnp.int32, (1, LANES), 1)
     sums = jnp.where(lane < LANES // 2, squares(totals[0]), squares(totals[1]))
     sums_ref[...] = jnp.broadcast_to(sums, (8, LANES))
+    source.wait()
+    conc_ref[0], conc_ref[1] = plane_spectrum(
+        data_ref, 1, SOURCE_ROWS, ahead_ref, back_ref, plane_ref
+    )
+    for f in range(6):
+        for copy in copy_lines(strain_ref.at[f], lines_ref.at[f], out_sems.at[f], False):
+            copy.wait()
 
 
 def plane_update_kernel(
@@ -449,32 +535,48 @@
     out_ref[peers_of(LOW, LAST_ROWS), :] = jnp.broadcast_to(sums_ref[:1, :], (DEVICES, LANES))
 
 
-def z_last_kernel(in_ref, back_ref, out_ref, norm_ref, spec_ref):
+def z_last_kernel(in_ref, back_ref, out_ref, norm_ref, spec_ref, lines_ref, sems):
+    lines = z_back(in_ref, 0, LAST_ROWS, back_ref, spec_ref).T
+    lines_ref[...] = lines.reshape(LOW, HIGH, LY, N)
+    copies = copy_lines(out_ref, lines_ref, sems, False)
+    for copy in copies:
+        copy.start()
     sums = in_ref[peers_of(LOW, LAST_ROWS), :]
     lane = lax.broadcasted_iota(jnp.int32, sums.shape, 1)
     row = lax.broadcasted_iota(jnp.int32, (8, LANES), 0)
     first = jnp.sum(jnp.where(lane < LANES // 2, sums, 0.0))
     second = jnp.sum(jnp.where(lane < LANES // 2, 0.0, sums))
-    norm_ref[...] = jnp.sqrt(jnp.where(row == 0, first, second) * (1.0 / float(N) ** 3))
-    lines = z_back(in_ref, 0, LAST_ROWS, back_ref, spec_ref).T
-    for low in range(LOW):
-        for high in range(HIGH):
-            start = (low * HIGH + high) * LY
-            out_ref[high * LOW + low] = lines[start : start + LY, :]
-
-
-def call(kernel, name, args, outs, scratch=(), places=0, mib=24):
-    memory = [pltpu.SMEM] * places + [pltpu.VMEM] * (len(args) - places)
+    norms = jnp.sqrt(jnp.where(row == 0, first, second) * (1.0 / float(N) ** 3))
+    norm_ref[0] = norms[0, 0]
+    norm_ref[1] = norms[1, 0]
+    for copy in copies:
+        copy.wait()
+
+
+SPACES = {"vmem": pltpu.VMEM, "smem": pltpu.SMEM, "hbm": pltpu.HBM}
+
+
+def call(kernel, name, args, outs, scratch=(), sems=(), mib=24):
+    operands = [
+        pltpu.with_memory_space_constraint(value, pltpu.HBM) if space == "hbm" else value
+        for space, value in args
+    ]
     return pl.pallas_call(
         kernel,
-        out_shape=[jax.ShapeDtypeStruct(shape, F32) for shape in outs],
-        in_specs=[pl.BlockSpec(memory_space=m) for m in memory],
-        out_specs=[pl.BlockSpec(memory_space=pltpu.VMEM) for _ in outs],
-        scratch_shapes=[pltpu.VMEM(shape, F32) for shape in scratch],
+        out_shape=[
+            pltpu.HBM(shape, F32) if space == "hbm" else jax.ShapeDtypeStruct(shape, F32)
+            for space, shape in outs
+        ],
+        in_specs=[pl.BlockSpec(memory_space=SPACES[space]) for space, _ in args],
+        out_specs=[pl.BlockSpec(memory_space=SPACES[space]) for space, _ in outs],
+        scratch_shapes=[
+            *[pltpu.VMEM(s, F32) if isinstance(s, tuple) else s for s in scratch],
+            *[pltpu.SemaphoreType.DMA(shape) for shape in sems],
+        ],
         name=name,
         interpret=INTERPRET,
         compiler_params=pltpu.CompilerParams(vmem_limit_bytes=mib * 1024 * 1024),
-    )(*args)
+    )(*operands)
 
 
 def exchange(array):
@@ -490,71 +592,83 @@
 BLOCK = (LX, LY, N)
 CELL = (N, CELLS)
 PLANE = (2, N, N)
+LINES = (LOW, HIGH, LY, N)
+SMALL = (8, CELLS)
 
 
 def shards(concentration):
-    line_ahead, line_back, ahead, back = [jnp.asarray(table) for table in build_tables()]
-    place = lax.axis_index(AXES).astype(jnp.int32)[None]
-
-    cells, data = call(
-        source_kernel, "source", (concentration, ahead), [CELL, wire(SOURCE_ROWS)], [(CELLS, N)]
+    tables = [jnp.asarray(table) for table in build_tables()]
+    line_ahead, line_back, ahead, back = [("vmem", table) for table in tables]
+    place = ("smem", lax.axis_index(AXES).astype(jnp.int32)[None])
+
+    cells, data, edge = call(
+        source_kernel,
+        "source",
+        [place, ("hbm", concentration), ("hbm", tables[2])],
+        [("vmem", CELL), ("vmem", wire(SOURCE_ROWS)), ("vmem", SMALL)],
+        [LINES, pltpu.VMEM((3, N, N), BF16)],
+        [(HIGH,), ()],
     )
     source = exchange(data)
-    (data,) = call(
+    data, mean = call(
         plane_first_kernel,
         "plane_first",
-        (place, source, line_ahead, line_back),
-        [wire(FIRST_ROWS)],
+        [place, ("vmem", source), line_ahead, line_back],
+        [("vmem", wire(FIRST_ROWS)), ("vmem", SMALL)],
         [PLANE, (3, *PLANE)],
-        places=1,
     )
     data = exchange(data)
-    conc_spec, trace = call(
-        aside_first_kernel,
-        "aside_first",
-        (source, cells, line_ahead, line_back),
-        [PLANE, CELL],
-        [PLANE],
-    )
     past, data = call(
         z_sweep_kernel,
         "z_sweep",
-        (data, cells, trace, back, ahead),
-        [(6, *CELL), wire(SWEEP_ROWS)],
-        [CELL, (6, *CELL)],
+        [("vmem", data), ("vmem", cells), ("vmem", edge), ("vmem", mean), back, ahead],
+        [("hbm", (6, *CELL)), ("vmem", wire(SWEEP_ROWS))],
+        [(6, *CELL), CELL, (6, *CELL)],
+        [()],
     )
     data = exchange(data)
     (data,) = call(
         plane_green_kernel,
         "plane_green",
-        (place, data, line_ahead, line_back),
-        [wire(SWEEP_ROWS)],
+        [place, ("vmem", data), line_ahead, line_back],
+        [("vmem", wire(SWEEP_ROWS))],
         [PLANE, (6, *PLANE)],
-        places=1,
     )
     data = exchange(data)
-    strain, data = call(
+    now, data = call(
         z_drive_kernel,
         "z_drive",
-        (data, cells, back, ahead),
-        [(6, *CELL), wire(DRIVE_ROWS)],
-        [CELL, CELL],
+        [("vmem", data), ("vmem", cells), back, ahead],
+        [("hbm", (6, *CELL)), ("vmem", wire(DRIVE_ROWS))],
+        [(6, *CELL), CELL, CELL],
+        [(6,)],
     )
     data = exchange(data)
-    strain, sums = call(aside_last_kernel, "aside_last", (strain, past), [(6, *BLOCK), (8, LANES)])
+    strain, conc_spec, sums = call(
+        aside_kernel,
+        "aside",
+        [("hbm", now), ("hbm", past), ("hbm", source), line_ahead, line_back],
+        [("hbm", (6, *BLOCK)), ("vmem", PLANE), ("vmem", (8, LANES))],
+        [(6, *CELL), (6, *CELL), wire(SOURCE_ROWS), (6, *LINES), PLANE],
+        [(6,), (6,), (), (6, HIGH)],
+    )
     (data,) = call(
         plane_update_kernel,
         "plane_update",
-        (place, data, conc_spec, sums, line_ahead, line_back),
-        [wire(LAST_ROWS)],
+        [place, ("vmem", data), ("vmem", conc_spec), ("vmem", sums), line_ahead, line_back],
+        [("vmem", wire(LAST_ROWS))],
         [PLANE],
-        places=1,
     )
     data = exchange(data)
     conc_next, norms = call(
-        z_last_kernel, "z_last", (data, back), [BLOCK, (8, LANES)], [CELL]
-    )
-    return conc_next, strain, norms[:2, 0]
+        z_last_kernel,
+        "z_last",
+        [("vmem", data), back],
+        [("hbm", BLOCK), ("smem", (2,))],
+        [CELL, LINES],
+        [(HIGH,)],
+    )
+    return conc_next, strain, norms
 
 
 def solution(mesh):

time: 250 us -> 239 us (0.956)
  blocking collectives: 109 us -> 179 us
  waiting for transfers between devices: 53.5 us -> 8.49 us
  local copies, waits for them, and re-layouts: 21 us -> 0.03 us
  starting transfers between devices: 21.7 us -> 5.36 us
    all_to_all x3 -> x5, blocking collectives: 109 us -> 179 us  [exchange(): rows = lax.all_to_all(rows, AXES, split_axis=0, concat_axis=0, tiled=True)]
    all_to_all x3 -> x1, waiting for transfers between devices: 53.5 us -> 8.49 us  [exchange(): rows = lax.all_to_all(rows, AXES, split_axis=0, concat_axis=0, tiled=True)]
    unnamed x48 -> x10, local copies, waits for them, and re-layouts: 20.4 us -> 0.03 us
    all_to_all x3 -> x1, starting transfers between devices: 21.7 us -> 5.36 us  [exchange(): rows = lax.all_to_all(rows, AXES, split_axis=0, concat_axis=0, tiled=True)]
    pallas_call x9 -> x8, Pallas kernels: 43.2 us -> 44.7 us  [call(): pl.pallas_call(kernel, out_shape=[pltpu.HBM(shape, F32) if space == 'hbm'...]
  transfers between devices with their start and end apart: 3 -> 1, of which waited for: 3 -> 1; matrix products, arithmetic and copies ran while one was open for 0% -> 0% of each run, Pallas kernels for 2% -> 2%
where the time goes in v3:
time: 239 us; the launch traced here: 238 us
  blocking collectives  179 us (75%)
  Pallas kernels  44.7 us (19%)
  waiting for transfers between devices  8.49 us (4%)
  starting transfers between devices  5.36 us (2%)
    all_to_all x5, blocking collectives, exchange(): rows = lax.all_to_all(rows, AXES, split_axis=0, concat_axis=0, tiled=True)  179 us
    pallas_call x8, Pallas kernels, call(): pl.pallas_call(kernel, out_shape=[pltpu.HBM(shape, F32) if space == 'hbm'...  44.7 us
    all_to_all x1, waiting for transfers between devices, exchange(): rows = lax.all_to_all(rows, AXES, split_axis=0, concat_axis=0, tiled=True)  8.49 us
    all_to_all x1, starting transfers between devices, exchange(): rows = lax.all_to_all(rows, AXES, split_axis=0, concat_axis=0, tiled=True)  5.36 us
  transfers between devices with their start and end apart: 1, of which 1 were waited for; matrix products, arithmetic and copies ran while one was open for 0% of the time, Pallas kernels for 2%

profile of v3, /device:TPU:1, one launch (start us, length us, event | category | flops | bytes accessed | tf_op | source)
XLA Modules:
  0.0 238.4 jit_solution(12874036309741380485)
XLA Ops:
  0.6 0.0 copy-start.1
  0.6 0.0 copy-start.2
  0.7 2.8 %source.1 = (f32[256,512]{1,0:T(8,128)S(1)}, f32[2176,128]{1,0:T(8,128)S(1)}, f32[8,512]{1,0:T(8,128)S(1)}) custom-call(s32[1]{0:T(128)} %bitcast.place_ref, f32[32,16,256]{2,1,0:T(8,128)} %conc_ref.1, bf16[3,256,256]{2,1,0:T(8,128)(2,1)} %constant.33.clone.far_ref.ahead_ref), custom_call_target="tpu_custom_call" | custom-call | tf_op jit(solution)/shard_map/source/pallas_call | solution.py:564
  3.5 30.8 %all_to_all.54 = f32[128,1,2176]{2,1,0:T(1,128)S(1)} all-to-all(f32[128,1,2176]{2,1,0:T(1,128)S(1)} %bitcast.24), channel_id=1, replica_groups=mesh['row_0'=4,'row_1'=2,'col_0'=4,'col_1'=4] {'row_0','row_1','col_0','..., dimensions={0} | all-to-all | bytes 2228224 | tf_op jit(solution)/shard_map/all_to_all | solution.py:584
  34.3 0.0 copy-done.1
  34.3 0.0 copy-done.2
  34.3 4.4 %plane_first.1 = (f32[5120,128]{1,0:T(8,128)S(1)}, f32[8,512]{1,0:T(8,128)S(1)}) custom-call(s32[1]{0:T(128)} %bitcast.place_ref, f32[2176,128]{1,0:T(8,128)S(1)} %bitcast.17, bf16[2,2,256,256]{3,2,1,0:T(8,128)(2,1)S(1)} %copy-done.1, bf16[2,2,256,256]{3,2,1,0:T(8,128)(2,1)S(1)} %copy-done.2), custom_call_target="tpu_custom_call" | custom-call | tf_op jit(solution)/shard_map/plane_first/pallas_call | solution.py:564
  38.7 0.0 copy-start.3
  38.7 0.0 copy-start.4
  38.7 39.0 %all_to_all.55 = f32[128,1,5120]{2,1,0:T(1,128)S(1)} all-to-all(f32[128,1,5120]{2,1,0:T(1,128)S(1)} %bitcast.20), channel_id=1, replica_groups=mesh['row_0'=4,'row_1'=2,'col_0'=4,'col_1'=4] {'row_0','row_1','col_0','..., dimensions={0} | all-to-all | bytes 5242880 | tf_op jit(solution)/shard_map/all_to_all | solution.py:584
  77.6 0.0 copy-done
  77.6 0.0 copy-done.3
  77.7 0.0 copy-done.4
  77.7 6.7 %z_sweep.1 = (f32[6,256,512]{2,1,0:T(8,128)}, f32[6144,128]{1,0:T(8,128)S(1)}) custom-call(f32[5120,128]{1,0:T(8,128)S(1)} %bitcast.16, f32[256,512]{1,0:T(8,128)S(1)} %get-tuple-element.19.cells_ref, f32[8,512]{1,0:T(8,128)S(1)} %get-tuple-element.20.edge_ref, f32[8,512]{1,0:T(8,128)S(1)} %get-tuple-element.21.mean_ref, bf16[2,256,256]{2,1,0:T(8,128)(2,1)S(1)} %copy-done.4, ...), custom_call_target="tpu_custom_call" | custom-call | tf_op jit(solution)/shard_map/z_sweep/pallas_call | solution.py:564
  84.4 45.4 %all_to_all.56 = f32[128,1,6144]{2,1,0:T(1,128)S(1)} all-to-all(f32[128,1,6144]{2,1,0:T(1,128)S(1)} %bitcast.19), channel_id=1, replica_groups=mesh['row_0'=4,'row_1'=2,'col_0'=4,'col_1'=4] {'row_0','row_1','col_0','..., dimensions={0} | all-to-all | bytes 6291456 | tf_op jit(solution)/shard_map/all_to_all | solution.py:584
  129.7 15.0 %plane_green.1 = f32[6144,128]{1,0:T(8,128)S(1)} custom-call(s32[1]{0:T(128)} %bitcast.place_ref, f32[6144,128]{1,0:T(8,128)S(1)} %bitcast.14, bf16[2,2,256,256]{3,2,1,0:T(8,128)(2,1)S(1)} %copy-done.1, bf16[2,2,256,256]{3,2,1,0:T(8,128)(2,1)S(1)} %copy-done.2), custom_call_target="tpu_custom_call" | custom-call | tf_op jit(solution)/shard_map/plane_green/pallas_call | solution.py:564
  144.7 45.4 %all_to_all.57 = f32[128,1,6144]{2,1,0:T(1,128)S(1)} all-to-all(f32[128,1,6144]{2,1,0:T(1,128)S(1)} %bitcast.15), channel_id=1, replica_groups=mesh['row_0'=4,'row_1'=2,'col_0'=4,'col_1'=4] {'row_0','row_1','col_0','..., dimensions={0} | all-to-all | bytes 6291456 | tf_op jit(solution)/shard_map/all_to_all | solution.py:584
  190.1 5.9 %z_drive.1 = (f32[6,256,512]{2,1,0:T(8,128)}, f32[1024,128]{1,0:T(8,128)}) custom-call(f32[6144,128]{1,0:T(8,128)S(1)} %bitcast.13, f32[256,512]{1,0:T(8,128)S(1)} %get-tuple-element.19.cells_ref, bf16[2,256,256]{2,1,0:T(8,128)(2,1)S(1)} %copy-done.4, bf16[3,256,256]{2,1,0:T(8,128)(2,1)S(1)} %copy-done.3), custom_call_target="tpu_custom_call" | custom-call | tf_op jit(solution)/shard_map/z_drive/pallas_call | solution.py:564
  196.0 5.4 %all-to-all-start.4 = ((f32[128,1,1024]{2,1,0:T(1,128)}), f32[128,1,1024]{2,1,0:T(1,128)S(1)}, u32[]{:S(2)}, u32[]{:S(2)}) async-start(f32[128,1,1024]{2,1,0:T(1,128)} %bitcast.9), calls=%async_computation.4 | async-start | bytes 1048576 | tf_op jit(solution)/shard_map/all_to_all | solution.py:584
  201.4 5.6 %aside.1 = (f32[6,32,16,256]{3,2,1,0:T(8,128)}, f32[2,256,256]{2,1,0:T(8,128)S(1)}, f32[8,128]{1,0:T(8,128)S(1)}) custom-call(f32[6,256,512]{2,1,0:T(8,128)} %get-tuple-element.24.now_ref, f32[6,256,512]{2,1,0:T(8,128)} %get-tuple-element.25.then_ref, f32[2176,128]{1,0:T(8,128)} %bitcast.18, bf16[2,2,256,256]{3,2,1,0:T(8,128)(2,1)S(1)} %copy-done.1, ...), custom_call_target="tpu_custom_call" | custom-call | tf_op jit(solution)/shard_map/aside/pallas_call | solution.py:564
  206.9 8.5 %all-to-all-done.4 = f32[128,1,1024]{2,1,0:T(1,128)S(1)} async-done(((f32[128,1,1024]{2,1,0:T(1,128)}), f32[128,1,1024]{2,1,0:T(1,128)S(1)}, u32[]{:S(2)}, u32[]{:S(2)}) %all-to-all-start.4) | async-done | bytes 524320 | tf_op jit(solution)/shard_map/all_to_all | solution.py:584
  215.4 2.3 plane_update.1
  217.7 18.5 %all_to_all.58 = f32[128,1,1152]{2,1,0:T(1,128)S(1)} all-to-all(f32[128,1,1152]{2,1,0:T(1,128)S(1)} %bitcast.22), channel_id=1, replica_groups=mesh['row_0'=4,'row_1'=2,'col_0'=4,'col_1'=4] {'row_0','row_1','col_0','..., dimensions={0} | all-to-all | bytes 1179648 | tf_op jit(solution)/shard_map/all_to_all | solution.py:584
  236.2 2.1 z_last.1
  (1 shorter events, 0.0 us)
Async XLA Ops:
  0.6 33.6 %copy-start.1 = (bf16[2,2,256,256]{3,2,1,0:T(8,128)(2,1)S(1)}, bf16[2,2,256,256]{3,2,1,0:T(8,128)(2,1)}, u32[]{:S(2)}) copy-start(bf16[2,2,256,256]{3,2,1,0:T(8,128)(2,1)} %constant.31.clone.ahead_ref) | copy-start | bytes 1572868
  0.6 33.6 %copy-start.2 = (bf16[2,2,256,256]{3,2,1,0:T(8,128)(2,1)S(1)}, bf16[2,2,256,256]{3,2,1,0:T(8,128)(2,1)}, u32[]{:S(2)}) copy-start(bf16[2,2,256,256]{3,2,1,0:T(8,128)(2,1)} %constant.32.clone.back_ref) | copy-start | bytes 1572868
  34.3 43.4 %copy-start = (f32[128,1,2176]{2,1,0:T(1,128)}, f32[128,1,2176]{2,1,0:T(1,128)S(1)}, u32[]{:S(2)}) copy-start(f32[128,1,2176]{2,1,0:T(1,128)S(1)} %all_to_all.54) | copy-start | bytes 3342340
  38.7 39.0 %copy-start.3 = (bf16[3,256,256]{2,1,0:T(8,128)(2,1)S(1)}, bf16[3,256,256]{2,1,0:T(8,128)(2,1)}, u32[]{:S(2)}) copy-start(bf16[3,256,256]{2,1,0:T(8,128)(2,1)} %constant.33.clone.far_ref.ahead_ref) | copy-start | bytes 1179652
  38.7 39.0 %copy-start.4 = (bf16[2,256,256]{2,1,0:T(8,128)(2,1)S(1)}, bf16[2,256,256]{2,1,0:T(8,128)(2,1)}, u32[]{:S(2)}) copy-start(bf16[2,256,256]{2,1,0:T(8,128)(2,1)} %constant.34.clone.back_ref) | copy-start | bytes 786436
  196.0 19.4 %all-to-all-start.4 = ((f32[128,1,1024]{2,1,0:T(1,128)}), f32[128,1,1024]{2,1,0:T(1,128)S(1)}, u32[]{:S(2)}, u32[]{:S(2)}) async-start(f32[128,1,1024]{2,1,0:T(1,128)} %bitcast.9), calls=%async_computation.4 | async-start | bytes 1048576 | tf_op jit(solution)/shard_map/all_to_all | solution.py:584

commit v4 on v3

--- a/solution.py
+++ b/solution.py
@@ -39,7 +39,9 @@
 F32 = jnp.float32
 BF16 = jnp.bfloat16
 INTERPRET = False
-UNROLL = 1
+PLANE_UNROLL = 6
+SWEEP_UNROLL = 3
+DRIVE_UNROLL = 6
 SOURCE_ROWS = 2 * LOW + 1
 FIRST_ROWS = 5 * LOW
 SWEEP_ROWS = 6 * LOW
@@ -72,11 +74,8 @@
             np.block([[np.cos(angle), np.sin(angle)], [-np.sin(angle), np.cos(angle)]])
         )
     line_ahead = np.stack([pieces_of(line, 2) for line in lines])
-    line_back = np.stack([pieces_of(line.T, 2) for line in lines])
     ahead = np.concatenate([cosine[:HALF], -sine[:HALF]], axis=0)
-    weight = np.where(half == 0, 1.0, 2.0) / float(N) ** 3
-    back = np.concatenate([cosine[:, :HALF] * weight, -sine[:, :HALF] * weight], axis=1)
-    return line_ahead, line_back, pieces_of(ahead, 3), pieces_of(back, 2)
+    return line_ahead, pieces_of(ahead, 3)
 
 
 def split(value, count):
@@ -214,6 +213,18 @@
                 out_ref[rows_of(i * COLS + h * 8 + j, f, pitch), :] = parts[j]
 
 
+def each(count, unroll, body):
+    def step(i, carry):
+        for slot in range(unroll):
+            body(i * unroll + slot, slot)
+        return carry
+
+    if count == unroll:
+        step(0, 0)
+    else:
+        lax.fori_loop(0, count // unroll, step, 0)
+
+
 def signed(index):
     return jnp.where(index < HALF, index, index - N).astype(F32) * UNIT
 
@@ -256,18 +267,25 @@
     place_ref,
     conc_ref,
     far_ref,
+    far_line_ref,
     cells_ref,
     out_ref,
     edge_ref,
+    back_ref,
+    ahead_ref,
+    line_ref,
+    line_back_ref,
     lines_ref,
-    ahead_ref,
     sems,
     far_sem,
+    line_sem,
 ):
     copies = copy_lines(conc_ref, lines_ref, sems, True)
     copies.append(pltpu.make_async_copy(far_ref, ahead_ref, far_sem))
+    line = pltpu.make_async_copy(far_line_ref, line_ref, line_sem)
     for copy in copies:
         copy.start()
+    line.start()
     for copy in copies:
         copy.wait()
     conc = lines_ref[...].reshape(CELLS, N).T
@@ -283,6 +301,14 @@
     out_ref[peers_of(2 * LOW, SOURCE_ROWS), :] = jnp.broadcast_to(total, (DEVICES, LANES))
     z_ahead(source, 0, SOURCE_ROWS, ahead_ref, out_ref)
     z_ahead(conc, 1, SOURCE_ROWS, ahead_ref, out_ref)
+    lane = lax.broadcasted_iota(jnp.int32, (N, N), 1)
+    weight = jnp.where(lane % HALF == 0, 1.0, 2.0) * (1.0 / float(N) ** 3)
+    for i in range(2):
+        back_ref[i] = (ahead_ref[i].astype(F32).T * weight).astype(BF16)
+    line.wait()
+    for b in range(2):
+        for i in range(2):
+            line_back_ref[b, i] = line_ref[b, i].astype(F32).T.astype(BF16)
 
 
 def plane_first_kernel(
@@ -290,7 +316,7 @@
 ):
     mean = jnp.sum(in_ref[peers_of(2 * LOW, SOURCE_ROWS), :]) * (1.0 / float(N) ** 3)
     mean_ref[...] = jnp.full((8, CELLS), mean, F32)
-    data = list(plane_spectrum(in_ref, 0, SOURCE_ROWS, ahead_ref, back_ref, plane_ref))
+    data = list(plane_spectrum(in_ref, 0, SOURCE_ROWS, ahead_ref, back_ref, plane_ref.at[5]))
     wave_y = []
     for b in range(2):
         wave_x, wave, wave_z = waves(place_ref, b, 0, N)
@@ -315,7 +341,7 @@
         if factor is not None:
             real = real * factor
             imag = imag * factor
-        x_back(real, imag, f, FIRST_ROWS, back_ref, plane_ref, out_ref)
+        x_back(real, imag, f, FIRST_ROWS, back_ref, plane_ref.at[f], out_ref)
 
 
 def z_sweep_kernel(
@@ -333,7 +359,8 @@
     sem,
 ):
     for f, component in enumerate(FIRST_FIELDS):
-        strain_ref[component] = z_back(in_ref, f, FIRST_ROWS, back_ref, spec_ref)
+        spec = spec_ref.at[f]
+        strain_ref[component] = z_back(in_ref, f, FIRST_ROWS, back_ref, spec)
 
     def block(b, carry):
         rows = pl.ds(pl.multiple_of(b * 8, 8), 8)
@@ -356,22 +383,20 @@
     past = pltpu.make_async_copy(strain_ref, past_ref, sem)
     past.start()
 
-    def ahead(f, carry):
+    def ahead(f, slot):
         z_ahead(tau_ref[f], f, SWEEP_ROWS, ahead_ref, out_ref)
-        return carry
-
-    lax.fori_loop(0, 6, ahead, 0, unroll=UNROLL)
+
+    each(6, SWEEP_UNROLL, ahead)
     past.wait()
 
 
 def plane_green_kernel(place_ref, in_ref, ahead_ref, back_ref, out_ref, plane_ref, spec_ref):
-    def ahead(f, carry):
+    def ahead(f, slot):
         spec_ref[f, 0], spec_ref[f, 1] = plane_spectrum(
-            in_ref, f, SWEEP_ROWS, ahead_ref, back_ref, plane_ref
+            in_ref, f, SWEEP_ROWS, ahead_ref, back_ref, plane_ref.at[slot]
         )
-        return carry
-
-    lax.fori_loop(0, 6, ahead, 0, unroll=UNROLL)
+
+    each(6, PLANE_UNROLL, ahead)
 
     def block(b, carry):
         start = pl.multiple_of(b * 8, 8)
@@ -402,12 +427,11 @@
 
     lax.fori_loop(0, N // 8, block, 0)
 
-    def back(f, carry):
+    def back(f, slot):
         real, imag = y_back(spec_ref[f, 0], spec_ref[f, 1], ahead_ref)
-        x_back(real, imag, f, SWEEP_ROWS, back_ref, plane_ref, out_ref)
-        return carry
-
-    lax.fori_loop(0, 6, back, 0, unroll=UNROLL)
+        x_back(real, imag, f, SWEEP_ROWS, back_ref, plane_ref.at[slot], out_ref)
+
+    each(6, PLANE_UNROLL, back)
 
 
 def z_drive_kernel(
@@ -425,12 +449,11 @@
     def far(f):
         return pltpu.make_async_copy(strain_ref.at[f], far_ref.at[f], sems.at[f])
 
-    def inverse(f, carry):
-        strain_ref[f] = z_back(in_ref, f, SWEEP_ROWS, back_ref, spec_ref)
+    def inverse(f, slot):
+        strain_ref[f] = z_back(in_ref, f, SWEEP_ROWS, back_ref, spec_ref.at[slot])
         far(f).start()
-        return carry
-
-    lax.fori_loop(0, 6, inverse, 0, unroll=UNROLL)
+
+    each(6, DRIVE_UNROLL, inverse)
 
     def block(b, carry):
         rows = pl.ds(pl.multiple_of(b * 8, 8), 8)
@@ -564,11 +587,11 @@
     return pl.pallas_call(
         kernel,
         out_shape=[
-            pltpu.HBM(shape, F32) if space == "hbm" else jax.ShapeDtypeStruct(shape, F32)
-            for space, shape in outs
+            pltpu.HBM(shape, F32) if space == "hbm" else jax.ShapeDtypeStruct(shape, *kind or (F32,))
+            for space, shape, *kind in outs
         ],
         in_specs=[pl.BlockSpec(memory_space=SPACES[space]) for space, _ in args],
-        out_specs=[pl.BlockSpec(memory_space=SPACES[space]) for space, _ in outs],
+        out_specs=[pl.BlockSpec(memory_space=SPACES[space]) for space, *_ in outs],
         scratch_shapes=[
             *[pltpu.VMEM(s, F32) if isinstance(s, tuple) else s for s in scratch],
             *[pltpu.SemaphoreType.DMA(shape) for shape in sems],
@@ -598,24 +621,32 @@
 
 def shards(concentration):
     tables = [jnp.asarray(table) for table in build_tables()]
-    line_ahead, line_back, ahead, back = [("vmem", table) for table in tables]
     place = ("smem", lax.axis_index(AXES).astype(jnp.int32)[None])
 
-    cells, data, edge = call(
+    cells, data, edge, *tables = call(
         source_kernel,
         "source",
-        [place, ("hbm", concentration), ("hbm", tables[2])],
-        [("vmem", CELL), ("vmem", wire(SOURCE_ROWS)), ("vmem", SMALL)],
-        [LINES, pltpu.VMEM((3, N, N), BF16)],
-        [(HIGH,), ()],
-    )
+        [place, ("hbm", concentration), ("hbm", tables[1]), ("hbm", tables[0])],
+        [
+            ("vmem", CELL),
+            ("vmem", wire(SOURCE_ROWS)),
+            ("vmem", SMALL),
+            ("vmem", (2, N, N), BF16),
+            ("vmem", (3, N, N), BF16),
+            ("vmem", (2, 2, N, N), BF16),
+            ("vmem", (2, 2, N, N), BF16),
+        ],
+        [LINES],
+        [(HIGH,), (), ()],
+    )
+    back, ahead, line_ahead, line_back = [("vmem", table) for table in tables]
     source = exchange(data)
     data, mean = call(
         plane_first_kernel,
         "plane_first",
         [place, ("vmem", source), line_ahead, line_back],
         [("vmem", wire(FIRST_ROWS)), ("vmem", SMALL)],
-        [PLANE, (3, *PLANE)],
+        [(6, *PLANE), (3, *PLANE)],
     )
     data = exchange(data)
     past, data = call(
@@ -623,7 +654,7 @@
         "z_sweep",
         [("vmem", data), ("vmem", cells), ("vmem", edge), ("vmem", mean), back, ahead],
         [("hbm", (6, *CELL)), ("vmem", wire(SWEEP_ROWS))],
-        [(6, *CELL), CELL, (6, *CELL)],
+        [(6, *CELL), (5, *CELL), (6, *CELL)],
         [()],
     )
     data = exchange(data)
@@ -632,7 +663,7 @@
         "plane_green",
         [place, ("vmem", data), line_ahead, line_back],
         [("vmem", wire(SWEEP_ROWS))],
-        [PLANE, (6, *PLANE)],
+        [(PLANE_UNROLL, *PLANE), (6, *PLANE)],
     )
     data = exchange(data)
     now, data = call(
@@ -640,7 +671,7 @@
         "z_drive",
         [("vmem", data), ("vmem", cells), back, ahead],
         [("hbm", (6, *CELL)), ("vmem", wire(DRIVE_ROWS))],
-        [(6, *CELL), CELL, CELL],
+        [(6, *CELL), (DRIVE_UNROLL, *CELL), CELL],
         [(6,)],
     )
     data = exchange(data)

time: 239 us -> 231 us (0.967)
  Pallas kernels: 44.7 us -> 36.8 us
    pallas_call x8, Pallas kernels: 44.7 us -> 36.8 us  [call(): pl.pallas_call(kernel, out_shape=[pltpu.HBM(shape, F32) if space == 'hbm'...]
where the time goes in v4:
time: 231 us; the launch traced here: 230 us
  blocking collectives  179 us (77%)
  Pallas kernels  36.8 us (16%)
  waiting for transfers between devices  8.49 us (4%)
  starting transfers between devices  5.36 us (2%)
    all_to_all x5, blocking collectives, exchange(): rows = lax.all_to_all(rows, AXES, split_axis=0, concat_axis=0, tiled=True)  179 us
    pallas_call x8, Pallas kernels, call(): pl.pallas_call(kernel, out_shape=[pltpu.HBM(shape, F32) if space == 'hbm'...  36.8 us
    all_to_all x1, waiting for transfers between devices, exchange(): rows = lax.all_to_all(rows, AXES, split_axis=0, concat_axis=0, tiled=True)  8.49 us
    all_to_all x1, starting transfers between devices, exchange(): rows = lax.all_to_all(rows, AXES, split_axis=0, concat_axis=0, tiled=True)  5.36 us
  transfers between devices with their start and end apart: 1, of which 1 were waited for; matrix products, arithmetic and copies ran while one was open for 0% of the time, Pallas kernels for 2%

profile of v4, /device:TPU:1, one launch (start us, length us, event | category | flops | bytes accessed | tf_op | source)
XLA Modules:
  0.0 230.4 jit_solution(2490499466988832946)
XLA Ops:
  0.6 3.0 %source.1 = (f32[256,512]{1,0:T(8,128)S(1)}, f32[2176,128]{1,0:T(8,128)S(1)}, f32[8,512]{1,0:T(8,128)S(1)}, bf16[2,256,256]{2,1,0:T(8,128)(2,1)S(1)}, bf16[3,256...) custom-call(s32[1]{0:T(128)} %bitcast.place_ref, ...), custom_call_target="tpu_custom_call" | custom-call | tf_op jit(solution)/shard_map/source/pallas_call | solution.py:587
  3.7 30.8 %all_to_all.54 = f32[128,1,2176]{2,1,0:T(1,128)S(1)} all-to-all(f32[128,1,2176]{2,1,0:T(1,128)S(1)} %bitcast.24), channel_id=1, replica_groups=mesh['row_0'=4,'row_1'=2,'col_0'=4,'col_1'=4] {'row_0','row_1','col_0','..., dimensions={0} | all-to-all | bytes 2228224 | tf_op jit(solution)/shard_map/all_to_all | solution.py:607
  34.5 0.0 copy-start
  34.5 4.4 %plane_first.1 = (f32[5120,128]{1,0:T(8,128)S(1)}, f32[8,512]{1,0:T(8,128)S(1)}) custom-call(s32[1]{0:T(128)} %bitcast.place_ref, f32[2176,128]{1,0:T(8,128)S(1)} %bitcast.17, bf16[2,2,256,256]{3,2,1,0:T(8,128)(2,1)S(1)} %get-tuple-element.22.ahead_ref, bf16[2,2,256,256]{3,2,1,0:T(8,128)(2,1)S(1)} %get-tuple-element.23.back_ref), custom_call_target="tpu_custom_call" | custom-call | tf_op jit(solution)/shard_map/plane_first/pallas_call | solution.py:587
  38.9 38.8 %all_to_all.55 = f32[128,1,5120]{2,1,0:T(1,128)S(1)} all-to-all(f32[128,1,5120]{2,1,0:T(1,128)S(1)} %bitcast.20), channel_id=1, replica_groups=mesh['row_0'=4,'row_1'=2,'col_0'=4,'col_1'=4] {'row_0','row_1','col_0','..., dimensions={0} | all-to-all | bytes 5242880 | tf_op jit(solution)/shard_map/all_to_all | solution.py:607
  77.7 0.0 copy-done
  77.7 5.7 %z_sweep.1 = (f32[6,256,512]{2,1,0:T(8,128)}, f32[6144,128]{1,0:T(8,128)S(1)}) custom-call(f32[5120,128]{1,0:T(8,128)S(1)} %bitcast.16, f32[256,512]{1,0:T(8,128)S(1)} %get-tuple-element.25.cells_ref, f32[8,512]{1,0:T(8,128)S(1)} %get-tuple-element.26.edge_ref, f32[8,512]{1,0:T(8,128)S(1)} %get-tuple-element.27.mean_ref, ...), custom_call_target="tpu_custom_call" | custom-call | tf_op jit(solution)/shard_map/z_sweep/pallas_call | solution.py:587
  83.4 45.4 %all_to_all.56 = f32[128,1,6144]{2,1,0:T(1,128)S(1)} all-to-all(f32[128,1,6144]{2,1,0:T(1,128)S(1)} %bitcast.19), channel_id=1, replica_groups=mesh['row_0'=4,'row_1'=2,'col_0'=4,'col_1'=4] {'row_0','row_1','col_0','..., dimensions={0} | all-to-all | bytes 6291456 | tf_op jit(solution)/shard_map/all_to_all | solution.py:607
  128.7 9.4 %plane_green.1 = f32[6144,128]{1,0:T(8,128)S(1)} custom-call(s32[1]{0:T(128)} %bitcast.place_ref, f32[6144,128]{1,0:T(8,128)S(1)} %bitcast.14, bf16[2,2,256,256]{3,2,1,0:T(8,128)(2,1)S(1)} %get-tuple-element.22.ahead_ref, bf16[2,2,256,256]{3,2,1,0:T(8,128)(2,1)S(1)} %get-tuple-element.23.back_ref), custom_call_target="tpu_custom_call" | custom-call | tf_op jit(solution)/shard_map/plane_green/pallas_call | solution.py:587
  138.2 45.4 %all_to_all.57 = f32[128,1,6144]{2,1,0:T(1,128)S(1)} all-to-all(f32[128,1,6144]{2,1,0:T(1,128)S(1)} %bitcast.15), channel_id=1, replica_groups=mesh['row_0'=4,'row_1'=2,'col_0'=4,'col_1'=4] {'row_0','row_1','col_0','..., dimensions={0} | all-to-all | bytes 6291456 | tf_op jit(solution)/shard_map/all_to_all | solution.py:607
  183.5 4.4 %z_drive.1 = (f32[6,256,512]{2,1,0:T(8,128)}, f32[1024,128]{1,0:T(8,128)}) custom-call(f32[6144,128]{1,0:T(8,128)S(1)} %bitcast.13, f32[256,512]{1,0:T(8,128)S(1)} %get-tuple-element.25.cells_ref, bf16[2,256,256]{2,1,0:T(8,128)(2,1)S(1)} %get-tuple-element.28.back_ref, bf16[3,256,256]{2,1,0:T(8,128)(2,1)S(1)} %get-tuple-element.29.ahead_ref), custom_call_target="tpu_custom_call" | custom-call | tf_op jit(solution)/shard_map/z_drive/pallas_call | solution.py:587
  187.9 5.4 %all-to-all-start.4 = ((f32[128,1,1024]{2,1,0:T(1,128)}), f32[128,1,1024]{2,1,0:T(1,128)S(1)}, u32[]{:S(2)}, u32[]{:S(2)}) async-start(f32[128,1,1024]{2,1,0:T(1,128)} %bitcast.9), calls=%async_computation.4 | async-start | bytes 1048576 | tf_op jit(solution)/shard_map/all_to_all | solution.py:607
  193.3 5.5 %aside.1 = (f32[6,32,16,256]{3,2,1,0:T(8,128)}, f32[2,256,256]{2,1,0:T(8,128)S(1)}, f32[8,128]{1,0:T(8,128)S(1)}) custom-call(f32[6,256,512]{2,1,0:T(8,128)} %get-tuple-element.32.now_ref, f32[6,256,512]{2,1,0:T(8,128)} %get-tuple-element.33.then_ref, f32[2176,128]{1,0:T(8,128)} %bitcast.18, bf16[2,2,256,256]{3,2,1,0:T(8,128)(2,1)S(1)} %get-tuple-element.22.ahead_ref, ...), custom_call_target="tpu_custom_call" | custom-call | tf_op jit(solution)/shard_map/aside/pallas_call | solution.py:587
  198.9 8.5 %all-to-all-done.4 = f32[128,1,1024]{2,1,0:T(1,128)S(1)} async-done(((f32[128,1,1024]{2,1,0:T(1,128)}), f32[128,1,1024]{2,1,0:T(1,128)S(1)}, u32[]{:S(2)}, u32[]{:S(2)}) %all-to-all-start.4) | async-done | bytes 524320 | tf_op jit(solution)/shard_map/all_to_all | solution.py:607
  207.4 2.3 %plane_update.1 = f32[1152,128]{1,0:T(8,128)S(1)} custom-call(s32[1]{0:T(128)} %bitcast.place_ref, f32[1024,128]{1,0:T(8,128)S(1)} %bitcast.23, f32[2,256,256]{2,1,0:T(8,128)S(1)} %get-tuple-element.34.conc_ref, f32[8,128]{1,0:T(8,128)S(1)} %get-tuple-element.35.sums_ref, bf16[2,2,256,256]{3,2,1,0:T(8,128)(2,1)S(1)} %get-tuple-element.22.ahead_ref, ...), custom_call_target="tpu_custom_call" | custom-call | tf_op jit(solution)/shard_map/plane_update/pallas_call | solution.py:587
  209.7 18.5 %all_to_all.58 = f32[128,1,1152]{2,1,0:T(1,128)S(1)} all-to-all(f32[128,1,1152]{2,1,0:T(1,128)S(1)} %bitcast.22), channel_id=1, replica_groups=mesh['row_0'=4,'row_1'=2,'col_0'=4,'col_1'=4] {'row_0','row_1','col_0','..., dimensions={0} | all-to-all | bytes 1179648 | tf_op jit(solution)/shard_map/all_to_all | solution.py:607
  228.2 2.1 z_last.1
Async XLA Ops:
  34.5 43.2 %copy-start = (f32[128,1,2176]{2,1,0:T(1,128)}, f32[128,1,2176]{2,1,0:T(1,128)S(1)}, u32[]{:S(2)}) copy-start(f32[128,1,2176]{2,1,0:T(1,128)S(1)} %all_to_all.54) | copy-start | bytes 3342340
  187.9 19.4 %all-to-all-start.4 = ((f32[128,1,1024]{2,1,0:T(1,128)}), f32[128,1,1024]{2,1,0:T(1,128)S(1)}, u32[]{:S(2)}, u32[]{:S(2)}) async-start(f32[128,1,1024]{2,1,0:T(1,128)} %bitcast.9), calls=%async_computation.4 | async-start | bytes 1048576 | tf_op jit(solution)/shard_map/all_to_all | solution.py:607

commit v5 on v4

--- a/solution.py
+++ b/solution.py
@@ -42,6 +42,7 @@
 PLANE_UNROLL = 6
 SWEEP_UNROLL = 3
 DRIVE_UNROLL = 6
+BLOCK_UNROLL = 2
 SOURCE_ROWS = 2 * LOW + 1
 FIRST_ROWS = 5 * LOW
 SWEEP_ROWS = 6 * LOW
@@ -123,8 +124,8 @@
     return pl.ds(row, DEVICES, stride=pitch)
 
 
-def z_ahead(value, f, pitch, ahead_ref, out_ref):
-    spectrum = product(table(ahead_ref), split(value, 3))
+def z_ahead(value, f, pitch, pieces, ahead_ref, out_ref):
+    spectrum = product(table(ahead_ref), split(value, pieces))
     for t in range(LOW // 2):
         lanes = slice(t * LANES, (t + 1) * LANES)
         parts = swap_lanes([spectrum[:HALF, lanes], spectrum[HALF:, lanes]], LANES // 2)
@@ -229,17 +230,21 @@
     return jnp.where(index < HALF, index, index - N).astype(F32) * UNIT
 
 
-def row_waves(start, count, lanes):
-    row = lax.broadcasted_iota(jnp.int32, (count, lanes), 0) + start
+def row_waves(start, count):
+    row = lax.broadcasted_iota(jnp.int32, (count, LANES), 0) + start
     return signed(2 * (row % HALF) + row // HALF)
 
 
-def waves(place_ref, branch, start, count):
-    shape = (count, N)
-    lane = lax.broadcasted_iota(jnp.int32, shape, 1)
-    wave_y = signed(2 * (lane % HALF) + branch)
-    wave_z = jnp.full(shape, place_ref[0], jnp.int32).astype(F32) * UNIT
-    return row_waves(start, count, N), wave_y, wave_z
+def lane_waves(branch, count):
+    return signed(2 * lax.broadcasted_iota(jnp.int32, (count, LANES), 1) + branch)
+
+
+def depth_wave(place_ref, count):
+    return jnp.full((count, LANES), place_ref[0], jnp.int32).astype(F32) * UNIT
+
+
+def twice(half):
+    return jnp.concatenate([half, half], axis=1)
 
 
 def squares(total):
@@ -249,9 +254,9 @@
 
 
 def source_of(conc):
-    first = FIRST_LOW + FIRST_RISE * conc
-    shear = SHEAR_LOW + SHEAR_RISE * conc
-    return -(3.0 * first + 2.0 * shear) * EIGEN_STRAIN * conc
+    rise = -EIGEN_STRAIN * (3.0 * FIRST_RISE + 2.0 * SHEAR_RISE)
+    low = -EIGEN_STRAIN * (3.0 * FIRST_LOW + 2.0 * SHEAR_LOW)
+    return (low + rise * conc) * conc
 
 
 def copy_lines(far, lines_ref, sems, inward):
@@ -299,8 +304,8 @@
     total = sum(total[:, t * LANES : (t + 1) * LANES] for t in range(CELLS // LANES))
     total = jnp.sum(total, axis=0, keepdims=True)
     out_ref[peers_of(2 * LOW, SOURCE_ROWS), :] = jnp.broadcast_to(total, (DEVICES, LANES))
-    z_ahead(source, 0, SOURCE_ROWS, ahead_ref, out_ref)
-    z_ahead(conc, 1, SOURCE_ROWS, ahead_ref, out_ref)
+    z_ahead(source, 0, SOURCE_ROWS, 3, ahead_ref, out_ref)
+    z_ahead(conc, 1, SOURCE_ROWS, 2, ahead_ref, out_ref)
     lane = lax.broadcasted_iota(jnp.int32, (N, N), 1)
     weight = jnp.where(lane % HALF == 0, 1.0, 2.0) * (1.0 / float(N) ** 3)
     for i in range(2):
@@ -317,20 +322,21 @@
     mean = jnp.sum(in_ref[peers_of(2 * LOW, SOURCE_ROWS), :]) * (1.0 / float(N) ** 3)
     mean_ref[...] = jnp.full((8, CELLS), mean, F32)
     data = list(plane_spectrum(in_ref, 0, SOURCE_ROWS, ahead_ref, back_ref, plane_ref.at[5]))
+    wave_x = row_waves(0, N)
+    wave_z = depth_wave(place_ref, N)
     wave_y = []
+    partial = wave_x * wave_x + wave_z * wave_z
     for b in range(2):
-        wave_x, wave, wave_z = waves(place_ref, b, 0, N)
-        wave_y.append(wave)
-        square = wave_x * wave_x + wave * wave + wave_z * wave_z
+        wave = lane_waves(b, N)
+        wave_y.append(twice(wave))
+        square = partial + wave * wave
         nonzero = square > 0.0
         safe = jnp.where(nonzero, square, 1.0)
-        data[b] = data[b] * jnp.where(nonzero, TRACE / safe, 0.0)
+        data[b] = data[b] * twice(jnp.where(nonzero, TRACE / safe, 0.0))
     for power in range(3):
         if power:
             data = [data[b] * wave_y[b] for b in range(2)]
         line_ref[power, 0], line_ref[power, 1] = y_back(data[0], data[1], ahead_ref)
-    wave_x = row_waves(0, N, N)
-    wave_z = jnp.full((N, N), place_ref[0], jnp.int32).astype(F32) * UNIT
     plan = ((2, 0, 0), (0, 2, 0), (0, 1, 1), (1, 0, 1), (1, 1, 0))
     for f, (power_x, power_y, power_z) in enumerate(plan):
         real = line_ref[power_y, 0]
@@ -339,8 +345,8 @@
         for wave in [wave_x] * power_x + [wave_z] * power_z:
             factor = wave if factor is None else factor * wave
         if factor is not None:
-            real = real * factor
-            imag = imag * factor
+            real = real * twice(factor)
+            imag = imag * twice(factor)
         x_back(real, imag, f, FIRST_ROWS, back_ref, plane_ref.at[f], out_ref)
 
 
@@ -362,29 +368,26 @@
         spec = spec_ref.at[f]
         strain_ref[component] = z_back(in_ref, f, FIRST_ROWS, back_ref, spec)
 
-    def block(b, carry):
+    def block(b, slot):
         rows = pl.ds(pl.multiple_of(b * 8, 8), 8)
         conc = cells_ref[rows, :]
-        source = source_of(conc)
-        trace = TRACE * (source - edge_ref[...] - mean_ref[...])
+        source = source_of(conc) - mean_ref[...]
+        trace = TRACE * (source - edge_ref[...])
         strain = [strain_ref[f, rows, :] for f in range(6) if f != 2]
         strain.insert(2, trace - strain[0] - strain[1])
         strain_ref[2, rows, :] = strain[2]
-        first = FIRST_LOW + FIRST_RISE * conc
-        shear = SHEAR_LOW + SHEAR_RISE * conc
-        normal = (first - FIRST_REF) * trace + source
-        excess = 2.0 * (shear - SHEAR_REF)
+        normal = ((FIRST_LOW - FIRST_REF) + FIRST_RISE * conc) * trace + source
+        excess = 2.0 * (SHEAR_LOW - SHEAR_REF) + 2.0 * SHEAR_RISE * conc
         for f in range(6):
             tau = excess * strain[f]
             tau_ref[f, rows, :] = tau + normal if f < 3 else tau
-        return carry
-
-    lax.fori_loop(0, N // 8, block, 0)
+
+    each(N // 8, BLOCK_UNROLL, block)
     past = pltpu.make_async_copy(strain_ref, past_ref, sem)
     past.start()
 
     def ahead(f, slot):
-        z_ahead(tau_ref[f], f, SWEEP_ROWS, ahead_ref, out_ref)
+        z_ahead(tau_ref[f], f, SWEEP_ROWS, 2, ahead_ref, out_ref)
 
     each(6, SWEEP_UNROLL, ahead)
     past.wait()
@@ -398,34 +401,39 @@
 
     each(6, PLANE_UNROLL, ahead)
 
-    def block(b, carry):
+    waves_y = [lane_waves(branch, 8) for branch in range(2)]
+    wave_z = depth_wave(place_ref, 8)
+
+    def block(b, slot):
         start = pl.multiple_of(b * 8, 8)
         rows = pl.ds(start, 8)
+        wave_x = row_waves(start, 8)
+        partial = wave_x * wave_x + wave_z * wave_z
         for branch in range(2):
-            wave_x, wave_y, wave_z = waves(place_ref, branch, start, 8)
-            square = wave_x * wave_x + wave_y * wave_y + wave_z * wave_z
+            wave_y = waves_y[branch]
+            square = partial + wave_y * wave_y
             nonzero = square > 0.0
-            safe = jnp.where(nonzero, square, 1.0)
-            inverse = 1.0 / safe
-            scale = jnp.where(nonzero, inverse * (1.0 / SHEAR_REF), 0.0)
+            inverse = 1.0 / jnp.where(nonzero, square, 1.0)
+            scale = jnp.where(nonzero, inverse * (0.5 / SHEAR_REF), 0.0)
             inverse = inverse * BETA_REF
-            tau = [spec_ref[f, branch, rows, :] for f in range(6)]
-            force_x = tau[0] * wave_x + tau[5] * wave_y + tau[4] * wave_z
-            force_y = tau[5] * wave_x + tau[1] * wave_y + tau[3] * wave_z
-            force_z = tau[4] * wave_x + tau[3] * wave_y + tau[2] * wave_z
-            along = (wave_x * force_x + wave_y * force_y + wave_z * force_z) * inverse
-            moved_x = scale * (along * wave_x - force_x)
-            moved_y = scale * (along * wave_y - force_y)
-            moved_z = scale * (along * wave_z - force_z)
-            spec_ref[0, branch, rows, :] = wave_x * moved_x
-            spec_ref[1, branch, rows, :] = wave_y * moved_y
-            spec_ref[2, branch, rows, :] = wave_z * moved_z
-            spec_ref[3, branch, rows, :] = 0.5 * (wave_y * moved_z + wave_z * moved_y)
-            spec_ref[4, branch, rows, :] = 0.5 * (wave_x * moved_z + wave_z * moved_x)
-            spec_ref[5, branch, rows, :] = 0.5 * (wave_x * moved_y + wave_y * moved_x)
-        return carry
-
-    lax.fori_loop(0, N // 8, block, 0)
+            for h in range(2):
+                lanes = slice(h * LANES, (h + 1) * LANES)
+                tau = [spec_ref[f, branch, rows, lanes] for f in range(6)]
+                force_x = tau[0] * wave_x + tau[5] * wave_y + tau[4] * wave_z
+                force_y = tau[5] * wave_x + tau[1] * wave_y + tau[3] * wave_z
+                force_z = tau[4] * wave_x + tau[3] * wave_y + tau[2] * wave_z
+                along = (wave_x * force_x + wave_y * force_y + wave_z * force_z) * inverse
+                moved_x = scale * (along * wave_x - force_x)
+                moved_y = scale * (along * wave_y - force_y)
+                moved_z = scale * (along * wave_z - force_z)
+                spec_ref[0, branch, rows, lanes] = (wave_x + wave_x) * moved_x
+                spec_ref[1, branch, rows, lanes] = (wave_y + wave_y) * moved_y
+                spec_ref[2, branch, rows, lanes] = (wave_z + wave_z) * moved_z
+                spec_ref[3, branch, rows, lanes] = wave_y * moved_z + wave_z * moved_y
+                spec_ref[4, branch, rows, lanes] = wave_x * moved_z + wave_z * moved_x
+                spec_ref[5, branch, rows, lanes] = wave_x * moved_y + wave_y * moved_x
+
+    each(N // 8, BLOCK_UNROLL, block)
 
     def back(f, slot):
         real, imag = y_back(spec_ref[f, 0], spec_ref[f, 1], ahead_ref)
@@ -455,12 +463,13 @@
 
     each(6, DRIVE_UNROLL, inverse)
 
-    def block(b, carry):
+    rise = -EIGEN_STRAIN * (3.0 * FIRST_RISE + 2.0 * SHEAR_RISE)
+    low = -EIGEN_STRAIN * (3.0 * FIRST_LOW + 2.0 * SHEAR_LOW)
+
+    def block(b, slot):
         rows = pl.ds(pl.multiple_of(b * 8, 8), 8)
         conc = cells_ref[rows, :]
         strain = [strain_ref[f, rows, :] for f in range(6)]
-        first = FIRST_LOW + FIRST_RISE * conc
-        shear = SHEAR_LOW + SHEAR_RISE * conc
         dilation = EIGEN_STRAIN * conc
         part = [strain[f] - dilation for f in range(3)]
         trace = part[0] + part[1] + part[2]
@@ -475,12 +484,11 @@
             chemical
             + 0.5 * FIRST_RISE * trace * trace
             + SHEAR_RISE * energy
-            - EIGEN_STRAIN * (3.0 * first + 2.0 * shear) * trace
+            + (low + rise * conc) * trace
         )
-        return carry
-
-    lax.fori_loop(0, N // 8, block, 0)
-    z_ahead(drive_ref[...], 0, DRIVE_ROWS, ahead_ref, out_ref)
+
+    each(N // 8, BLOCK_UNROLL, block)
+    z_ahead(drive_ref[...], 0, DRIVE_ROWS, 2, ahead_ref, out_ref)
     for f in range(6):
         far(f).wait()
 
@@ -548,11 +556,15 @@
     place_ref, in_ref, conc_ref, sums_ref, ahead_ref, back_ref, out_ref, plane_ref
 ):
     data = list(plane_spectrum(in_ref, 0, DRIVE_ROWS, ahead_ref, back_ref, plane_ref))
+    wave_x = row_waves(0, N)
+    wave_z = depth_wave(place_ref, N)
+    partial = wave_x * wave_x + wave_z * wave_z
     for b in range(2):
-        wave_x, wave_y, wave_z = waves(place_ref, b, 0, N)
-        square = wave_x * wave_x + wave_y * wave_y + wave_z * wave_z
-        denominator = 1.0 + TIME_STEP * GRADIENT_ENERGY * square * square
-        data[b] = (conc_ref[b] - TIME_STEP * square * data[b]) / denominator
+        wave_y = lane_waves(b, N)
+        square = partial + wave_y * wave_y
+        inverse = 1.0 / (1.0 + TIME_STEP * GRADIENT_ENERGY * square * square)
+        drive = TIME_STEP * square * inverse
+        data[b] = conc_ref[b] * twice(inverse) - data[b] * twice(drive)
     real, imag = y_back(data[0], data[1], ahead_ref)
     x_back(real, imag, 0, LAST_ROWS, back_ref, plane_ref, out_ref)
     out_ref[peers_of(LOW, LAST_ROWS), :] = jnp.broadcast_to(sums_ref[:1, :], (DEVICES, LANES))

time: 231 us -> 228 us (0.987)
  Pallas kernels: 36.8 us -> 34.2 us
    pallas_call x8, Pallas kernels: 36.8 us -> 34.2 us  [call(): pl.pallas_call(kernel, out_shape=[pltpu.HBM(shape, F32) if space == 'hbm'...]
where the time goes in v5:
time: 228 us
  blocking collectives  179 us (79%)
  Pallas kernels  34.2 us (15%)
  waiting for transfers between devices  8.49 us (4%)
  starting transfers between devices  5.36 us (2%)
    all_to_all x5, blocking collectives, exchange(): rows = lax.all_to_all(rows, AXES, split_axis=0, concat_axis=0, tiled=True)  179 us
    pallas_call x8, Pallas kernels, call(): pl.pallas_call(kernel, out_shape=[pltpu.HBM(shape, F32) if space == 'hbm'...  34.2 us
    all_to_all x1, waiting for transfers between devices, exchange(): rows = lax.all_to_all(rows, AXES, split_axis=0, concat_axis=0, tiled=True)  8.49 us
    all_to_all x1, starting transfers between devices, exchange(): rows = lax.all_to_all(rows, AXES, split_axis=0, concat_axis=0, tiled=True)  5.36 us
  transfers between devices with their start and end apart: 1, of which 1 were waited for; matrix products, arithmetic and copies ran while one was open for 0% of the time, Pallas kernels for 2%

profile of v5, /device:TPU:1, one launch (start us, length us, event | category | flops | bytes accessed | tf_op | source)
XLA Modules:
  0.0 227.8 jit_solution(14968517923832981611)
XLA Ops:
  0.6 2.7 %source.1 = (f32[256,512]{1,0:T(8,128)S(1)}, f32[2176,128]{1,0:T(8,128)S(1)}, f32[8,512]{1,0:T(8,128)S(1)}, bf16[2,256,256]{2,1,0:T(8,128)(2,1)S(1)}, bf16[3,256...) custom-call(s32[1]{0:T(128)} %bitcast.place_ref, ...), custom_call_target="tpu_custom_call" | custom-call | tf_op jit(solution)/shard_map/source/pallas_call | solution.py:599
  3.4 30.8 %all_to_all.54 = f32[128,1,2176]{2,1,0:T(1,128)S(1)} all-to-all(f32[128,1,2176]{2,1,0:T(1,128)S(1)} %bitcast.24), channel_id=1, replica_groups=mesh['row_0'=4,'row_1'=2,'col_0'=4,'col_1'=4] {'row_0','row_1','col_0','..., dimensions={0} | all-to-all | bytes 2228224 | tf_op jit(solution)/shard_map/all_to_all | solution.py:619
  34.2 0.0 copy-start
  34.2 4.3 %plane_first.1 = (f32[5120,128]{1,0:T(8,128)S(1)}, f32[8,512]{1,0:T(8,128)S(1)}) custom-call(s32[1]{0:T(128)} %bitcast.place_ref, f32[2176,128]{1,0:T(8,128)S(1)} %bitcast.17, bf16[2,2,256,256]{3,2,1,0:T(8,128)(2,1)S(1)} %get-tuple-element.22.ahead_ref, bf16[2,2,256,256]{3,2,1,0:T(8,128)(2,1)S(1)} %get-tuple-element.23.back_ref), custom_call_target="tpu_custom_call" | custom-call | tf_op jit(solution)/shard_map/plane_first/pallas_call | solution.py:599
  38.5 38.8 %all_to_all.55 = f32[128,1,5120]{2,1,0:T(1,128)S(1)} all-to-all(f32[128,1,5120]{2,1,0:T(1,128)S(1)} %bitcast.20), channel_id=1, replica_groups=mesh['row_0'=4,'row_1'=2,'col_0'=4,'col_1'=4] {'row_0','row_1','col_0','..., dimensions={0} | all-to-all | bytes 5242880 | tf_op jit(solution)/shard_map/all_to_all | solution.py:619
  77.3 0.0 copy-done
  77.3 4.1 %z_sweep.1 = (f32[6,256,512]{2,1,0:T(8,128)}, f32[6144,128]{1,0:T(8,128)S(1)}) custom-call(f32[5120,128]{1,0:T(8,128)S(1)} %bitcast.16, f32[256,512]{1,0:T(8,128)S(1)} %get-tuple-element.25.cells_ref, f32[8,512]{1,0:T(8,128)S(1)} %get-tuple-element.26.edge_ref, f32[8,512]{1,0:T(8,128)S(1)} %get-tuple-element.27.mean_ref, ...), custom_call_target="tpu_custom_call" | custom-call | tf_op jit(solution)/shard_map/z_sweep/pallas_call | solution.py:599
  81.5 45.4 %all_to_all.56 = f32[128,1,6144]{2,1,0:T(1,128)S(1)} all-to-all(f32[128,1,6144]{2,1,0:T(1,128)S(1)} %bitcast.19), channel_id=1, replica_groups=mesh['row_0'=4,'row_1'=2,'col_0'=4,'col_1'=4] {'row_0','row_1','col_0','..., dimensions={0} | all-to-all | bytes 6291456 | tf_op jit(solution)/shard_map/all_to_all | solution.py:619
  126.8 9.3 %plane_green.1 = f32[6144,128]{1,0:T(8,128)S(1)} custom-call(s32[1]{0:T(128)} %bitcast.place_ref, f32[6144,128]{1,0:T(8,128)S(1)} %bitcast.14, bf16[2,2,256,256]{3,2,1,0:T(8,128)(2,1)S(1)} %get-tuple-element.22.ahead_ref, bf16[2,2,256,256]{3,2,1,0:T(8,128)(2,1)S(1)} %get-tuple-element.23.back_ref), custom_call_target="tpu_custom_call" | custom-call | tf_op jit(solution)/shard_map/plane_green/pallas_call | solution.py:599
  136.1 45.4 %all_to_all.57 = f32[128,1,6144]{2,1,0:T(1,128)S(1)} all-to-all(f32[128,1,6144]{2,1,0:T(1,128)S(1)} %bitcast.15), channel_id=1, replica_groups=mesh['row_0'=4,'row_1'=2,'col_0'=4,'col_1'=4] {'row_0','row_1','col_0','..., dimensions={0} | all-to-all | bytes 6291456 | tf_op jit(solution)/shard_map/all_to_all | solution.py:619
  181.4 4.0 %z_drive.1 = (f32[6,256,512]{2,1,0:T(8,128)}, f32[1024,128]{1,0:T(8,128)}) custom-call(f32[6144,128]{1,0:T(8,128)S(1)} %bitcast.13, f32[256,512]{1,0:T(8,128)S(1)} %get-tuple-element.25.cells_ref, bf16[2,256,256]{2,1,0:T(8,128)(2,1)S(1)} %get-tuple-element.28.back_ref, bf16[3,256,256]{2,1,0:T(8,128)(2,1)S(1)} %get-tuple-element.29.ahead_ref), custom_call_target="tpu_custom_call" | custom-call | tf_op jit(solution)/shard_map/z_drive/pallas_call | solution.py:599
  185.4 5.4 %all-to-all-start.4 = ((f32[128,1,1024]{2,1,0:T(1,128)}), f32[128,1,1024]{2,1,0:T(1,128)S(1)}, u32[]{:S(2)}, u32[]{:S(2)}) async-start(f32[128,1,1024]{2,1,0:T(1,128)} %bitcast.9), calls=%async_computation.4 | async-start | bytes 1048576 | tf_op jit(solution)/shard_map/all_to_all | solution.py:619
  190.8 5.5 %aside.1 = (f32[6,32,16,256]{3,2,1,0:T(8,128)}, f32[2,256,256]{2,1,0:T(8,128)S(1)}, f32[8,128]{1,0:T(8,128)S(1)}) custom-call(f32[6,256,512]{2,1,0:T(8,128)} %get-tuple-element.32.now_ref, f32[6,256,512]{2,1,0:T(8,128)} %get-tuple-element.33.then_ref, f32[2176,128]{1,0:T(8,128)} %bitcast.18, bf16[2,2,256,256]{3,2,1,0:T(8,128)(2,1)S(1)} %get-tuple-element.22.ahead_ref, ...), custom_call_target="tpu_custom_call" | custom-call | tf_op jit(solution)/shard_map/aside/pallas_call | solution.py:599
  196.3 8.5 %all-to-all-done.4 = f32[128,1,1024]{2,1,0:T(1,128)S(1)} async-done(((f32[128,1,1024]{2,1,0:T(1,128)}), f32[128,1,1024]{2,1,0:T(1,128)S(1)}, u32[]{:S(2)}, u32[]{:S(2)}) %all-to-all-start.4) | async-done | bytes 524320 | tf_op jit(solution)/shard_map/all_to_all | solution.py:619
  204.8 2.2 plane_update.1
  207.1 18.5 %all_to_all.58 = f32[128,1,1152]{2,1,0:T(1,128)S(1)} all-to-all(f32[128,1,1152]{2,1,0:T(1,128)S(1)} %bitcast.22), channel_id=1, replica_groups=mesh['row_0'=4,'row_1'=2,'col_0'=4,'col_1'=4] {'row_0','row_1','col_0','..., dimensions={0} | all-to-all | bytes 1179648 | tf_op jit(solution)/shard_map/all_to_all | solution.py:619
  225.6 2.1 z_last.1
Async XLA Ops:
  34.2 43.2 %copy-start = (f32[128,1,2176]{2,1,0:T(1,128)}, f32[128,1,2176]{2,1,0:T(1,128)S(1)}, u32[]{:S(2)}) copy-start(f32[128,1,2176]{2,1,0:T(1,128)S(1)} %all_to_all.54) | copy-start | bytes 3342340
  185.4 19.4 %all-to-all-start.4 = ((f32[128,1,1024]{2,1,0:T(1,128)}), f32[128,1,1024]{2,1,0:T(1,128)S(1)}, u32[]{:S(2)}, u32[]{:S(2)}) async-start(f32[128,1,1024]{2,1,0:T(1,128)} %bitcast.9), calls=%async_computation.4 | async-start | bytes 1048576 | tf_op jit(solution)/shard_map/all_to_all | solution.py:619

commit v6 on v5

--- a/solution.py
+++ b/solution.py
@@ -43,7 +43,7 @@
 SWEEP_UNROLL = 3
 DRIVE_UNROLL = 6
 BLOCK_UNROLL = 2
-SOURCE_ROWS = 2 * LOW + 1
+SOURCE_ROWS = 2 * LOW
 FIRST_ROWS = 5 * LOW
 SWEEP_ROWS = 6 * LOW
 DRIVE_ROWS = LOW
@@ -195,7 +195,7 @@
     )
 
 
-def x_back(real, imag, f, pitch, back_ref, plane_ref, out_ref):
+def x_back(real, imag, f, pitch, back_ref, plane_ref, out_ref, mark=None):
     lines = []
     for b in range(2):
         rows = slice(b * HALF, (b + 1) * HALF)
@@ -203,6 +203,9 @@
         lines.append(product(table(back_ref.at[b]), split(data, 2)))
     plane_ref[0] = lines[0] + lines[1]
     plane_ref[1] = lines[0] - lines[1]
+    if mark is not None:
+        for half in range(2):
+            plane_ref[half, HALF:] = jnp.where(mark[0], mark[1], plane_ref[half, HALF:])
     for i in range(ROWS):
         for h in range(2):
             parts = []
@@ -301,9 +304,6 @@
     edge = jnp.where(row % 2 == 0, total, -total)
     edge = jnp.sum(edge, axis=0, keepdims=True) * (1.0 / N)
     edge_ref[...] = jnp.where(row % 2 == 0, edge, -edge)
-    total = sum(total[:, t * LANES : (t + 1) * LANES] for t in range(CELLS // LANES))
-    total = jnp.sum(total, axis=0, keepdims=True)
-    out_ref[peers_of(2 * LOW, SOURCE_ROWS), :] = jnp.broadcast_to(total, (DEVICES, LANES))
     z_ahead(source, 0, SOURCE_ROWS, 3, ahead_ref, out_ref)
     z_ahead(conc, 1, SOURCE_ROWS, 2, ahead_ref, out_ref)
     lane = lax.broadcasted_iota(jnp.int32, (N, N), 1)
@@ -317,11 +317,11 @@
 
 
 def plane_first_kernel(
-    place_ref, in_ref, ahead_ref, back_ref, out_ref, mean_ref, plane_ref, line_ref
+    place_ref, in_ref, ahead_ref, back_ref, out_ref, plane_ref, line_ref
 ):
-    mean = jnp.sum(in_ref[peers_of(2 * LOW, SOURCE_ROWS), :]) * (1.0 / float(N) ** 3)
-    mean_ref[...] = jnp.full((8, CELLS), mean, F32)
     data = list(plane_spectrum(in_ref, 0, SOURCE_ROWS, ahead_ref, back_ref, plane_ref.at[5]))
+    mean = jnp.broadcast_to(data[0][:1, :1] * (1.0 / float(N) ** 3), (HALF, N))
+    bottom = jnp.full((HALF, N), place_ref[0], jnp.int32) == 0
     wave_x = row_waves(0, N)
     wave_z = depth_wave(place_ref, N)
     wave_y = []
@@ -347,14 +347,14 @@
         if factor is not None:
             real = real * twice(factor)
             imag = imag * twice(factor)
-        x_back(real, imag, f, FIRST_ROWS, back_ref, plane_ref.at[f], out_ref)
+        mark = (bottom, mean) if f == 0 else None
+        x_back(real, imag, f, FIRST_ROWS, back_ref, plane_ref.at[f], out_ref, mark)
 
 
 def z_sweep_kernel(
     in_ref,
     cells_ref,
     edge_ref,
-    mean_ref,
     back_ref,
     ahead_ref,
     past_ref,
@@ -368,10 +368,15 @@
         spec = spec_ref.at[f]
         strain_ref[component] = z_back(in_ref, f, FIRST_ROWS, back_ref, spec)
 
+    mean = in_ref[:LOW, :]
+    lane = lax.broadcasted_iota(jnp.int32, mean.shape, 1)
+    mean = jnp.where(lane < LANES // 2, pltpu.roll(mean, LANES // 2, 1), mean)
+    mean = jnp.concatenate([mean] * (CELLS // LANES), axis=1)
+
     def block(b, slot):
         rows = pl.ds(pl.multiple_of(b * 8, 8), 8)
         conc = cells_ref[rows, :]
-        source = source_of(conc) - mean_ref[...]
+        source = source_of(conc) - mean
         trace = TRACE * (source - edge_ref[...])
         strain = [strain_ref[f, rows, :] for f in range(6) if f != 2]
         strain.insert(2, trace - strain[0] - strain[1])
@@ -448,11 +453,13 @@
     back_ref,
     ahead_ref,
     far_ref,
-    out_ref,
+    far_out_ref,
     strain_ref,
     spec_ref,
     drive_ref,
+    out_ref,
     sems,
+    out_sem,
 ):
     def far(f):
         return pltpu.make_async_copy(strain_ref.at[f], far_ref.at[f], sems.at[f])
@@ -489,8 +496,11 @@
 
     each(N // 8, BLOCK_UNROLL, block)
     z_ahead(drive_ref[...], 0, DRIVE_ROWS, 2, ahead_ref, out_ref)
+    out = pltpu.make_async_copy(out_ref, far_out_ref, out_sem)
+    out.start()
     for f in range(6):
         far(f).wait()
+    out.wait()
 
 
 def aside_kernel(
@@ -653,18 +663,18 @@
     )
     back, ahead, line_ahead, line_back = [("vmem", table) for table in tables]
     source = exchange(data)
-    data, mean = call(
+    (data,) = call(
         plane_first_kernel,
         "plane_first",
         [place, ("vmem", source), line_ahead, line_back],
-        [("vmem", wire(FIRST_ROWS)), ("vmem", SMALL)],
+        [("vmem", wire(FIRST_ROWS))],
         [(6, *PLANE), (3, *PLANE)],
     )
     data = exchange(data)
     past, data = call(
         z_sweep_kernel,
         "z_sweep",
-        [("vmem", data), ("vmem", cells), ("vmem", edge), ("vmem", mean), back, ahead],
+        [("vmem", data), ("vmem", cells), ("vmem", edge), back, ahead],
         [("hbm", (6, *CELL)), ("vmem", wire(SWEEP_ROWS))],
         [(6, *CELL), (5, *CELL), (6, *CELL)],
         [()],
@@ -682,9 +692,9 @@
         z_drive_kernel,
         "z_drive",
         [("vmem", data), ("vmem", cells), back, ahead],
-        [("hbm", (6, *CELL)), ("vmem", wire(DRIVE_ROWS))],
-        [(6, *CELL), (DRIVE_UNROLL, *CELL), CELL],
-        [(6,)],
+        [("hbm", (6, *CELL)), ("hbm", wire(DRIVE_ROWS))],
+        [(6, *CELL), (DRIVE_UNROLL, *CELL), CELL, wire(DRIVE_ROWS)],
+        [(6,), ()],
     )
     data = exchange(data)
     strain, conc_spec, sums = call(

time: 228 us -> 227 us (level)
  no operation moved by 1% of the time
where the time goes in v6:
time: 227 us
  blocking collectives  178 us (78%)
  Pallas kernels  34 us (15%)
  waiting for transfers between devices  8.49 us (4%)
  starting transfers between devices  5.36 us (2%)
    all_to_all x5, blocking collectives, exchange(): rows = lax.all_to_all(rows, AXES, split_axis=0, concat_axis=0, tiled=True)  178 us
    pallas_call x8, Pallas kernels, call(): pl.pallas_call(kernel, out_shape=[pltpu.HBM(shape, F32) if space == 'hbm'...  34 us
    all_to_all x1, waiting for transfers between devices, exchange(): rows = lax.all_to_all(rows, AXES, split_axis=0, concat_axis=0, tiled=True)  8.49 us
    all_to_all x1, starting transfers between devices, exchange(): rows = lax.all_to_all(rows, AXES, split_axis=0, concat_axis=0, tiled=True)  5.36 us
  transfers between devices with their start and end apart: 1, of which 1 were waited for; matrix products, arithmetic and copies ran while one was open for 0% of the time, Pallas kernels for 2%

profile of v6, /device:TPU:1, one launch (start us, length us, event | category | flops | bytes accessed | tf_op | source)
XLA Modules:
  0.0 226.9 jit_solution(15114778318460619043)
XLA Ops:
  0.6 2.7 %source.1 = (f32[256,512]{1,0:T(8,128)S(1)}, f32[2048,128]{1,0:T(8,128)S(1)}, f32[8,512]{1,0:T(8,128)S(1)}, bf16[2,256,256]{2,1,0:T(8,128)(2,1)S(1)}, bf16[3,256...) custom-call(s32[1]{0:T(128)} %bitcast.place_ref, ...), custom_call_target="tpu_custom_call" | custom-call | tf_op jit(solution)/shard_map/source/pallas_call | solution.py:609
  3.4 30.2 %all_to_all.54 = f32[128,1,2048]{2,1,0:T(1,128)S(1)} all-to-all(f32[128,1,2048]{2,1,0:T(1,128)S(1)} %bitcast.24), channel_id=1, replica_groups=mesh['row_0'=4,'row_1'=2,'col_0'=4,'col_1'=4] {'row_0','row_1','col_0','..., dimensions={0} | all-to-all | bytes 2097152 | tf_op jit(solution)/shard_map/all_to_all | solution.py:629
  33.5 0.0 copy-start
  33.5 4.3 %plane_first.1 = f32[5120,128]{1,0:T(8,128)S(1)} custom-call(s32[1]{0:T(128)} %bitcast.place_ref, f32[2048,128]{1,0:T(8,128)S(1)} %bitcast.18, bf16[2,2,256,256]{3,2,1,0:T(8,128)(2,1)S(1)} %get-tuple-element.20.ahead_ref, bf16[2,2,256,256]{3,2,1,0:T(8,128)(2,1)S(1)} %get-tuple-element.21.back_ref), custom_call_target="tpu_custom_call" | custom-call | tf_op jit(solution)/shard_map/plane_first/pallas_call | solution.py:609
  37.8 38.8 %all_to_all.55 = f32[128,1,5120]{2,1,0:T(1,128)S(1)} all-to-all(f32[128,1,5120]{2,1,0:T(1,128)S(1)} %bitcast.17), channel_id=1, replica_groups=mesh['row_0'=4,'row_1'=2,'col_0'=4,'col_1'=4] {'row_0','row_1','col_0','..., dimensions={0} | all-to-all | bytes 5242880 | tf_op jit(solution)/shard_map/all_to_all | solution.py:629
  76.6 0.0 copy-done
  76.6 4.1 %z_sweep.1 = (f32[6,256,512]{2,1,0:T(8,128)}, f32[6144,128]{1,0:T(8,128)S(1)}) custom-call(f32[5120,128]{1,0:T(8,128)S(1)} %bitcast.16, f32[256,512]{1,0:T(8,128)S(1)} %get-tuple-element.22.cells_ref, f32[8,512]{1,0:T(8,128)S(1)} %get-tuple-element.23.edge_ref, bf16[2,256,256]{2,1,0:T(8,128)(2,1)S(1)} %get-tuple-element.24.back_ref, ...), custom_call_target="tpu_custom_call" | custom-call | tf_op jit(solution)/shard_map/z_sweep/pallas_call | solution.py:609
  80.7 45.4 %all_to_all.56 = f32[128,1,6144]{2,1,0:T(1,128)S(1)} all-to-all(f32[128,1,6144]{2,1,0:T(1,128)S(1)} %bitcast.20), channel_id=1, replica_groups=mesh['row_0'=4,'row_1'=2,'col_0'=4,'col_1'=4] {'row_0','row_1','col_0','..., dimensions={0} | all-to-all | bytes 6291456 | tf_op jit(solution)/shard_map/all_to_all | solution.py:629
  126.1 9.1 %plane_green.1 = f32[6144,128]{1,0:T(8,128)S(1)} custom-call(s32[1]{0:T(128)} %bitcast.place_ref, f32[6144,128]{1,0:T(8,128)S(1)} %bitcast.14, bf16[2,2,256,256]{3,2,1,0:T(8,128)(2,1)S(1)} %get-tuple-element.20.ahead_ref, bf16[2,2,256,256]{3,2,1,0:T(8,128)(2,1)S(1)} %get-tuple-element.21.back_ref), custom_call_target="tpu_custom_call" | custom-call | tf_op jit(solution)/shard_map/plane_green/pallas_call | solution.py:609
  135.2 45.4 %all_to_all.57 = f32[128,1,6144]{2,1,0:T(1,128)S(1)} all-to-all(f32[128,1,6144]{2,1,0:T(1,128)S(1)} %bitcast.15), channel_id=1, replica_groups=mesh['row_0'=4,'row_1'=2,'col_0'=4,'col_1'=4] {'row_0','row_1','col_0','..., dimensions={0} | all-to-all | bytes 6291456 | tf_op jit(solution)/shard_map/all_to_all | solution.py:629
  180.6 3.9 %z_drive.1 = (f32[6,256,512]{2,1,0:T(8,128)}, f32[1024,128]{1,0:T(8,128)}) custom-call(f32[6144,128]{1,0:T(8,128)S(1)} %bitcast.13, f32[256,512]{1,0:T(8,128)S(1)} %get-tuple-element.22.cells_ref, bf16[2,256,256]{2,1,0:T(8,128)(2,1)S(1)} %get-tuple-element.24.back_ref, bf16[3,256,256]{2,1,0:T(8,128)(2,1)S(1)} %get-tuple-element.25.ahead_ref), custom_call_target="tpu_custom_call" | custom-call | tf_op jit(solution)/shard_map/z_drive/pallas_call | solution.py:609
  184.5 5.4 %all-to-all-start.4 = ((f32[128,1,1024]{2,1,0:T(1,128)}), f32[128,1,1024]{2,1,0:T(1,128)S(1)}, u32[]{:S(2)}, u32[]{:S(2)}) async-start(f32[128,1,1024]{2,1,0:T(1,128)} %bitcast.25), calls=%async_computation.4 | async-start | bytes 1048576 | tf_op jit(solution)/shard_map/all_to_all | solution.py:629
  189.9 5.5 %aside.1 = (f32[6,32,16,256]{3,2,1,0:T(8,128)}, f32[2,256,256]{2,1,0:T(8,128)S(1)}, f32[8,128]{1,0:T(8,128)S(1)}) custom-call(f32[6,256,512]{2,1,0:T(8,128)} %get-tuple-element.28.now_ref, f32[6,256,512]{2,1,0:T(8,128)} %get-tuple-element.29.then_ref, f32[2048,128]{1,0:T(8,128)} %bitcast.19, bf16[2,2,256,256]{3,2,1,0:T(8,128)(2,1)S(1)} %get-tuple-element.20.ahead_ref, ...), custom_call_target="tpu_custom_call" | custom-call | tf_op jit(solution)/shard_map/aside/pallas_call | solution.py:609
  195.4 8.5 %all-to-all-done.4 = f32[128,1,1024]{2,1,0:T(1,128)S(1)} async-done(((f32[128,1,1024]{2,1,0:T(1,128)}), f32[128,1,1024]{2,1,0:T(1,128)S(1)}, u32[]{:S(2)}, u32[]{:S(2)}) %all-to-all-start.4) | async-done | bytes 524320 | tf_op jit(solution)/shard_map/all_to_all | solution.py:629
  203.9 2.2 plane_update.1
  206.2 18.5 %all_to_all.58 = f32[128,1,1152]{2,1,0:T(1,128)S(1)} all-to-all(f32[128,1,1152]{2,1,0:T(1,128)S(1)} %bitcast.22), channel_id=1, replica_groups=mesh['row_0'=4,'row_1'=2,'col_0'=4,'col_1'=4] {'row_0','row_1','col_0','..., dimensions={0} | all-to-all | bytes 1179648 | tf_op jit(solution)/shard_map/all_to_all | solution.py:629
  224.7 2.1 z_last.1
Async XLA Ops:
  33.5 43.1 %copy-start = (f32[128,1,2048]{2,1,0:T(1,128)}, f32[128,1,2048]{2,1,0:T(1,128)S(1)}, u32[]{:S(2)}) copy-start(f32[128,1,2048]{2,1,0:T(1,128)S(1)} %all_to_all.54) | copy-start | bytes 3145732
  184.5 19.4 %all-to-all-start.4 = ((f32[128,1,1024]{2,1,0:T(1,128)}), f32[128,1,1024]{2,1,0:T(1,128)S(1)}, u32[]{:S(2)}, u32[]{:S(2)}) async-start(f32[128,1,1024]{2,1,0:T(1,128)} %bitcast.25), calls=%async_computation.4 | async-start | bytes 1048576 | tf_op jit(solution)/shard_map/all_to_all | solution.py:629

commit v7 on v6

--- a/solution.py
+++ b/solution.py
@@ -114,6 +114,11 @@
         for i in range(len(parts)):
             if i & step == 0:
                 a, b = parts[i], parts[i + step]
+                if len(parts) > 2 and 2 * width == LANES:
+                    moved = pltpu.roll(jnp.where(low, b, a), width, axis)
+                    parts[i] = jnp.where(low, a, moved)
+                    parts[i + step] = jnp.where(low, moved, b)
+                    continue
                 parts[i] = jnp.where(low, a, pltpu.roll(b, width, axis))
                 parts[i + step] = jnp.where(low, pltpu.roll(a, LANES - width, axis), b)
         step *= 2

time: 227 us -> 227 us (level)
  no operation moved by 1% of the time
where the time goes in v7:
time: 227 us; the launch traced here: 226 us
  blocking collectives  178 us (78%)
  Pallas kernels  33.4 us (15%)
  waiting for transfers between devices  8.54 us (4%)
  starting transfers between devices  5.36 us (2%)
    all_to_all x5, blocking collectives, exchange(): rows = lax.all_to_all(rows, AXES, split_axis=0, concat_axis=0, tiled=True)  178 us
    pallas_call x8, Pallas kernels, call(): pl.pallas_call(kernel, out_shape=[pltpu.HBM(shape, F32) if space == 'hbm'...  33.4 us
    all_to_all x1, waiting for transfers between devices, exchange(): rows = lax.all_to_all(rows, AXES, split_axis=0, concat_axis=0, tiled=True)  8.54 us
    all_to_all x1, starting transfers between devices, exchange(): rows = lax.all_to_all(rows, AXES, split_axis=0, concat_axis=0, tiled=True)  5.36 us
  transfers between devices with their start and end apart: 1, of which 1 were waited for; matrix products, arithmetic and copies ran while one was open for 0% of the time, Pallas kernels for 2%

profile of v7, /device:TPU:1, one launch (start us, length us, event | category | flops | bytes accessed | tf_op | source)
XLA Modules:
  0.0 226.4 jit_solution(12588627186647308210)
XLA Ops:
  0.6 2.7 %source.1 = (f32[256,512]{1,0:T(8,128)S(1)}, f32[2048,128]{1,0:T(8,128)S(1)}, f32[8,512]{1,0:T(8,128)S(1)}, bf16[2,256,256]{2,1,0:T(8,128)(2,1)S(1)}, bf16[3,256...) custom-call(s32[1]{0:T(128)} %bitcast.place_ref, ...), custom_call_target="tpu_custom_call" | custom-call | tf_op jit(solution)/shard_map/source/pallas_call | solution.py:614
  3.4 30.2 %all_to_all.54 = f32[128,1,2048]{2,1,0:T(1,128)S(1)} all-to-all(f32[128,1,2048]{2,1,0:T(1,128)S(1)} %bitcast.24), channel_id=1, replica_groups=mesh['row_0'=4,'row_1'=2,'col_0'=4,'col_1'=4] {'row_0','row_1','col_0','..., dimensions={0} | all-to-all | bytes 2097152 | tf_op jit(solution)/shard_map/all_to_all | solution.py:634
  33.5 0.0 copy-start
  33.5 4.0 %plane_first.1 = f32[5120,128]{1,0:T(8,128)S(1)} custom-call(s32[1]{0:T(128)} %bitcast.place_ref, f32[2048,128]{1,0:T(8,128)S(1)} %bitcast.18, bf16[2,2,256,256]{3,2,1,0:T(8,128)(2,1)S(1)} %get-tuple-element.20.ahead_ref, bf16[2,2,256,256]{3,2,1,0:T(8,128)(2,1)S(1)} %get-tuple-element.21.back_ref), custom_call_target="tpu_custom_call" | custom-call | tf_op jit(solution)/shard_map/plane_first/pallas_call | solution.py:614
  37.5 38.8 %all_to_all.55 = f32[128,1,5120]{2,1,0:T(1,128)S(1)} all-to-all(f32[128,1,5120]{2,1,0:T(1,128)S(1)} %bitcast.17), channel_id=1, replica_groups=mesh['row_0'=4,'row_1'=2,'col_0'=4,'col_1'=4] {'row_0','row_1','col_0','..., dimensions={0} | all-to-all | bytes 5242880 | tf_op jit(solution)/shard_map/all_to_all | solution.py:634
  76.3 0.0 copy-done
  76.3 4.1 %z_sweep.1 = (f32[6,256,512]{2,1,0:T(8,128)}, f32[6144,128]{1,0:T(8,128)S(1)}) custom-call(f32[5120,128]{1,0:T(8,128)S(1)} %bitcast.16, f32[256,512]{1,0:T(8,128)S(1)} %get-tuple-element.22.cells_ref, f32[8,512]{1,0:T(8,128)S(1)} %get-tuple-element.23.edge_ref, bf16[2,256,256]{2,1,0:T(8,128)(2,1)S(1)} %get-tuple-element.24.back_ref, ...), custom_call_target="tpu_custom_call" | custom-call | tf_op jit(solution)/shard_map/z_sweep/pallas_call | solution.py:614
  80.4 45.4 %all_to_all.56 = f32[128,1,6144]{2,1,0:T(1,128)S(1)} all-to-all(f32[128,1,6144]{2,1,0:T(1,128)S(1)} %bitcast.20), channel_id=1, replica_groups=mesh['row_0'=4,'row_1'=2,'col_0'=4,'col_1'=4] {'row_0','row_1','col_0','..., dimensions={0} | all-to-all | bytes 6291456 | tf_op jit(solution)/shard_map/all_to_all | solution.py:634
  125.7 9.0 %plane_green.1 = f32[6144,128]{1,0:T(8,128)S(1)} custom-call(s32[1]{0:T(128)} %bitcast.place_ref, f32[6144,128]{1,0:T(8,128)S(1)} %bitcast.14, bf16[2,2,256,256]{3,2,1,0:T(8,128)(2,1)S(1)} %get-tuple-element.20.ahead_ref, bf16[2,2,256,256]{3,2,1,0:T(8,128)(2,1)S(1)} %get-tuple-element.21.back_ref), custom_call_target="tpu_custom_call" | custom-call | tf_op jit(solution)/shard_map/plane_green/pallas_call | solution.py:614
  134.8 45.4 %all_to_all.57 = f32[128,1,6144]{2,1,0:T(1,128)S(1)} all-to-all(f32[128,1,6144]{2,1,0:T(1,128)S(1)} %bitcast.15), channel_id=1, replica_groups=mesh['row_0'=4,'row_1'=2,'col_0'=4,'col_1'=4] {'row_0','row_1','col_0','..., dimensions={0} | all-to-all | bytes 6291456 | tf_op jit(solution)/shard_map/all_to_all | solution.py:634
  180.1 3.9 %z_drive.1 = (f32[6,256,512]{2,1,0:T(8,128)}, f32[1024,128]{1,0:T(8,128)}) custom-call(f32[6144,128]{1,0:T(8,128)S(1)} %bitcast.13, f32[256,512]{1,0:T(8,128)S(1)} %get-tuple-element.22.cells_ref, bf16[2,256,256]{2,1,0:T(8,128)(2,1)S(1)} %get-tuple-element.24.back_ref, bf16[3,256,256]{2,1,0:T(8,128)(2,1)S(1)} %get-tuple-element.25.ahead_ref), custom_call_target="tpu_custom_call" | custom-call | tf_op jit(solution)/shard_map/z_drive/pallas_call | solution.py:614
  184.1 5.4 %all-to-all-start.4 = ((f32[128,1,1024]{2,1,0:T(1,128)}), f32[128,1,1024]{2,1,0:T(1,128)S(1)}, u32[]{:S(2)}, u32[]{:S(2)}) async-start(f32[128,1,1024]{2,1,0:T(1,128)} %bitcast.25), calls=%async_computation.4 | async-start | bytes 1048576 | tf_op jit(solution)/shard_map/all_to_all | solution.py:634
  189.4 5.5 %aside.1 = (f32[6,32,16,256]{3,2,1,0:T(8,128)}, f32[2,256,256]{2,1,0:T(8,128)S(1)}, f32[8,128]{1,0:T(8,128)S(1)}) custom-call(f32[6,256,512]{2,1,0:T(8,128)} %get-tuple-element.28.now_ref, f32[6,256,512]{2,1,0:T(8,128)} %get-tuple-element.29.then_ref, f32[2048,128]{1,0:T(8,128)} %bitcast.19, bf16[2,2,256,256]{3,2,1,0:T(8,128)(2,1)S(1)} %get-tuple-element.20.ahead_ref, ...), custom_call_target="tpu_custom_call" | custom-call | tf_op jit(solution)/shard_map/aside/pallas_call | solution.py:614
  195.0 8.5 %all-to-all-done.4 = f32[128,1,1024]{2,1,0:T(1,128)S(1)} async-done(((f32[128,1,1024]{2,1,0:T(1,128)}), f32[128,1,1024]{2,1,0:T(1,128)S(1)}, u32[]{:S(2)}, u32[]{:S(2)}) %all-to-all-start.4) | async-done | bytes 524320 | tf_op jit(solution)/shard_map/all_to_all | solution.py:634
  203.5 2.2 plane_update.1
  205.7 18.5 %all_to_all.58 = f32[128,1,1152]{2,1,0:T(1,128)S(1)} all-to-all(f32[128,1,1152]{2,1,0:T(1,128)S(1)} %bitcast.22), channel_id=1, replica_groups=mesh['row_0'=4,'row_1'=2,'col_0'=4,'col_1'=4] {'row_0','row_1','col_0','..., dimensions={0} | all-to-all | bytes 1179648 | tf_op jit(solution)/shard_map/all_to_all | solution.py:634
  224.2 2.1 z_last.1
Async XLA Ops:
  33.5 42.7 %copy-start = (f32[128,1,2048]{2,1,0:T(1,128)}, f32[128,1,2048]{2,1,0:T(1,128)S(1)}, u32[]{:S(2)}) copy-start(f32[128,1,2048]{2,1,0:T(1,128)S(1)} %all_to_all.54) | copy-start | bytes 3145732
  184.1 19.4 %all-to-all-start.4 = ((f32[128,1,1024]{2,1,0:T(1,128)}), f32[128,1,1024]{2,1,0:T(1,128)S(1)}, u32[]{:S(2)}, u32[]{:S(2)}) async-start(f32[128,1,1024]{2,1,0:T(1,128)} %bitcast.25), calls=%async_computation.4 | async-start | bytes 1048576 | tf_op jit(solution)/shard_map/all_to_all | solution.py:634

commit v8 on v7

--- a/solution.py
+++ b/solution.py
@@ -42,7 +42,7 @@
 PLANE_UNROLL = 6
 SWEEP_UNROLL = 3
 DRIVE_UNROLL = 6
-BLOCK_UNROLL = 2
+BLOCK_UNROLL = 4
 SOURCE_ROWS = 2 * LOW
 FIRST_ROWS = 5 * LOW
 SWEEP_ROWS = 6 * LOW

time: 227 us -> 226 us (level)
  no operation moved by 1% of the time
where the time goes in v8:
time: 226 us
  blocking collectives  178 us (79%)
  Pallas kernels  33.2 us (15%)
  waiting for transfers between devices  8.54 us (4%)
  starting transfers between devices  5.36 us (2%)
    all_to_all x5, blocking collectives, exchange(): rows = lax.all_to_all(rows, AXES, split_axis=0, concat_axis=0, tiled=True)  178 us
    pallas_call x8, Pallas kernels, call(): pl.pallas_call(kernel, out_shape=[pltpu.HBM(shape, F32) if space == 'hbm'...  33.2 us
    all_to_all x1, waiting for transfers between devices, exchange(): rows = lax.all_to_all(rows, AXES, split_axis=0, concat_axis=0, tiled=True)  8.54 us
    all_to_all x1, starting transfers between devices, exchange(): rows = lax.all_to_all(rows, AXES, split_axis=0, concat_axis=0, tiled=True)  5.36 us
  transfers between devices with their start and end apart: 1, of which 1 were waited for; matrix products, arithmetic and copies ran while one was open for 0% of the time, Pallas kernels for 2%

profile of v8, /device:TPU:1, one launch (start us, length us, event | category | flops | bytes accessed | tf_op | source)
XLA Modules:
  0.0 226.2 jit_solution(8058759633206665934)
XLA Ops:
  0.6 2.7 %source.1 = (f32[256,512]{1,0:T(8,128)S(1)}, f32[2048,128]{1,0:T(8,128)S(1)}, f32[8,512]{1,0:T(8,128)S(1)}, bf16[2,256,256]{2,1,0:T(8,128)(2,1)S(1)}, bf16[3,256...) custom-call(s32[1]{0:T(128)} %bitcast.place_ref, ...), custom_call_target="tpu_custom_call" | custom-call | tf_op jit(solution)/shard_map/source/pallas_call | solution.py:614
  3.4 30.2 %all_to_all.54 = f32[128,1,2048]{2,1,0:T(1,128)S(1)} all-to-all(f32[128,1,2048]{2,1,0:T(1,128)S(1)} %bitcast.24), channel_id=1, replica_groups=mesh['row_0'=4,'row_1'=2,'col_0'=4,'col_1'=4] {'row_0','row_1','col_0','..., dimensions={0} | all-to-all | bytes 2097152 | tf_op jit(solution)/shard_map/all_to_all | solution.py:634
  33.5 0.0 copy-start
  33.5 4.0 %plane_first.1 = f32[5120,128]{1,0:T(8,128)S(1)} custom-call(s32[1]{0:T(128)} %bitcast.place_ref, f32[2048,128]{1,0:T(8,128)S(1)} %bitcast.18, bf16[2,2,256,256]{3,2,1,0:T(8,128)(2,1)S(1)} %get-tuple-element.20.ahead_ref, bf16[2,2,256,256]{3,2,1,0:T(8,128)(2,1)S(1)} %get-tuple-element.21.back_ref), custom_call_target="tpu_custom_call" | custom-call | tf_op jit(solution)/shard_map/plane_first/pallas_call | solution.py:614
  37.5 38.8 %all_to_all.55 = f32[128,1,5120]{2,1,0:T(1,128)S(1)} all-to-all(f32[128,1,5120]{2,1,0:T(1,128)S(1)} %bitcast.17), channel_id=1, replica_groups=mesh['row_0'=4,'row_1'=2,'col_0'=4,'col_1'=4] {'row_0','row_1','col_0','..., dimensions={0} | all-to-all | bytes 5242880 | tf_op jit(solution)/shard_map/all_to_all | solution.py:634
  76.3 0.0 copy-done
  76.3 4.1 %z_sweep.1 = (f32[6,256,512]{2,1,0:T(8,128)}, f32[6144,128]{1,0:T(8,128)S(1)}) custom-call(f32[5120,128]{1,0:T(8,128)S(1)} %bitcast.16, f32[256,512]{1,0:T(8,128)S(1)} %get-tuple-element.22.cells_ref, f32[8,512]{1,0:T(8,128)S(1)} %get-tuple-element.23.edge_ref, bf16[2,256,256]{2,1,0:T(8,128)(2,1)S(1)} %get-tuple-element.24.back_ref, ...), custom_call_target="tpu_custom_call" | custom-call | tf_op jit(solution)/shard_map/z_sweep/pallas_call | solution.py:614
  80.3 45.4 %all_to_all.56 = f32[128,1,6144]{2,1,0:T(1,128)S(1)} all-to-all(f32[128,1,6144]{2,1,0:T(1,128)S(1)} %bitcast.20), channel_id=1, replica_groups=mesh['row_0'=4,'row_1'=2,'col_0'=4,'col_1'=4] {'row_0','row_1','col_0','..., dimensions={0} | all-to-all | bytes 6291456 | tf_op jit(solution)/shard_map/all_to_all | solution.py:634
  125.7 8.9 %plane_green.1 = f32[6144,128]{1,0:T(8,128)S(1)} custom-call(s32[1]{0:T(128)} %bitcast.place_ref, f32[6144,128]{1,0:T(8,128)S(1)} %bitcast.14, bf16[2,2,256,256]{3,2,1,0:T(8,128)(2,1)S(1)} %get-tuple-element.20.ahead_ref, bf16[2,2,256,256]{3,2,1,0:T(8,128)(2,1)S(1)} %get-tuple-element.21.back_ref), custom_call_target="tpu_custom_call" | custom-call | tf_op jit(solution)/shard_map/plane_green/pallas_call | solution.py:614
  134.6 45.4 %all_to_all.57 = f32[128,1,6144]{2,1,0:T(1,128)S(1)} all-to-all(f32[128,1,6144]{2,1,0:T(1,128)S(1)} %bitcast.15), channel_id=1, replica_groups=mesh['row_0'=4,'row_1'=2,'col_0'=4,'col_1'=4] {'row_0','row_1','col_0','..., dimensions={0} | all-to-all | bytes 6291456 | tf_op jit(solution)/shard_map/all_to_all | solution.py:634
  180.0 3.9 %z_drive.1 = (f32[6,256,512]{2,1,0:T(8,128)}, f32[1024,128]{1,0:T(8,128)}) custom-call(f32[6144,128]{1,0:T(8,128)S(1)} %bitcast.13, f32[256,512]{1,0:T(8,128)S(1)} %get-tuple-element.22.cells_ref, bf16[2,256,256]{2,1,0:T(8,128)(2,1)S(1)} %get-tuple-element.24.back_ref, bf16[3,256,256]{2,1,0:T(8,128)(2,1)S(1)} %get-tuple-element.25.ahead_ref), custom_call_target="tpu_custom_call" | custom-call | tf_op jit(solution)/shard_map/z_drive/pallas_call | solution.py:614
  183.8 5.4 %all-to-all-start.4 = ((f32[128,1,1024]{2,1,0:T(1,128)}), f32[128,1,1024]{2,1,0:T(1,128)S(1)}, u32[]{:S(2)}, u32[]{:S(2)}) async-start(f32[128,1,1024]{2,1,0:T(1,128)} %bitcast.25), calls=%async_computation.4 | async-start | bytes 1048576 | tf_op jit(solution)/shard_map/all_to_all | solution.py:634
  189.2 5.5 %aside.1 = (f32[6,32,16,256]{3,2,1,0:T(8,128)}, f32[2,256,256]{2,1,0:T(8,128)S(1)}, f32[8,128]{1,0:T(8,128)S(1)}) custom-call(f32[6,256,512]{2,1,0:T(8,128)} %get-tuple-element.28.now_ref, f32[6,256,512]{2,1,0:T(8,128)} %get-tuple-element.29.then_ref, f32[2048,128]{1,0:T(8,128)} %bitcast.19, bf16[2,2,256,256]{3,2,1,0:T(8,128)(2,1)S(1)} %get-tuple-element.20.ahead_ref, ...), custom_call_target="tpu_custom_call" | custom-call | tf_op jit(solution)/shard_map/aside/pallas_call | solution.py:614
  194.7 8.5 %all-to-all-done.4 = f32[128,1,1024]{2,1,0:T(1,128)S(1)} async-done(((f32[128,1,1024]{2,1,0:T(1,128)}), f32[128,1,1024]{2,1,0:T(1,128)S(1)}, u32[]{:S(2)}, u32[]{:S(2)}) %all-to-all-start.4) | async-done | bytes 524320 | tf_op jit(solution)/shard_map/all_to_all | solution.py:634
  203.3 2.2 plane_update.1
  205.4 18.5 %all_to_all.58 = f32[128,1,1152]{2,1,0:T(1,128)S(1)} all-to-all(f32[128,1,1152]{2,1,0:T(1,128)S(1)} %bitcast.22), channel_id=1, replica_groups=mesh['row_0'=4,'row_1'=2,'col_0'=4,'col_1'=4] {'row_0','row_1','col_0','..., dimensions={0} | all-to-all | bytes 1179648 | tf_op jit(solution)/shard_map/all_to_all | solution.py:634
  223.9 2.1 z_last.1
Async XLA Ops:
  33.5 42.7 %copy-start = (f32[128,1,2048]{2,1,0:T(1,128)}, f32[128,1,2048]{2,1,0:T(1,128)S(1)}, u32[]{:S(2)}) copy-start(f32[128,1,2048]{2,1,0:T(1,128)S(1)} %all_to_all.54) | copy-start | bytes 3145732
  183.8 19.4 %all-to-all-start.4 = ((f32[128,1,1024]{2,1,0:T(1,128)}), f32[128,1,1024]{2,1,0:T(1,128)S(1)}, u32[]{:S(2)}, u32[]{:S(2)}) async-start(f32[128,1,1024]{2,1,0:T(1,128)} %bitcast.25), calls=%async_computation.4 | async-start | bytes 1048576 | tf_op jit(solution)/shard_map/all_to_all | solution.py:634
